TPU v7x, 32 devices: a whole 2x2x4 slice. The times are simulated.
32 devices in a mesh: row: 16 (over z, y, core), col: 2 (over x).
Axes of the slice: x: 2, y: 2, z: 4, core: 2. Of those that a mesh axis runs over, the one named last changes fastest.
Arguments:
- pair_act: bfloat16 [192, 192, 128], P('row', 'col'), may hold values from -6 to 6
- tile_mask: int32 [12, 12], replicated, may hold values 0 or 1
- w_left_gate: bfloat16 [128, 128], replicated, may hold values from -0.5 to 0.5
- w_left: bfloat16 [128, 128], replicated, may hold values from -0.5 to 0.5
- w_right_gate: bfloat16 [128, 128], replicated, may hold values from -0.5 to 0.5
- w_right: bfloat16 [128, 128], replicated, may hold values from -0.5 to 0.5
- w_out_gate: bfloat16 [128, 128], replicated, may hold values from -0.5 to 0.5
- w_out: bfloat16 [128, 128], replicated, may hold values from -0.5 to 0.5
Outputs:
- update: bfloat16 [192, 192, 128], P('row', 'col')
All inputs are finite; a program needn't handle non-finite values.
Results may differ from a plain program's by a relative error of at most 0.0083.
Values may be sent and summed in bfloat16 or wider, within the bound.
No kernel may reach another device: no remote copies, remote signals or barrier semaphores. Data moves between devices by JAX's collectives and lax.ppermute only.
A program may use at most 64 MiB of HBM per device.

v0:
```python
import jax
import jax.numpy as jnp
from jax import lax
from jax.sharding import PartitionSpec as P

TILES = 12


def norm_axis(values, axis):
    mean = jnp.mean(values, axis=axis, keepdims=True)
    centred = values - mean
    spread = jnp.mean(centred * centred, axis=axis, keepdims=True)
    return centred * lax.rsqrt(spread + 1e-05)


def local(pair_act, tile_mask, w_left_gate, w_left, w_right_gate, w_right, w_out_gate, w_out):
    rows, cols, width = pair_act.shape
    residues = rows * lax.axis_size("row")
    tile = residues // TILES
    normed = norm_axis(pair_act.astype(jnp.float32), 2).astype(jnp.bfloat16)
    tile_range = lax.iota(jnp.int32, TILES)
    row_ids = (lax.axis_index("row") * rows + lax.iota(jnp.int32, rows)) // tile
    col_ids = (lax.axis_index("col") * cols + lax.iota(jnp.int32, cols)) // tile
    row_hot = (row_ids[:, None] == tile_range[None, :]).astype(jnp.float32)
    col_hot = (col_ids[:, None] == tile_range[None, :]).astype(jnp.float32)
    pair_mask = jnp.dot(
        jnp.dot(row_hot, tile_mask.astype(jnp.float32), preferred_element_type=jnp.float32),
        col_hot.T,
        preferred_element_type=jnp.float32,
    )

    def project(weight):
        return jnp.einsum("ijd,de->eij", normed, weight, preferred_element_type=jnp.float32)

    left = (jax.nn.sigmoid(project(w_left_gate)) * project(w_left) * pair_mask[None]).astype(
        jnp.bfloat16
    )
    right = (jax.nn.sigmoid(project(w_right_gate)) * project(w_right) * pair_mask[None]).astype(
        jnp.bfloat16
    )
    left_rows, right_rows = (
        lax.all_to_all(left, "row", split_axis=0, concat_axis=1, tiled=True),
        lax.all_to_all(right, "row", split_axis=0, concat_axis=1, tiled=True),
    )
    right_block = lax.all_to_all(right_rows, "col", split_axis=1, concat_axis=2, tiled=True)
    triangle = jnp.einsum(
        "cik,cjk->jci",
        lax.all_gather(left_rows, "col", axis=2, tiled=True),
        right_block,
        preferred_element_type=jnp.float32,
    )
    triangle = triangle.astype(jnp.bfloat16)
    owned = lax.all_to_all(triangle, "row", split_axis=2, concat_axis=1, tiled=True)
    scaled = norm_axis(owned.astype(jnp.float32), 1).astype(jnp.bfloat16)
    projected = jnp.einsum("jci,ce->ije", scaled, w_out, preferred_element_type=jnp.float32)
    gate = jax.nn.sigmoid(
        jnp.einsum("ijd,de->ije", normed, w_out_gate, preferred_element_type=jnp.float32)
    )
    return (gate * projected).astype(jnp.bfloat16)


def solution(mesh):
    return jax.shard_map(
        local,
        mesh=mesh,
        in_specs=(P("row", "col", None), P(), P(), P(), P(), P(), P(), P()),
        out_specs=P("row", "col", None),
        check_vma=False,
    )
```

profile of v0, /device:TPU:0, one launch (start us, length us, event | category | flops | bytes accessed | tf_op | source)
XLA Modules:
  0.0 84.8 jit_solution(9804419726071187752)
XLA Ops:
  0.0 1.2 %convert_reduce_fusion = f32[12,96]{1,0:T(8,128)S(1)} fusion(bf16[12,96,128]{2,1,0:T(8,128)(2,1)} %param.8), kind=kLoop, calls=%fused_computation.34 | loop fusion | flops 293760 | bytes 299520 | tf_op jit(solution)/shard_map/reduce_sum | solution.py:10
  1.2 0.5 fusion.26
  1.7 0.0 copy-start.7
  1.7 0.8 fusion.8
  2.5 0.3 fusion.18
  2.8 0.5 copy-done.2
  3.3 0.5 fusion.17
  3.8 1.2 %copy.22 = bf16[128,12,96]{2,1,0:T(8,128)(2,1)} copy(bf16[128,12,96]{0,2,1:T(8,128)(2,1)S(1)} %fusion.17) | data formatting | bytes 589824 | tf_op jit(solution)/shard_map/convert_element_type | solution.py:38
  5.0 7.5 %all-to-all-start = ((bf16[128,12,96]{2,1,0:T(8,128)(2,1)}), bf16[128,12,96]{2,1,0:T(8,128)(2,1)S(1)}, u32[]{:S(2)}, u32[]{:S(2)}) async-start(bf16[128,12,96]{2,1,0:T(8,128)(2,1)} %copy.22), calls=%async_computation | async-start | bytes 1048576 | tf_op jit(solution)/shard_map/all_to_all | solution.py:43
  12.6 0.0 copy-start.3
  12.6 0.8 fusion.5
  13.4 0.5 fusion.16
  13.9 1.2 %copy.27 = bf16[128,12,96]{2,1,0:T(8,128)(2,1)} copy(bf16[128,12,96]{0,2,1:T(8,128)(2,1)S(1)} %fusion.16) | data formatting | bytes 589824 | tf_op jit(solution)/shard_map/convert_element_type | solution.py:35
  15.1 11.7 %all-to-all-done = bf16[128,12,96]{2,1,0:T(8,128)(2,1)S(1)} async-done(((bf16[128,12,96]{2,1,0:T(8,128)(2,1)}), bf16[128,12,96]{2,1,0:T(8,128)(2,1)S(1)}, u32[]{:S(2)}, u32[]{:S(2)}) %all-to-all-start) | async-done | bytes 294944 | tf_op jit(solution)/shard_map/all_to_all | solution.py:43
  26.8 4.2 %all-to-all-start.2 = ((bf16[128,12,96]{2,1,0:T(8,128)(2,1)}), bf16[128,12,96]{2,1,0:T(8,128)(2,1)S(1)}, u32[]{:S(2)}, u32[]{:S(2)}) async-start(bf16[128,12,96]{2,1,0:T(8,128)(2,1)} %copy.27), calls=%async_computation.2 | async-start | bytes 1048576 | tf_op jit(solution)/shard_map/all_to_all | solution.py:42
  31.0 0.8 copy.24
  31.9 13.4 %all-to-all-done.2 = bf16[128,12,96]{2,1,0:T(8,128)(2,1)S(1)} async-done(((bf16[128,12,96]{2,1,0:T(8,128)(2,1)}), bf16[128,12,96]{2,1,0:T(8,128)(2,1)S(1)}, u32[]{:S(2)}, u32[]{:S(2)}) %all-to-all-start.2) | async-done | bytes 294944 | tf_op jit(solution)/shard_map/all_to_all | solution.py:42
  45.3 3.5 %all-to-all-start.1 = ((bf16[8,192,96]{2,0,1:T(8,128)(2,1)}), bf16[8,192,96]{2,0,1:T(8,128)(2,1)S(1)}, u32[]{:S(2)}, u32[]{:S(2)}) async-start(bf16[8,192,96]{2,0,1:T(8,128)(2,1)} %bitcast.7), calls=%async_computation.1 | async-start | bytes 786432 | tf_op jit(solution)/shard_map/all_to_all | solution.py:45
  48.8 0.1 copy.29
  48.9 0.4 copy.30
  49.3 15.0 %all_gather.3 = bf16[8,192,192]{1,0,2:T(8,128)(2,1)S(1)} all-gather(bf16[8,192,96]{1,0,2:T(8,128)(2,1)S(1)} %copy.30), channel_id=1, replica_groups=mesh['row'=16,'col'=2] {'col'}, dimensions={2}, use_global_device_ids=true | all-gather | bytes 884736 | tf_op jit(solution)/shard_map/all_gather | solution.py:48
  64.3 0.4 copy.26
  64.7 0.2 all_to_all.53
  65.0 0.3 fusion.15
  65.3 1.0 %copy.32 = bf16[96,8,192]{0,1,2:T(8,128)(2,1)} copy(bf16[96,8,192]{2,0,1:T(8,128)(2,1)S(1)} %fusion.15) | data formatting | bytes 589824 | tf_op jit(solution)/shard_map/convert_element_type | solution.py:52
  66.2 4.5 %all-to-all-start.3 = ((bf16[96,8,192]{0,1,2:T(8,128)(2,1)}), bf16[96,8,192]{0,1,2:T(8,128)(2,1)S(1)}, u32[]{:S(2)}, u32[]{:S(2)}) async-start(bf16[96,8,192]{0,1,2:T(8,128)(2,1)} %copy.32), calls=%async_computation.3 | async-start | bytes 786432 | tf_op jit(solution)/shard_map/all_to_all | solution.py:53
  70.8 0.8 fusion.11
  71.6 11.4 %all-to-all-done.3 = bf16[96,8,192]{0,1,2:T(8,128)(2,1)S(1)} async-done(((bf16[96,8,192]{0,1,2:T(8,128)(2,1)}), bf16[96,8,192]{0,1,2:T(8,128)(2,1)S(1)}, u32[]{:S(2)}, u32[]{:S(2)}) %all-to-all-start.3) | async-done | bytes 294944 | tf_op jit(solution)/shard_map/all_to_all | solution.py:53
  83.0 0.1 fusion.29
  83.1 0.1 multiply_reduce_fusion
  83.2 0.6 copy-done.4
  83.8 1.0 %fusion.14 = bf16[12,96,128]{2,1,0:T(8,128)(2,1)} fusion(f32[12,96,128]{2,1,0:T(8,128)S(1)} %fusion.11, f32[96,12]{0,1:T(8,128)S(1)} %add_rsqrt_fusion, f32[96,12]{0,1:T(8,128)S(1)} %broadcast_multiply_fusion, bf16[128,128]{1,0:T(8,128)(2,1)S(1)} %copy-done.4, bf16[96,8,16,12]{0,1,3,2:T(8,128)(2,1)S(1)} %bitcast.61), kind=kOutput, calls=%fused_computation.21 | convolution fusion | flops 38633472 | bytes 1221632 | tf_op jit(solution)/shard_map/jci,ce->ije/dot_general | solution.py:55
  (19 shorter events, 0.1 us)
Async XLA Ops:
  0.0 1.7 %copy-start = (bf16[128,128]{1,0:T(8,128)(2,1)S(1)}, bf16[128,128]{1,0:T(8,128)(2,1)}, u32[]{:S(2)}) copy-start(bf16[128,128]{1,0:T(8,128)(2,1)} %param.12) | copy-start | bytes 98308
  0.0 1.2 %copy-start.1 = (bf16[12,96,128]{2,1,0:T(8,128)(2,1)S(1)}, bf16[12,96,128]{2,1,0:T(8,128)(2,1)}, u32[]{:S(2)}) copy-start(bf16[12,96,128]{2,1,0:T(8,128)(2,1)} %param.8) | copy-start | bytes 884740
  1.7 0.8 copy-start.7
  2.5 0.8 copy-start.2
  5.0 7.6 %copy-start.5 = (bf16[128,128]{1,0:T(8,128)(2,1)S(1)}, bf16[128,128]{1,0:T(8,128)(2,1)}, u32[]{:S(2)}) copy-start(bf16[128,128]{1,0:T(8,128)(2,1)} %param.10) | copy-start | bytes 98308
  5.0 21.8 %all-to-all-start = ((bf16[128,12,96]{2,1,0:T(8,128)(2,1)}), bf16[128,12,96]{2,1,0:T(8,128)(2,1)S(1)}, u32[]{:S(2)}, u32[]{:S(2)}) async-start(bf16[128,12,96]{2,1,0:T(8,128)(2,1)} %copy.22), calls=%async_computation | async-start | bytes 1048576 | tf_op jit(solution)/shard_map/all_to_all | solution.py:43
  12.6 0.8 copy-start.3
  26.8 18.4 %all-to-all-start.2 = ((bf16[128,12,96]{2,1,0:T(8,128)(2,1)}), bf16[128,12,96]{2,1,0:T(8,128)(2,1)S(1)}, u32[]{:S(2)}, u32[]{:S(2)}) async-start(bf16[128,12,96]{2,1,0:T(8,128)(2,1)} %copy.27), calls=%async_computation.2 | async-start | bytes 1048576 | tf_op jit(solution)/shard_map/all_to_all | solution.py:42
  45.3 19.0 %all-to-all-start.1 = ((bf16[8,192,96]{2,0,1:T(8,128)(2,1)}), bf16[8,192,96]{2,0,1:T(8,128)(2,1)S(1)}, u32[]{:S(2)}, u32[]{:S(2)}) async-start(bf16[8,192,96]{2,0,1:T(8,128)(2,1)} %bitcast.7), calls=%async_computation.1 | async-start | bytes 786432 | tf_op jit(solution)/shard_map/all_to_all | solution.py:45
  66.2 4.6 %copy-start.6 = (bf16[128,128]{1,0:T(8,128)(2,1)S(1)}, bf16[128,128]{1,0:T(8,128)(2,1)}, u32[]{:S(2)}) copy-start(bf16[128,128]{1,0:T(8,128)(2,1)} %param.14) | copy-start | bytes 98308
  66.2 16.7 %all-to-all-start.3 = ((bf16[96,8,192]{0,1,2:T(8,128)(2,1)}), bf16[96,8,192]{0,1,2:T(8,128)(2,1)S(1)}, u32[]{:S(2)}, u32[]{:S(2)}) async-start(bf16[96,8,192]{0,1,2:T(8,128)(2,1)} %copy.32), calls=%async_computation.3 | async-start | bytes 786432 | tf_op jit(solution)/shard_map/all_to_all | solution.py:53
  83.1 0.8 copy-start.4
where the time goes:
time: 85.6 us; the launch traced here: 84.8 us
  waiting for transfers between devices  36.5 us (43%)
  starting transfers between devices  19.7 us (23%)
  blocking collectives  15 us (18%)
  local copies, waits for them, and re-layouts  6.45 us (8%)
  matrix products  4.94 us (6%)
  other arithmetic  1.92 us (2%)
    all_gather x1, blocking collectives, local(): lax.all_gather(left_rows, 'col', axis=2, tiled=True)  15 us
    all_to_all x1, waiting for transfers between devices, local(): lax.all_to_all(left, 'row', split_axis=0, concat_axis=1, tiled=True)  13.4 us
    all_to_all x1, waiting for transfers between devices, local(): lax.all_to_all(right, 'row', split_axis=0, concat_axis=1, tiled=True)  11.7 us
    all_to_all x1, waiting for transfers between devices, local(): lax.all_to_all(triangle, 'row', split_axis=2, concat_axis=1, tiled=True)  11.4 us
    all_to_all x1, starting transfers between devices, local(): lax.all_to_all(right, 'row', split_axis=0, concat_axis=1, tiled=True)  7.55 us
    all_to_all x1, starting transfers between devices, local(): lax.all_to_all(triangle, 'row', split_axis=2, concat_axis=1, tiled=True)  4.54 us
    all_to_all x1, starting transfers between devices, local(): lax.all_to_all(left, 'row', split_axis=0, concat_axis=1, tiled=True)  4.16 us
    all_to_all x1, starting transfers between devices, local(): lax.all_to_all(right_rows, 'col', split_axis=1, concat_axis=2, tiled=True)  3.47 us
  transfers between devices with their start and end apart: 4, of which 3 were waited for; matrix products, arithmetic and copies ran while one was open for 5% of the time, Pallas kernels for 0%

commit v1 on v0

v1 whole, which is shorter than its diff:
```python
import functools

import jax
import jax.numpy as jnp
from jax import lax
from jax.experimental import pallas as pl
from jax.experimental.pallas import tpu as pltpu
from jax.sharding import PartitionSpec as P

TILES = 12
LANES = 128
SUBLANES = 8
EPS = 1e-05
F32 = jnp.float32
BF16 = jnp.bfloat16
NT = (((1,), (1,)), ((), ()))
TN = (((0,), (0,)), ((), ()))


def norm_axis(values, axis):
    mean = jnp.mean(values, axis=axis, keepdims=True)
    centred = values - mean
    spread = jnp.mean(centred * centred, axis=axis, keepdims=True)
    return centred * lax.rsqrt(spread + EPS)


def dot(a, b, dims=(((1,), (0,)), ((), ()))):
    return lax.dot_general(a, b, dims, preferred_element_type=F32)


def project_kernel(cols, tile, owned, x_ref, mask_ref, lg_ref, l_ref, rg_ref, r_ref, out_ref):
    pairs, width = x_ref.shape
    channels = l_ref.shape[1]
    row = lax.broadcasted_iota(jnp.int32, (2 * channels, channels), 0)
    channel = lax.broadcasted_iota(jnp.int32, (2 * channels, channels), 1)
    within = row % (2 * owned)
    source = row // (2 * owned) * owned + within % owned
    hit = source == channel
    pick_left = jnp.where(hit & (within < owned), 1.0, 0.0).astype(BF16)
    pick_right = jnp.where(hit & (within >= owned), 1.0, 0.0).astype(BF16)
    gates = (dot(pick_left, lg_ref[...], NT) + dot(pick_right, rg_ref[...], NT)).astype(BF16)
    values = (dot(pick_left, l_ref[...], NT) + dot(pick_right, r_ref[...], NT)).astype(BF16)
    for start in range(0, pairs, LANES):
        normed = norm_axis(x_ref[pl.ds(start, LANES), :].astype(F32), 1).astype(BF16)
        gate = jax.nn.sigmoid(dot(gates, normed, NT))
        value = dot(values, normed, NT)
        kept = mask_ref[:, pl.ds(start, LANES)]
        made = (gate * value * kept).astype(BF16)
        out_ref[:, :, pl.ds(start, LANES)] = made.reshape(out_ref.shape[0], 2 * owned, LANES)


def triangle_kernel(rows, cols, owned, in_ref, out_ref, factors, products):
    blocks, splits = in_ref.shape[0], in_ref.shape[1]
    group = 2 * owned
    for q in range(splits):
        for r in range(blocks):
            flat = in_ref[r, q].astype(F32)
            for i in range(rows):
                at = (r * rows + i) * group
                factors[q, pl.ds(at, group), :] = flat[:, i * cols : (i + 1) * cols]
    residues = blocks * rows
    for c in range(owned):
        left = [factors[q, pl.ds(c, residues, group), :].astype(BF16) for q in range(splits)]
        right = [factors[q, pl.ds(owned + c, residues, group), :].astype(BF16) for q in range(splits)]
        for q in range(splits):
            total = sum(
                dot(left[s], right[s][q * cols : (q + 1) * cols], NT) for s in range(splits)
            )
            products[q, pl.ds(c, residues, owned), :] = total
    for q in range(splits):
        for r in range(blocks):
            pieces = [products[q, pl.ds((r * rows + i) * owned, owned), :] for i in range(rows)]
            out_ref[r, q] = jnp.concatenate(pieces, axis=1).astype(BF16)


def gate_kernel(x_ref, w_ref, out_ref):
    normed = norm_axis(x_ref[...].astype(F32), 1).astype(BF16)
    out_ref[...] = jax.nn.sigmoid(dot(normed, w_ref[...]))


def output_kernel(t_ref, gate_ref, w_ref, out_ref):
    pairs = gate_ref.shape[0]
    for start in range(0, pairs, LANES):
        scaled = norm_axis(t_ref[:, pl.ds(start, LANES)].astype(F32), 0).astype(BF16)
        projected = dot(scaled, w_ref[...], TN)
        here = pl.ds(start, LANES)
        out_ref[here, :] = (gate_ref[here, :] * projected).astype(BF16)


def call(body, out, scratch=(), flops=0, **params):
    return pl.pallas_call(
        body,
        out_shape=out,
        scratch_shapes=list(scratch),
        cost_estimate=pl.CostEstimate(flops=flops, bytes_accessed=flops // 100, transcendentals=0),
        compiler_params=pltpu.CompilerParams(**params),
    )


def mask_of(tile_mask, rows, cols):
    tile = rows * lax.axis_size("row") // TILES
    tile_range = lax.iota(jnp.int32, TILES)
    row_ids = (lax.axis_index("row") * rows + lax.iota(jnp.int32, rows)) // tile
    col_ids = (lax.axis_index("col") * cols + lax.iota(jnp.int32, cols)) // tile
    row_hot = (row_ids[:, None] == tile_range[None, :]).astype(F32)
    col_hot = (col_ids[:, None] == tile_range[None, :]).astype(F32)
    some = dot(row_hot, tile_mask.astype(F32))
    return dot(some, col_hot.T)


def by_channels(pair_act, tile_mask, w_left_gate, w_left, w_right_gate, w_right, w_out_gate, w_out):
    rows, cols, width = pair_act.shape
    blocks, splits = lax.axis_size("row"), lax.axis_size("col")
    devices = blocks * splits
    channels = w_left.shape[1]
    owned = channels // devices
    pairs = rows * cols
    tile = rows * blocks // TILES
    flat = pair_act.reshape(pairs, width)
    pair_mask = mask_of(tile_mask, rows, cols).reshape(1, pairs)
    factors = call(
        functools.partial(project_kernel, cols, tile, owned),
        jax.ShapeDtypeStruct((devices, 2 * owned, pairs), BF16),
        flops=8 * pairs * width * channels,
    )(flat, pair_mask, w_left_gate, w_left, w_right_gate, w_right)
    factors = lax.all_to_all(factors, ("row", "col"), 0, 0, tiled=True)
    gate = call(
        gate_kernel, jax.ShapeDtypeStruct((pairs, width), F32), flops=2 * pairs * width * width
    )(flat, w_out_gate)
    residues = rows * blocks
    triangle = call(
        functools.partial(triangle_kernel, rows, cols, owned),
        jax.ShapeDtypeStruct((blocks, splits, owned, pairs), BF16),
        scratch=(
            pltpu.VMEM((splits, residues * 2 * owned, cols), F32),
            pltpu.VMEM((splits, residues * owned, cols), F32),
        ),
        flops=2 * owned * residues**3,
    )(factors.reshape(blocks, splits, 2 * owned, pairs))
    owned_pairs = lax.all_to_all(
        triangle.reshape(devices, owned, pairs), ("row", "col"), 0, 0, tiled=True
    )
    out = call(
        output_kernel,
        jax.ShapeDtypeStruct((pairs, width), BF16),
        flops=2 * pairs * width * channels,
    )(owned_pairs.reshape(channels, pairs), gate, w_out)
    return out.reshape(rows, cols, width)


def by_rows(pair_act, tile_mask, w_left_gate, w_left, w_right_gate, w_right, w_out_gate, w_out):
    rows, cols, width = pair_act.shape
    normed = norm_axis(pair_act.astype(F32), 2).astype(BF16)
    pair_mask = mask_of(tile_mask, rows, cols)

    def project(weight):
        return jnp.einsum("ijd,de->eij", normed, weight, preferred_element_type=F32)

    left = (jax.nn.sigmoid(project(w_left_gate)) * project(w_left) * pair_mask[None]).astype(BF16)
    right = (jax.nn.sigmoid(project(w_right_gate)) * project(w_right) * pair_mask[None]).astype(
        BF16
    )
    left_rows, right_rows = (
        lax.all_to_all(left, "row", split_axis=0, concat_axis=1, tiled=True),
        lax.all_to_all(right, "row", split_axis=0, concat_axis=1, tiled=True),
    )
    right_block = lax.all_to_all(right_rows, "col", split_axis=1, concat_axis=2, tiled=True)
    triangle = jnp.einsum(
        "cik,cjk->jci",
        lax.all_gather(left_rows, "col", axis=2, tiled=True),
        right_block,
        preferred_element_type=F32,
    )
    triangle = triangle.astype(BF16)
    owned = lax.all_to_all(triangle, "row", split_axis=2, concat_axis=1, tiled=True)
    scaled = norm_axis(owned.astype(F32), 1).astype(BF16)
    projected = jnp.einsum("jci,ce->ije", scaled, w_out, preferred_element_type=F32)
    gate = jax.nn.sigmoid(jnp.einsum("ijd,de->ije", normed, w_out_gate, preferred_element_type=F32))
    return (gate * projected).astype(BF16)


def local(pair_act, tile_mask, w_left_gate, *weights):
    devices = lax.axis_size("row") * lax.axis_size("col")
    rows, cols, width = pair_act.shape
    channels = w_left_gate.shape[1]
    whole = channels % devices == 0 and 2 * channels // devices % SUBLANES == 0
    aligned = rows * cols % LANES == 0 and cols % SUBLANES == 0 and cols <= LANES
    form = by_channels if whole and aligned else by_rows
    return form(pair_act, tile_mask, w_left_gate, *weights)


def solution(mesh):
    return jax.shard_map(
        local,
        mesh=mesh,
        in_specs=(P("row", "col", None), P(), P(), P(), P(), P(), P(), P()),
        out_specs=P("row", "col", None),
        check_vma=False,
    )
```

time: 85.6 us -> 49.3 us (0.58)
  waiting for transfers between devices: 36.5 us -> 8.88 us
  starting transfers between devices: 19.7 us -> 3.62 us
  Pallas kernels: 0 us -> 10.1 us
  blocking collectives: 15 us -> 23.8 us
  matrix products: 4.94 us -> 0.29 us
  local copies, waits for them, and re-layouts: 6.45 us -> 2.15 us
  other arithmetic: 1.92 us -> 0.02 us
    all_to_all x4 -> x1, waiting for transfers between devices: 36.5 us -> 8.88 us  [by_channels(): lax.all_to_all(triangle.reshape(devices, owned, pairs), ('row', 'col'), 0...]
    all_to_all x0 -> x1, blocking collectives: none -> 23.8 us  [by_channels(): factors = lax.all_to_all(factors, ('row', 'col'), 0, 0, tiled=True)]
    all_to_all x4 -> x1, starting transfers between devices: 19.7 us -> 3.62 us  [by_channels(): lax.all_to_all(triangle.reshape(devices, owned, pairs), ('row', 'col'), 0...]
    all_gather x1 -> x0, blocking collectives: 15 us -> none  [local(): lax.all_gather(left_rows, 'col', axis=2, tiled=True)]
    pallas_call x0 -> x4, Pallas kernels: none -> 10.1 us  [the longest x1 2.86 us: by_channels(): call(functools.partial(project_kernel, cols, tile, owned), jax.ShapeDtype...]
    dot_general x8 -> x1, matrix products: 4.94 us -> 0.29 us  [dot(): return lax.dot_general(a, b, dims, preferred_element_type=F32)]
    convert_element_type x3 -> x0, local copies, waits for them, and re-layouts: 3.37 us -> none  [the longest x1 1.2 us: local(): (jax.nn.sigmoid(project(w_left_gate)) * project(w_left) * pair_mask[None]...]
    all_to_all x5 -> x0, local copies, waits for them, and re-layouts: 2 us -> none  [the longest x1 0.85 us: local(): lax.all_to_all(right, 'row', split_axis=0, concat_axis=1, tiled=True)]
  transfers between devices with their start and end apart: 4 -> 1, of which waited for: 3 -> 1; matrix products, arithmetic and copies ran while one was open for 5% -> 0% of each run, Pallas kernels for 0% -> 5%
where the time goes in v1:
time: 49.3 us; the launch traced here: 48.9 us
  blocking collectives  23.8 us (48%)
  Pallas kernels  10.1 us (20%)
  waiting for transfers between devices  8.88 us (18%)
  starting transfers between devices  3.62 us (7%)
  local copies, waits for them, and re-layouts  2.15 us (4%)
    all_to_all x1, blocking collectives, by_channels(): factors = lax.all_to_all(factors, ('row', 'col'), 0, 0, tiled=True)  23.8 us
    all_to_all x1, waiting for transfers between devices, by_channels(): lax.all_to_all(triangle.reshape(devices, owned, pairs), ('row', 'col'), 0...  8.88 us
    all_to_all x1, starting transfers between devices, by_channels(): lax.all_to_all(triangle.reshape(devices, owned, pairs), ('row', 'col'), 0...  3.62 us
    pallas_call x1, Pallas kernels, by_channels(): call(functools.partial(project_kernel, cols, tile, owned), jax.ShapeDtype...  2.86 us
    pallas_call x1, Pallas kernels, by_channels(): call(functools.partial(triangle_kernel, rows, cols, owned), jax.ShapeDtyp...  2.7 us
    pallas_call x1, Pallas kernels, by_channels(): call(gate_kernel, jax.ShapeDtypeStruct((pairs, width), F32), flops=2 * pa...  2.3 us
    pallas_call x1, Pallas kernels, by_channels(): call(output_kernel, jax.ShapeDtypeStruct((pairs, width), BF16), flops=2 *...  2.25 us
  transfers between devices with their start and end apart: 1, of which 1 were waited for; matrix products, arithmetic and copies ran while one was open for 0% of the time, Pallas kernels for 5%

profile of v1, /device:TPU:0, one launch (start us, length us, event | category | flops | bytes accessed | tf_op | source)
XLA Modules:
  0.0 48.9 jit_solution(17662846442240791143)
XLA Ops:
  0.0 0.0 copy-start
  0.0 0.7 %copy-done = s32[12,12]{1,0:T(8,128)S(1)} copy-done((s32[12,12]{1,0:T(8,128)S(1)}, s32[12,12]{1,0:T(8,128)}, u32[]{:S(2)}) %copy-start) | copy-done | bytes 600
  0.7 0.3 fusion
  1.0 0.7 %reshape.57.mask_ref = f32[1,1152]{1,0:T(1,128)} reshape(f32[12,96]{1,0:T(8,128)S(1)} %fusion) | data formatting | bytes 9216 | tf_op jit(solution)/shard_map/reshape | solution.py:120
  1.7 2.9 %shard_map.82 = bf16[32,8,1152]{2,1,0:T(8,128)(2,1)} custom-call(bf16[1152,128]{1,0:T(8,128)(2,1)} %bitcast.5, f32[1,1152]{1,0:T(1,128)} %reshape.57.mask_ref, bf16[128,128]{1,0:T(8,128)(2,1)} %lg_ref.1, bf16[128,128]{1,0:T(8,128)(2,1)} %l_ref.1, bf16[128,128]{1,0:T(8,128)(2,1)} %rg_ref.1, bf16[128,128]{1,0:T(8,128)(2,1)} %r_ref.1), custom_call_target="tpu_custom_call" | custom-call | flops 150994944 | bytes 1509949 | tf_op jit(solution)/shard_map/pallas_call | solution.py:121
  4.5 23.8 %all_to_all.10 = bf16[32,8,1152]{2,1,0:T(8,128)(2,1)} all-to-all(bf16[32,8,1152]{2,1,0:T(8,128)(2,1)} %shard_map.82), channel_id=1, replica_groups=mesh['row'=16,'col'=2] {'row','col'}, dimensions={0} | all-to-all | bytes 1179648 | tf_op jit(solution)/shard_map/all_to_all | solution.py:126
  28.3 2.7 %shard_map.83 = bf16[16,2,4,1152]{3,2,1,0:T(4,128)(2,1)} custom-call(bf16[16,2,8,1152]{3,2,1,0:T(8,128)(2,1)} %bitcast.4), custom_call_target="tpu_custom_call" | custom-call | flops 56623104 | bytes 566231 | tf_op jit(solution)/shard_map/pallas_call | solution.py:131
  31.0 3.6 %all-to-all-start.1 = ((bf16[32,4,1152]{2,1,0:T(4,128)(2,1)}), bf16[32,4,1152]{2,1,0:T(4,128)(2,1)S(1)}, u32[]{:S(2)}, u32[]{:S(2)}) async-start(bf16[32,4,1152]{2,1,0:T(4,128)(2,1)} %bitcast.7), calls=%async_computation.1 | async-start | bytes 589824 | tf_op jit(solution)/shard_map/all_to_all | solution.py:140
  34.7 2.3 %shard_map.84.gate_ref = f32[1152,128]{1,0:T(8,128)} custom-call(bf16[1152,128]{1,0:T(8,128)(2,1)} %bitcast.6, bf16[128,128]{1,0:T(8,128)(2,1)} %w_ref.2), custom_call_target="tpu_custom_call" | custom-call | flops 37748736 | bytes 377487 | tf_op jit(solution)/shard_map/pallas_call | solution.py:127
  37.0 8.9 %all-to-all-done.1 = bf16[32,4,1152]{2,1,0:T(4,128)(2,1)S(1)} async-done(((bf16[32,4,1152]{2,1,0:T(4,128)(2,1)}), bf16[32,4,1152]{2,1,0:T(4,128)(2,1)S(1)}, u32[]{:S(2)}, u32[]{:S(2)}) %all-to-all-start.1) | async-done | bytes 294944 | tf_op jit(solution)/shard_map/all_to_all | solution.py:140
  45.8 0.8 %reshape.60.t_ref = bf16[128,1152]{1,0:T(8,128)(2,1)} reshape(bf16[32,4,1152]{2,1,0:T(4,128)(2,1)S(1)} %all-to-all-done.1) | data formatting | bytes 589824 | tf_op jit(solution)/shard_map/reshape | solution.py:147
  46.6 2.3 %shard_map.85 = bf16[1152,128]{1,0:T(8,128)(2,1)} custom-call(bf16[128,1152]{1,0:T(8,128)(2,1)} %reshape.60.t_ref, f32[1152,128]{1,0:T(8,128)} %shard_map.84.gate_ref, bf16[128,128]{1,0:T(8,128)(2,1)} %w_ref.3), custom_call_target="tpu_custom_call" | custom-call | flops 37748736 | bytes 377487 | tf_op jit(solution)/shard_map/pallas_call | solution.py:143
  (2 shorter events, 0.0 us)
Async XLA Ops:
  0.0 0.7 %copy-start = (s32[12,12]{1,0:T(8,128)S(1)}, s32[12,12]{1,0:T(8,128)}, u32[]{:S(2)}) copy-start(s32[12,12]{1,0:T(8,128)} %param.9) | copy-start | bytes 1732
  31.0 14.8 %all-to-all-start.1 = ((bf16[32,4,1152]{2,1,0:T(4,128)(2,1)}), bf16[32,4,1152]{2,1,0:T(4,128)(2,1)S(1)}, u32[]{:S(2)}, u32[]{:S(2)}) async-start(bf16[32,4,1152]{2,1,0:T(4,128)(2,1)} %bitcast.7), calls=%async_computation.1 | async-start | bytes 589824 | tf_op jit(solution)/shard_map/all_to_all | solution.py:140

commit v2 on v1

--- a/solution.py
+++ b/solution.py
@@ -11,6 +11,8 @@
 LANES = 128
 SUBLANES = 8
 EPS = 1e-05
+GRANT = 16 * 2**20
+WIDE = 60 * 2**20
 F32 = jnp.float32
 BF16 = jnp.bfloat16
 NT = (((1,), (1,)), ((), ()))
@@ -28,7 +30,28 @@
     return lax.dot_general(a, b, dims, preferred_element_type=F32)
 
 
-def project_kernel(cols, tile, owned, x_ref, mask_ref, lg_ref, l_ref, rg_ref, r_ref, out_ref):
+def lane_mask(cols, tile, pairs, rows, tiles):
+    kinds = tiles.shape[0]
+    place = lax.broadcasted_iota(jnp.int32, (kinds, pairs), 1).astype(F32) + 0.5
+    kind = lax.broadcasted_iota(jnp.int32, (kinds, pairs), 0).astype(F32)
+    row = jnp.floor(place * (1.0 / cols))
+    col = place - row * cols
+    first_row = (lax.axis_index("row") * rows).astype(F32)
+    first_col = (lax.axis_index("col") * cols).astype(F32)
+    row_kind = jnp.floor((row + first_row + 0.5) * (1.0 / tile))
+    col_kind = jnp.floor((col + first_col) * (1.0 / tile))
+    row_hot = jnp.where(row_kind == kind, 1.0, 0.0)
+    col_hot = jnp.where(col_kind == kind, 1.0, 0.0).astype(BF16)
+    return jnp.sum(row_hot * dot(tiles.astype(F32).astype(BF16), col_hot), axis=0, keepdims=True)
+
+
+def project_kernel(rows, tile, owned, *refs):
+    far, (out_far, gate_far), near, (out_ref, gate_ref) = refs[:7], refs[7:9], refs[9:16], refs[16:18]
+    in_sems, out_sems = refs[18:]
+    copies = [pltpu.make_async_copy(a, b, in_sems.at[n]) for n, (a, b) in enumerate(zip(far, near))]
+    for copy in copies:
+        copy.start()
+    x_ref, tiles_ref, lg_ref, l_ref, rg_ref, r_ref, og_ref = near
     pairs, width = x_ref.shape
     channels = l_ref.shape[1]
     row = lax.broadcasted_iota(jnp.int32, (2 * channels, channels), 0)
@@ -38,15 +61,30 @@
     hit = source == channel
     pick_left = jnp.where(hit & (within < owned), 1.0, 0.0).astype(BF16)
     pick_right = jnp.where(hit & (within >= owned), 1.0, 0.0).astype(BF16)
+    for copy in copies:
+        copy.wait()
     gates = (dot(pick_left, lg_ref[...], NT) + dot(pick_right, rg_ref[...], NT)).astype(BF16)
     values = (dot(pick_left, l_ref[...], NT) + dot(pick_right, r_ref[...], NT)).astype(BF16)
-    for start in range(0, pairs, LANES):
-        normed = norm_axis(x_ref[pl.ds(start, LANES), :].astype(F32), 1).astype(BF16)
+    mask = lane_mask(pairs // rows, tile, pairs, rows, tiles_ref[...])
+    sent = []
+    for n, start in enumerate(range(0, pairs, LANES)):
+        here = pl.ds(start, LANES)
+        normed = norm_axis(x_ref[here, :].astype(F32), 1).astype(BF16)
         gate = jax.nn.sigmoid(dot(gates, normed, NT))
         value = dot(values, normed, NT)
-        kept = mask_ref[:, pl.ds(start, LANES)]
-        made = (gate * value * kept).astype(BF16)
-        out_ref[:, :, pl.ds(start, LANES)] = made.reshape(out_ref.shape[0], 2 * owned, LANES)
+        made = (gate * value * mask[:, start : start + LANES]).astype(BF16)
+        out_ref[:, :, here] = made.reshape(out_ref.shape[0], 2 * owned, LANES)
+        gate_ref[here, :] = jax.nn.sigmoid(dot(normed, og_ref[...]))
+        out_slice, gate_slice = (slice(None), slice(None), here), (here, slice(None))
+        for m, (near_ref, far_ref, part) in enumerate(
+            ((out_ref, out_far, out_slice), (gate_ref, gate_far, gate_slice))
+        ):
+            sent.append(
+                pltpu.make_async_copy(near_ref.at[part], far_ref.at[part], out_sems.at[m, n])
+            )
+            sent[-1].start()
+    for copy in sent:
+        copy.wait()
 
 
 def triangle_kernel(rows, cols, owned, in_ref, out_ref, factors, products):
@@ -73,28 +111,27 @@
             out_ref[r, q] = jnp.concatenate(pieces, axis=1).astype(BF16)
 
 
-def gate_kernel(x_ref, w_ref, out_ref):
-    normed = norm_axis(x_ref[...].astype(F32), 1).astype(BF16)
-    out_ref[...] = jax.nn.sigmoid(dot(normed, w_ref[...]))
-
-
 def output_kernel(t_ref, gate_ref, w_ref, out_ref):
     pairs = gate_ref.shape[0]
+    channels = w_ref.shape[0]
     for start in range(0, pairs, LANES):
-        scaled = norm_axis(t_ref[:, pl.ds(start, LANES)].astype(F32), 0).astype(BF16)
+        triangle = t_ref[:, :, pl.ds(start, LANES)].reshape(channels, LANES).astype(F32)
+        scaled = norm_axis(triangle, 0).astype(BF16)
         projected = dot(scaled, w_ref[...], TN)
         here = pl.ds(start, LANES)
         out_ref[here, :] = (gate_ref[here, :] * projected).astype(BF16)
 
 
-def call(body, out, scratch=(), flops=0, **params):
+def call(body, out, operands, scratch=(), flops=0, space=pltpu.VMEM, grant=GRANT):
     return pl.pallas_call(
         body,
         out_shape=out,
+        in_specs=[pl.BlockSpec(memory_space=space)] * len(operands),
+        out_specs=jax.tree.map(lambda _: pl.BlockSpec(memory_space=space), out),
         scratch_shapes=list(scratch),
         cost_estimate=pl.CostEstimate(flops=flops, bytes_accessed=flops // 100, transcendentals=0),
-        compiler_params=pltpu.CompilerParams(**params),
-    )
+        compiler_params=pltpu.CompilerParams(vmem_limit_bytes=grant),
+    )(*operands)
 
 
 def mask_of(tile_mask, rows, cols):
@@ -117,34 +154,43 @@
     pairs = rows * cols
     tile = rows * blocks // TILES
     flat = pair_act.reshape(pairs, width)
-    pair_mask = mask_of(tile_mask, rows, cols).reshape(1, pairs)
-    factors = call(
-        functools.partial(project_kernel, cols, tile, owned),
+    operands = (flat, tile_mask, w_left_gate, w_left, w_right_gate, w_right, w_out_gate)
+    made = (
         jax.ShapeDtypeStruct((devices, 2 * owned, pairs), BF16),
-        flops=8 * pairs * width * channels,
-    )(flat, pair_mask, w_left_gate, w_left, w_right_gate, w_right)
+        jax.ShapeDtypeStruct((pairs, width), F32),
+    )
+    factors, gate = call(
+        functools.partial(project_kernel, rows, tile, owned),
+        made,
+        operands,
+        scratch=[pltpu.VMEM(a.shape, a.dtype) for a in operands + made]
+        + [pltpu.SemaphoreType.DMA((n,)) for n in (len(operands),)]
+        + [pltpu.SemaphoreType.DMA((len(made), pairs // LANES))],
+        flops=10 * pairs * width * channels,
+        space=pltpu.HBM,
+        grant=WIDE,
+    )
     factors = lax.all_to_all(factors, ("row", "col"), 0, 0, tiled=True)
-    gate = call(
-        gate_kernel, jax.ShapeDtypeStruct((pairs, width), F32), flops=2 * pairs * width * width
-    )(flat, w_out_gate)
     residues = rows * blocks
     triangle = call(
         functools.partial(triangle_kernel, rows, cols, owned),
         jax.ShapeDtypeStruct((blocks, splits, owned, pairs), BF16),
+        (factors.reshape(blocks, splits, 2 * owned, pairs),),
         scratch=(
             pltpu.VMEM((splits, residues * 2 * owned, cols), F32),
             pltpu.VMEM((splits, residues * owned, cols), F32),
         ),
         flops=2 * owned * residues**3,
-    )(factors.reshape(blocks, splits, 2 * owned, pairs))
+    )
     owned_pairs = lax.all_to_all(
         triangle.reshape(devices, owned, pairs), ("row", "col"), 0, 0, tiled=True
     )
     out = call(
         output_kernel,
         jax.ShapeDtypeStruct((pairs, width), BF16),
+        (owned_pairs, gate, w_out),
         flops=2 * pairs * width * channels,
-    )(owned_pairs.reshape(channels, pairs), gate, w_out)
+    )
     return out.reshape(rows, cols, width)
 
 

time: 49.3 us -> 43.9 us (0.89)
  blocking collectives: 23.8 us -> 38.3 us
  waiting for transfers between devices: 8.88 us -> 0 us
  Pallas kernels: 10.1 us -> 5.3 us
  starting transfers between devices: 3.62 us -> 0 us
  local copies, waits for them, and re-layouts: 2.15 us -> 0.01 us
    all_to_all x0 -> x1, blocking collectives: none -> 14.6 us  [by_channels(): lax.all_to_all(triangle.reshape(devices, owned, pairs), ('row', 'col'), 0...]
    all_to_all x1 -> x0, waiting for transfers between devices: 8.88 us -> none  [by_channels(): lax.all_to_all(triangle.reshape(devices, owned, pairs), ('row', 'col'), 0...]
    pallas_call x4 -> x3, Pallas kernels: 10.1 us -> 5.3 us  [call(): pl.pallas_call(body, out_shape=out, in_specs=[pl.BlockSpec(memory_space=s...]
    all_to_all x1 -> x0, starting transfers between devices: 3.62 us -> none  [by_channels(): lax.all_to_all(triangle.reshape(devices, owned, pairs), ('row', 'col'), 0...]
    reshape x2 -> x0, local copies, waits for them, and re-layouts: 1.48 us -> none  [the longest x1 0.79 us: by_channels(): owned_pairs.reshape(channels, pairs)]
    unnamed x2 -> x4, local copies, waits for them, and re-layouts: 0.66 us -> 0.01 us
  transfers between devices with their start and end apart: 1 -> 0, of which waited for: 1 -> 0; matrix products, arithmetic and copies ran while one was open for 0% -> 0% of each run, Pallas kernels for 5% -> 0%
where the time goes in v2:
time: 43.9 us; the launch traced here: 43.7 us
  blocking collectives  38.3 us (87%)
  Pallas kernels  5.3 us (12%)
    all_to_all x1, blocking collectives, by_channels(): factors = lax.all_to_all(factors, ('row', 'col'), 0, 0, tiled=True)  23.7 us
    all_to_all x1, blocking collectives, by_channels(): lax.all_to_all(triangle.reshape(devices, owned, pairs), ('row', 'col'), 0...  14.6 us
    pallas_call x3, Pallas kernels, call(): pl.pallas_call(body, out_shape=out, in_specs=[pl.BlockSpec(memory_space=s...  5.3 us

profile of v2, /device:TPU:0, one launch (start us, length us, event | category | flops | bytes accessed | tf_op | source)
XLA Modules:
  0.0 43.7 jit_solution(6891671177606493868)
XLA Ops:
  0.0 3.1 %shard_map.82 = (bf16[32,8,1152]{2,1,0:T(8,128)(2,1)}, f32[1152,128]{1,0:T(8,128)}) custom-call(bf16[1152,128]{1,0:T(8,128)(2,1)} %bitcast.6, s32[12,12]{1,0:T(8,128)} %refs_1_.1, bf16[128,128]{1,0:T(8,128)(2,1)} %refs_2_.1, bf16[128,128]{1,0:T(8,128)(2,1)} %refs_3_.1, bf16[128,128]{1,0:T(8,128)(2,1)} %refs_4_.1, bf16[128,128]{1,0:T(8,128)(2,1)} %refs_5_.1, ...), custom_call_target="tpu_custom_call" | custom-call | flops 188743680 | bytes 1887436 | tf_op jit(solution)/shard_map/pallas_call | solution.py:126
  3.1 23.7 %all_to_all.10 = bf16[32,8,1152]{2,1,0:T(8,128)(2,1)S(1)} all-to-all(bf16[32,8,1152]{2,1,0:T(8,128)(2,1)} %get-tuple-element.7), channel_id=1, replica_groups=mesh['row'=16,'col'=2] {'row','col'}, dimensions={0} | all-to-all | bytes 1179648 | tf_op jit(solution)/shard_map/all_to_all | solution.py:173
  26.8 0.0 copy-start
  26.8 0.9 %shard_map.83 = bf16[16,2,4,1152]{3,2,1,0:T(4,128)(2,1)S(1)} custom-call(bf16[16,2,8,1152]{3,2,1,0:T(8,128)(2,1)S(1)} %bitcast.4), custom_call_target="tpu_custom_call" | custom-call | flops 56623104 | bytes 566231 | tf_op jit(solution)/shard_map/pallas_call | solution.py:126
  27.8 0.0 copy-start.1
  27.8 14.6 %all_to_all.11.t_ref = bf16[32,4,1152]{2,1,0:T(4,128)(2,1)S(1)} all-to-all(bf16[32,4,1152]{2,1,0:T(4,128)(2,1)S(1)} %bitcast.5), channel_id=1, replica_groups=mesh['row'=16,'col'=2] {'row','col'}, dimensions={0} | all-to-all | bytes 589824 | tf_op jit(solution)/shard_map/all_to_all | solution.py:185
  42.4 0.0 copy-done
  42.4 0.0 copy-done.1
  42.4 1.3 %shard_map.84 = bf16[1152,128]{1,0:T(8,128)(2,1)} custom-call(bf16[32,4,1152]{2,1,0:T(4,128)(2,1)S(1)} %all_to_all.11.t_ref, f32[1152,128]{1,0:T(8,128)S(1)} %copy-done, bf16[128,128]{1,0:T(8,128)(2,1)S(1)} %copy-done.1), custom_call_target="tpu_custom_call" | custom-call | flops 37748736 | bytes 377487 | tf_op jit(solution)/shard_map/pallas_call | solution.py:126
Async XLA Ops:
  26.8 15.6 %copy-start = (f32[1152,128]{1,0:T(8,128)S(1)}, f32[1152,128]{1,0:T(8,128)}, u32[]{:S(2)}) copy-start(f32[1152,128]{1,0:T(8,128)} %get-tuple-element.8.gate_ref) | copy-start | bytes 1769476
  27.8 14.6 %copy-start.1 = (bf16[128,128]{1,0:T(8,128)(2,1)S(1)}, bf16[128,128]{1,0:T(8,128)(2,1)}, u32[]{:S(2)}) copy-start(bf16[128,128]{1,0:T(8,128)(2,1)} %w_ref.1) | copy-start | bytes 98308

commit v3 on v2

--- a/solution.py
+++ b/solution.py
@@ -12,7 +12,6 @@
 SUBLANES = 8
 EPS = 1e-05
 GRANT = 16 * 2**20
-WIDE = 60 * 2**20
 F32 = jnp.float32
 BF16 = jnp.bfloat16
 NT = (((1,), (1,)), ((), ()))
@@ -46,9 +45,8 @@
 
 
 def project_kernel(rows, tile, owned, *refs):
-    far, (out_far, gate_far), near, (out_ref, gate_ref) = refs[:7], refs[7:9], refs[9:16], refs[16:18]
-    in_sems, out_sems = refs[18:]
-    copies = [pltpu.make_async_copy(a, b, in_sems.at[n]) for n, (a, b) in enumerate(zip(far, near))]
+    far, (out_ref, gate_ref), near, sems = refs[:7], refs[7:9], refs[9:16], refs[16]
+    copies = [pltpu.make_async_copy(a, b, sems.at[n]) for n, (a, b) in enumerate(zip(far, near))]
     for copy in copies:
         copy.start()
     x_ref, tiles_ref, lg_ref, l_ref, rg_ref, r_ref, og_ref = near
@@ -66,8 +64,7 @@
     gates = (dot(pick_left, lg_ref[...], NT) + dot(pick_right, rg_ref[...], NT)).astype(BF16)
     values = (dot(pick_left, l_ref[...], NT) + dot(pick_right, r_ref[...], NT)).astype(BF16)
     mask = lane_mask(pairs // rows, tile, pairs, rows, tiles_ref[...])
-    sent = []
-    for n, start in enumerate(range(0, pairs, LANES)):
+    for start in range(0, pairs, LANES):
         here = pl.ds(start, LANES)
         normed = norm_axis(x_ref[here, :].astype(F32), 1).astype(BF16)
         gate = jax.nn.sigmoid(dot(gates, normed, NT))
@@ -75,16 +72,6 @@
         made = (gate * value * mask[:, start : start + LANES]).astype(BF16)
         out_ref[:, :, here] = made.reshape(out_ref.shape[0], 2 * owned, LANES)
         gate_ref[here, :] = jax.nn.sigmoid(dot(normed, og_ref[...]))
-        out_slice, gate_slice = (slice(None), slice(None), here), (here, slice(None))
-        for m, (near_ref, far_ref, part) in enumerate(
-            ((out_ref, out_far, out_slice), (gate_ref, gate_far, gate_slice))
-        ):
-            sent.append(
-                pltpu.make_async_copy(near_ref.at[part], far_ref.at[part], out_sems.at[m, n])
-            )
-            sent[-1].start()
-    for copy in sent:
-        copy.wait()
 
 
 def triangle_kernel(rows, cols, owned, in_ref, out_ref, factors, products):
@@ -122,16 +109,16 @@
         out_ref[here, :] = (gate_ref[here, :] * projected).astype(BF16)
 
 
-def call(body, out, operands, scratch=(), flops=0, space=pltpu.VMEM, grant=GRANT):
+def call(body, out, operands, scratch=(), flops=0, space=pltpu.VMEM):
     return pl.pallas_call(
         body,
         out_shape=out,
         in_specs=[pl.BlockSpec(memory_space=space)] * len(operands),
-        out_specs=jax.tree.map(lambda _: pl.BlockSpec(memory_space=space), out),
+        out_specs=jax.tree.map(lambda _: pl.BlockSpec(memory_space=pltpu.VMEM), out),
         scratch_shapes=list(scratch),
         cost_estimate=pl.CostEstimate(flops=flops, bytes_accessed=flops // 100, transcendentals=0),
-        compiler_params=pltpu.CompilerParams(vmem_limit_bytes=grant),
-    )(*operands)
+        compiler_params=pltpu.CompilerParams(vmem_limit_bytes=GRANT),
+    )(*[pltpu.with_memory_space_constraint(a, space) for a in operands])
 
 
 def mask_of(tile_mask, rows, cols):
@@ -155,26 +142,20 @@
     tile = rows * blocks // TILES
     flat = pair_act.reshape(pairs, width)
     operands = (flat, tile_mask, w_left_gate, w_left, w_right_gate, w_right, w_out_gate)
-    made = (
-        jax.ShapeDtypeStruct((devices, 2 * owned, pairs), BF16),
-        jax.ShapeDtypeStruct((pairs, width), F32),
-    )
     factors, gate = call(
         functools.partial(project_kernel, rows, tile, owned),
-        made,
+        (pltpu.VMEM((devices, 2 * owned, pairs), BF16), pltpu.VMEM((pairs, width), F32)),
         operands,
-        scratch=[pltpu.VMEM(a.shape, a.dtype) for a in operands + made]
-        + [pltpu.SemaphoreType.DMA((n,)) for n in (len(operands),)]
-        + [pltpu.SemaphoreType.DMA((len(made), pairs // LANES))],
+        scratch=[pltpu.VMEM(a.shape, a.dtype) for a in operands]
+        + [pltpu.SemaphoreType.DMA((len(operands),))],
         flops=10 * pairs * width * channels,
         space=pltpu.HBM,
-        grant=WIDE,
     )
     factors = lax.all_to_all(factors, ("row", "col"), 0, 0, tiled=True)
     residues = rows * blocks
     triangle = call(
         functools.partial(triangle_kernel, rows, cols, owned),
-        jax.ShapeDtypeStruct((blocks, splits, owned, pairs), BF16),
+        pltpu.VMEM((blocks, splits, owned, pairs), BF16),
         (factors.reshape(blocks, splits, 2 * owned, pairs),),
         scratch=(
             pltpu.VMEM((splits, residues * 2 * owned, cols), F32),

time: 43.9 us -> 42.9 us (0.977)
  Pallas kernels: 5.3 us -> 4.5 us
    pallas_call x3, Pallas kernels: 5.3 us -> 4.5 us  [call(): pl.pallas_call(body, out_shape=out, in_specs=[pl.BlockSpec(memory_space=s...]
where the time goes in v3:
time: 42.9 us; the launch traced here: 42.6 us
  blocking collectives  38.1 us (89%)
  Pallas kernels  4.5 us (10%)
    all_to_all x1, blocking collectives, by_channels(): factors = lax.all_to_all(factors, ('row', 'col'), 0, 0, tiled=True)  23.5 us
    all_to_all x1, blocking collectives, by_channels(): lax.all_to_all(triangle.reshape(devices, owned, pairs), ('row', 'col'), 0...  14.6 us
    pallas_call x3, Pallas kernels, call(): pl.pallas_call(body, out_shape=out, in_specs=[pl.BlockSpec(memory_space=s...  4.5 us

profile of v3, /device:TPU:0, one launch (start us, length us, event | category | flops | bytes accessed | tf_op | source)
XLA Modules:
  0.0 42.6 jit_solution(16851954122334604000)
XLA Ops:
  0.0 2.3 %shard_map.82 = (bf16[32,8,1152]{2,1,0:T(8,128)(2,1)S(1)}, f32[1152,128]{1,0:T(8,128)S(1)}) custom-call(bf16[1152,128]{1,0:T(8,128)(2,1)} %bitcast.6, s32[12,12]{1,0:T(8,128)} %refs_1_.1, bf16[128,128]{1,0:T(8,128)(2,1)} %refs_2_.1, bf16[128,128]{1,0:T(8,128)(2,1)} %refs_3_.1, bf16[128,128]{1,0:T(8,128)(2,1)} %refs_4_.1, bf16[128,128]{1,0:T(8,128)(2,1)} %refs_5_.1, ...), custom_call_target="tpu_custom_call" | custom-call | flops 188743680 | bytes 1887436 | tf_op jit(solution)/shard_map/pallas_call | solution.py:113
  2.3 23.5 %all_to_all.10 = bf16[32,8,1152]{2,1,0:T(8,128)(2,1)S(1)} all-to-all(bf16[32,8,1152]{2,1,0:T(8,128)(2,1)S(1)} %get-tuple-element.7), channel_id=1, replica_groups=mesh['row'=16,'col'=2] {'row','col'}, dimensions={0} | all-to-all | bytes 1179648 | tf_op jit(solution)/shard_map/all_to_all | solution.py:154
  25.8 0.9 %shard_map.83 = bf16[16,2,4,1152]{3,2,1,0:T(4,128)(2,1)S(1)} custom-call(bf16[16,2,8,1152]{3,2,1,0:T(8,128)(2,1)S(1)} %bitcast.4), custom_call_target="tpu_custom_call" | custom-call | flops 56623104 | bytes 566231 | tf_op jit(solution)/shard_map/pallas_call | solution.py:113
  26.7 0.0 copy-start
  26.8 14.6 %all_to_all.11.t_ref = bf16[32,4,1152]{2,1,0:T(4,128)(2,1)S(1)} all-to-all(bf16[32,4,1152]{2,1,0:T(4,128)(2,1)S(1)} %bitcast.5), channel_id=1, replica_groups=mesh['row'=16,'col'=2] {'row','col'}, dimensions={0} | all-to-all | bytes 589824 | tf_op jit(solution)/shard_map/all_to_all | solution.py:166
  41.4 0.0 copy-done
  41.4 1.3 %shard_map.84 = bf16[1152,128]{1,0:T(8,128)(2,1)} custom-call(bf16[32,4,1152]{2,1,0:T(4,128)(2,1)S(1)} %all_to_all.11.t_ref, f32[1152,128]{1,0:T(8,128)S(1)} %get-tuple-element.8.gate_ref, bf16[128,128]{1,0:T(8,128)(2,1)S(1)} %copy-done), custom_call_target="tpu_custom_call" | custom-call | flops 37748736 | bytes 377487 | tf_op jit(solution)/shard_map/pallas_call | solution.py:113
Async XLA Ops:
  26.7 14.6 %copy-start = (bf16[128,128]{1,0:T(8,128)(2,1)S(1)}, bf16[128,128]{1,0:T(8,128)(2,1)}, u32[]{:S(2)}) copy-start(bf16[128,128]{1,0:T(8,128)(2,1)} %w_ref.1) | copy-start | bytes 98308

commit v4 on v3

--- a/solution.py
+++ b/solution.py
@@ -75,11 +75,11 @@
 
 
 def triangle_kernel(rows, cols, owned, in_ref, out_ref, factors, products):
-    blocks, splits = in_ref.shape[0], in_ref.shape[1]
+    splits, blocks = in_ref.shape[0], in_ref.shape[1]
     group = 2 * owned
     for q in range(splits):
         for r in range(blocks):
-            flat = in_ref[r, q].astype(F32)
+            flat = in_ref[q, r].astype(F32)
             for i in range(rows):
                 at = (r * rows + i) * group
                 factors[q, pl.ds(at, group), :] = flat[:, i * cols : (i + 1) * cols]
@@ -95,7 +95,7 @@
     for q in range(splits):
         for r in range(blocks):
             pieces = [products[q, pl.ds((r * rows + i) * owned, owned), :] for i in range(rows)]
-            out_ref[r, q] = jnp.concatenate(pieces, axis=1).astype(BF16)
+            out_ref[q, r] = jnp.concatenate(pieces, axis=1).astype(BF16)
 
 
 def output_kernel(t_ref, gate_ref, w_ref, out_ref):
@@ -151,12 +151,12 @@
         flops=10 * pairs * width * channels,
         space=pltpu.HBM,
     )
-    factors = lax.all_to_all(factors, ("row", "col"), 0, 0, tiled=True)
+    factors = lax.all_to_all(factors, ("col", "row"), 0, 0, tiled=True)
     residues = rows * blocks
     triangle = call(
         functools.partial(triangle_kernel, rows, cols, owned),
-        pltpu.VMEM((blocks, splits, owned, pairs), BF16),
-        (factors.reshape(blocks, splits, 2 * owned, pairs),),
+        pltpu.VMEM((splits, blocks, owned, pairs), BF16),
+        (factors.reshape(splits, blocks, 2 * owned, pairs),),
         scratch=(
             pltpu.VMEM((splits, residues * 2 * owned, cols), F32),
             pltpu.VMEM((splits, residues * owned, cols), F32),
@@ -164,7 +164,7 @@
         flops=2 * owned * residues**3,
     )
     owned_pairs = lax.all_to_all(
-        triangle.reshape(devices, owned, pairs), ("row", "col"), 0, 0, tiled=True
+        triangle.reshape(devices, owned, pairs), ("col", "row"), 0, 0, tiled=True
     )
     out = call(
         output_kernel,

time: 42.9 us -> 42.2 us (0.984)
  blocking collectives: 38.1 us -> 37.4 us
    all_to_all x2, blocking collectives: 38.1 us -> 37.4 us  [the longest x1 24.4 us: by_channels(): factors = lax.all_to_all(factors, ('col', 'row'), 0, 0, tiled=True)]
where the time goes in v4:
time: 42.2 us; the launch traced here: 42 us
  blocking collectives  37.4 us (89%)
  Pallas kernels  4.5 us (11%)
    all_to_all x1, blocking collectives, by_channels(): factors = lax.all_to_all(factors, ('col', 'row'), 0, 0, tiled=True)  24.4 us
    all_to_all x1, blocking collectives, by_channels(): lax.all_to_all(triangle.reshape(devices, owned, pairs), ('col', 'row'), 0...  13 us
    pallas_call x3, Pallas kernels, call(): pl.pallas_call(body, out_shape=out, in_specs=[pl.BlockSpec(memory_space=s...  4.5 us

profile of v4, /device:TPU:0, one launch (start us, length us, event | category | flops | bytes accessed | tf_op | source)
XLA Modules:
  0.0 42.0 jit_solution(15936832603027058963)
XLA Ops:
  0.0 2.3 %shard_map.82 = (bf16[32,8,1152]{2,1,0:T(8,128)(2,1)S(1)}, f32[1152,128]{1,0:T(8,128)S(1)}) custom-call(bf16[1152,128]{1,0:T(8,128)(2,1)} %bitcast.6, s32[12,12]{1,0:T(8,128)} %refs_1_.1, bf16[128,128]{1,0:T(8,128)(2,1)} %refs_2_.1, bf16[128,128]{1,0:T(8,128)(2,1)} %refs_3_.1, bf16[128,128]{1,0:T(8,128)(2,1)} %refs_4_.1, bf16[128,128]{1,0:T(8,128)(2,1)} %refs_5_.1, ...), custom_call_target="tpu_custom_call" | custom-call | flops 188743680 | bytes 1887436 | tf_op jit(solution)/shard_map/pallas_call | solution.py:113
  2.3 24.4 %all_to_all.10 = bf16[32,8,1152]{2,1,0:T(8,128)(2,1)S(1)} all-to-all(bf16[32,8,1152]{2,1,0:T(8,128)(2,1)S(1)} %get-tuple-element.7), channel_id=1, replica_groups=mesh['row'=16,'col'=2] {'col','row'}, dimensions={0} | all-to-all | bytes 1179648 | tf_op jit(solution)/shard_map/all_to_all | solution.py:154
  26.7 0.9 %shard_map.83 = bf16[2,16,4,1152]{3,2,1,0:T(4,128)(2,1)S(1)} custom-call(bf16[2,16,8,1152]{3,2,1,0:T(8,128)(2,1)S(1)} %bitcast.4), custom_call_target="tpu_custom_call" | custom-call | flops 56623104 | bytes 566231 | tf_op jit(solution)/shard_map/pallas_call | solution.py:113
  27.6 0.0 copy-start
  27.7 13.0 %all_to_all.11.t_ref = bf16[32,4,1152]{2,1,0:T(4,128)(2,1)S(1)} all-to-all(bf16[32,4,1152]{2,1,0:T(4,128)(2,1)S(1)} %bitcast.5), channel_id=1, replica_groups=mesh['row'=16,'col'=2] {'col','row'}, dimensions={0} | all-to-all | bytes 589824 | tf_op jit(solution)/shard_map/all_to_all | solution.py:166
  40.7 0.0 copy-done
  40.7 1.3 %shard_map.84 = bf16[1152,128]{1,0:T(8,128)(2,1)} custom-call(bf16[32,4,1152]{2,1,0:T(4,128)(2,1)S(1)} %all_to_all.11.t_ref, f32[1152,128]{1,0:T(8,128)S(1)} %get-tuple-element.8.gate_ref, bf16[128,128]{1,0:T(8,128)(2,1)S(1)} %copy-done), custom_call_target="tpu_custom_call" | custom-call | flops 37748736 | bytes 377487 | tf_op jit(solution)/shard_map/pallas_call | solution.py:113
Async XLA Ops:
  27.6 13.0 %copy-start = (bf16[128,128]{1,0:T(8,128)(2,1)S(1)}, bf16[128,128]{1,0:T(8,128)(2,1)}, u32[]{:S(2)}) copy-start(bf16[128,128]{1,0:T(8,128)(2,1)} %w_ref.1) | copy-start | bytes 98308

commit v5 on v4

--- a/solution.py
+++ b/solution.py
@@ -9,6 +9,8 @@
 
 TILES = 12
 LANES = 128
+WIDE = 256
+OWIDE = 256
 SUBLANES = 8
 EPS = 1e-05
 GRANT = 16 * 2**20
@@ -63,14 +65,15 @@
         copy.wait()
     gates = (dot(pick_left, lg_ref[...], NT) + dot(pick_right, rg_ref[...], NT)).astype(BF16)
     values = (dot(pick_left, l_ref[...], NT) + dot(pick_right, r_ref[...], NT)).astype(BF16)
-    mask = lane_mask(pairs // rows, tile, pairs, rows, tiles_ref[...])
-    for start in range(0, pairs, LANES):
-        here = pl.ds(start, LANES)
+    mask = lane_mask(pairs // rows, tile, pairs, rows, tiles_ref[...]).astype(BF16)
+    for start in range(0, pairs, WIDE):
+        wide = min(WIDE, pairs - start)
+        here = pl.ds(start, wide)
         normed = norm_axis(x_ref[here, :].astype(F32), 1).astype(BF16)
         gate = jax.nn.sigmoid(dot(gates, normed, NT))
         value = dot(values, normed, NT)
-        made = (gate * value * mask[:, start : start + LANES]).astype(BF16)
-        out_ref[:, :, here] = made.reshape(out_ref.shape[0], 2 * owned, LANES)
+        made = (gate * value).astype(BF16) * mask[:, start : start + wide]
+        out_ref[:, :, here] = made.reshape(out_ref.shape[0], 2 * owned, wide)
         gate_ref[here, :] = jax.nn.sigmoid(dot(normed, og_ref[...]))
 
 
@@ -84,14 +87,24 @@
                 at = (r * rows + i) * group
                 factors[q, pl.ds(at, group), :] = flat[:, i * cols : (i + 1) * cols]
     residues = blocks * rows
+    gap = LANES - cols
     for c in range(owned):
         left = [factors[q, pl.ds(c, residues, group), :].astype(BF16) for q in range(splits)]
         right = [factors[q, pl.ds(owned + c, residues, group), :].astype(BF16) for q in range(splits)]
+        empty = jnp.zeros((gap, cols), BF16)
+        spread = [
+            jnp.concatenate(
+                [p for q in range(splits) for p in (r[q * cols : (q + 1) * cols], empty)], axis=0
+            )
+            for r in right
+        ]
+        none = jnp.zeros((residues, gap), BF16)
+        lefts = jnp.concatenate([p for l in left for p in (l, none)], axis=1)
+        none = jnp.zeros((splits * LANES, gap), BF16)
+        rights = jnp.concatenate([p for r in spread for p in (r, none)], axis=1)
+        total = dot(lefts, rights, NT)
         for q in range(splits):
-            total = sum(
-                dot(left[s], right[s][q * cols : (q + 1) * cols], NT) for s in range(splits)
-            )
-            products[q, pl.ds(c, residues, owned), :] = total
+            products[q, pl.ds(c, residues, owned), :] = total[:, q * LANES : q * LANES + cols]
     for q in range(splits):
         for r in range(blocks):
             pieces = [products[q, pl.ds((r * rows + i) * owned, owned), :] for i in range(rows)]
@@ -101,11 +114,12 @@
 def output_kernel(t_ref, gate_ref, w_ref, out_ref):
     pairs = gate_ref.shape[0]
     channels = w_ref.shape[0]
-    for start in range(0, pairs, LANES):
-        triangle = t_ref[:, :, pl.ds(start, LANES)].reshape(channels, LANES).astype(F32)
+    for start in range(0, pairs, OWIDE):
+        wide = min(OWIDE, pairs - start)
+        triangle = t_ref[:, :, pl.ds(start, wide)].reshape(channels, wide).astype(F32)
         scaled = norm_axis(triangle, 0).astype(BF16)
         projected = dot(scaled, w_ref[...], TN)
-        here = pl.ds(start, LANES)
+        here = pl.ds(start, wide)
         out_ref[here, :] = (gate_ref[here, :] * projected).astype(BF16)
 
 

time: 42.2 us -> 41.7 us (0.988)
  Pallas kernels: 4.5 us -> 3.98 us
    pallas_call x3, Pallas kernels: 4.5 us -> 3.98 us  [call(): pl.pallas_call(body, out_shape=out, in_specs=[pl.BlockSpec(memory_space=s...]
where the time goes in v5:
time: 41.7 us; the launch traced here: 41.5 us
  blocking collectives  37.4 us (90%)
  Pallas kernels  3.98 us (10%)
    all_to_all x1, blocking collectives, by_channels(): factors = lax.all_to_all(factors, ('col', 'row'), 0, 0, tiled=True)  24.4 us
    all_to_all x1, blocking collectives, by_channels(): lax.all_to_all(triangle.reshape(devices, owned, pairs), ('col', 'row'), 0...  13 us
    pallas_call x3, Pallas kernels, call(): pl.pallas_call(body, out_shape=out, in_specs=[pl.BlockSpec(memory_space=s...  3.98 us

profile of v5, /device:TPU:0, one launch (start us, length us, event | category | flops | bytes accessed | tf_op | source)
XLA Modules:
  0.0 41.5 jit_solution(5344357986799605791)
XLA Ops:
  0.0 2.0 %shard_map.82 = (bf16[32,8,1152]{2,1,0:T(8,128)(2,1)S(1)}, f32[1152,128]{1,0:T(8,128)S(1)}) custom-call(bf16[1152,128]{1,0:T(8,128)(2,1)} %bitcast.6, s32[12,12]{1,0:T(8,128)} %refs_1_.1, bf16[128,128]{1,0:T(8,128)(2,1)} %refs_2_.1, bf16[128,128]{1,0:T(8,128)(2,1)} %refs_3_.1, bf16[128,128]{1,0:T(8,128)(2,1)} %refs_4_.1, bf16[128,128]{1,0:T(8,128)(2,1)} %refs_5_.1, ...), custom_call_target="tpu_custom_call" | custom-call | flops 188743680 | bytes 1887436 | tf_op jit(solution)/shard_map/pallas_call | solution.py:127
  2.0 24.4 %all_to_all.10 = bf16[32,8,1152]{2,1,0:T(8,128)(2,1)S(1)} all-to-all(bf16[32,8,1152]{2,1,0:T(8,128)(2,1)S(1)} %get-tuple-element.7), channel_id=1, replica_groups=mesh['row'=16,'col'=2] {'col','row'}, dimensions={0} | all-to-all | bytes 1179648 | tf_op jit(solution)/shard_map/all_to_all | solution.py:168
  26.4 0.8 %shard_map.83 = bf16[2,16,4,1152]{3,2,1,0:T(4,128)(2,1)S(1)} custom-call(bf16[2,16,8,1152]{3,2,1,0:T(8,128)(2,1)S(1)} %bitcast.4), custom_call_target="tpu_custom_call" | custom-call | flops 56623104 | bytes 566231 | tf_op jit(solution)/shard_map/pallas_call | solution.py:127
  27.2 0.0 copy-start
  27.3 13.0 %all_to_all.11.t_ref = bf16[32,4,1152]{2,1,0:T(4,128)(2,1)S(1)} all-to-all(bf16[32,4,1152]{2,1,0:T(4,128)(2,1)S(1)} %bitcast.5), channel_id=1, replica_groups=mesh['row'=16,'col'=2] {'col','row'}, dimensions={0} | all-to-all | bytes 589824 | tf_op jit(solution)/shard_map/all_to_all | solution.py:180
  40.3 0.0 copy-done
  40.3 1.2 %shard_map.84 = bf16[1152,128]{1,0:T(8,128)(2,1)} custom-call(bf16[32,4,1152]{2,1,0:T(4,128)(2,1)S(1)} %all_to_all.11.t_ref, f32[1152,128]{1,0:T(8,128)S(1)} %get-tuple-element.8.gate_ref, bf16[128,128]{1,0:T(8,128)(2,1)S(1)} %copy-done), custom_call_target="tpu_custom_call" | custom-call | flops 37748736 | bytes 377487 | tf_op jit(solution)/shard_map/pallas_call | solution.py:127
Async XLA Ops:
  27.2 13.0 %copy-start = (bf16[128,128]{1,0:T(8,128)(2,1)S(1)}, bf16[128,128]{1,0:T(8,128)(2,1)}, u32[]{:S(2)}) copy-start(bf16[128,128]{1,0:T(8,128)(2,1)} %w_ref.1) | copy-start | bytes 98308

commit v6 on v5

--- a/solution.py
+++ b/solution.py
@@ -6,6 +6,7 @@
 from jax.experimental import pallas as pl
 from jax.experimental.pallas import tpu as pltpu
 from jax.sharding import PartitionSpec as P
+
 
 TILES = 12
 LANES = 128
@@ -52,7 +53,7 @@
     for copy in copies:
         copy.start()
     x_ref, tiles_ref, lg_ref, l_ref, rg_ref, r_ref, og_ref = near
-    pairs, width = x_ref.shape
+    pairs, _ = x_ref.shape
     channels = l_ref.shape[1]
     row = lax.broadcasted_iota(jnp.int32, (2 * channels, channels), 0)
     channel = lax.broadcasted_iota(jnp.int32, (2 * channels, channels), 1)
@@ -123,12 +124,16 @@
         out_ref[here, :] = (gate_ref[here, :] * projected).astype(BF16)
 
 
+def space_of(out):
+    return getattr(out, "memory_space", pltpu.VMEM)
+
+
 def call(body, out, operands, scratch=(), flops=0, space=pltpu.VMEM):
     return pl.pallas_call(
         body,
         out_shape=out,
         in_specs=[pl.BlockSpec(memory_space=space)] * len(operands),
-        out_specs=jax.tree.map(lambda _: pl.BlockSpec(memory_space=pltpu.VMEM), out),
+        out_specs=jax.tree.map(lambda o: pl.BlockSpec(memory_space=space_of(o)), out),
         scratch_shapes=list(scratch),
         cost_estimate=pl.CostEstimate(flops=flops, bytes_accessed=flops // 100, transcendentals=0),
         compiler_params=pltpu.CompilerParams(vmem_limit_bytes=GRANT),
@@ -189,8 +194,204 @@
     return out.reshape(rows, cols, width)
 
 
+def halves_project_kernel(rows, tile, owned, *refs):
+    far, (left_ref, right_far, gate_ref), near = refs[:7], refs[7:10], refs[10:17]
+    right_ref, normed_ref, sems, right_sems = refs[17:]
+    copies = [pltpu.make_async_copy(a, b, sems.at[n]) for n, (a, b) in enumerate(zip(far, near))]
+    for copy in copies:
+        copy.start()
+    x_ref, tiles_ref, lg_ref, l_ref, rg_ref, r_ref, og_ref = near
+    pairs, _ = x_ref.shape
+    channels = l_ref.shape[1]
+    members = channels // owned
+    row = lax.broadcasted_iota(jnp.int32, (channels, channels), 0)
+    channel = lax.broadcasted_iota(jnp.int32, (channels, channels), 1)
+    owner = (row // owned) ^ member_number(members)
+    pick_left = jnp.where(owner * owned + row % owned == channel, 1.0, 0.0).astype(BF16)
+    pick_right = jnp.where(row == channel, 1.0, 0.0).astype(BF16)
+    for copy in copies:
+        copy.wait()
+    mask = lane_mask(pairs // rows, tile, pairs, rows, tiles_ref[...]).astype(BF16)
+    _, halves, _ = right_far.shape[:3]
+
+    def factor(pick, gate_w, value_w, target):
+        gates = dot(pick, gate_w[...], NT).astype(BF16)
+        values = dot(pick, value_w[...], NT).astype(BF16)
+
+        def make(normed, start, wide):
+            gate = jax.nn.sigmoid(dot(gates, normed, NT))
+            made = (gate * dot(values, normed, NT)).astype(BF16) * mask[:, start : start + wide]
+            target[..., pl.ds(start, wide)] = made.reshape(*target.shape[:-1], wide)
+
+        return make
+
+    make_right = factor(pick_right, rg_ref, r_ref, right_ref)
+    make_left = factor(pick_left, lg_ref, l_ref, left_ref)
+    strips = [(start, min(WIDE, pairs - start)) for start in range(0, pairs, WIDE)]
+    for start, wide in strips:
+        here = pl.ds(start, wide)
+        normed = norm_axis(x_ref[here, :].astype(F32), 1).astype(BF16)
+        normed_ref[here, :] = normed
+        make_right(normed, start, wide)
+    sent = [
+        pltpu.make_async_copy(right_ref, right_far.at[:, half], right_sems.at[half])
+        for half in range(halves)
+    ]
+    for copy in sent:
+        copy.start()
+    for start, wide in strips:
+        here = pl.ds(start, wide)
+        normed = normed_ref[here, :]
+        make_left(normed, start, wide)
+        gate_ref[here, :] = jax.nn.sigmoid(dot(normed, og_ref[...]))
+    for copy in sent:
+        copy.wait()
+
+
+def member_number(members):
+    near_rows = members // lax.axis_size("col")
+    return lax.axis_index("col") * near_rows + lax.axis_index("row") % near_rows
+
+
+def halves_triangle_kernel(rows, cols, members, steps, *refs):
+    left_refs, (right_ref, out_ref, lefts, rights, products) = refs[: len(steps)], refs[len(steps) :]
+    splits, blocks, owned = right_ref.shape[:3]
+    near_rows = members // splits
+    for q in range(splits):
+        for r in range(blocks):
+            flat = right_ref[q, r].astype(F32)
+            for i in range(rows):
+                at = (r * rows + i) * owned
+                rights[q, pl.ds(at, owned), :] = flat[:, i * cols : (i + 1) * cols]
+    me = member_number(members)
+    for left_ref, distances in zip(left_refs, steps):
+        for n, distance in enumerate(distances):
+            source = me ^ distance
+            q, r = source // near_rows, source % near_rows
+            flat = left_ref[n].astype(F32)
+            for i in range(rows):
+                at = pl.multiple_of((r * rows + i) * owned, owned)
+                lefts[q, pl.ds(at, owned), :] = flat[:, i * cols : (i + 1) * cols]
+    residues, half = blocks * rows, near_rows * rows
+    gap = LANES - cols
+    for c in range(owned):
+        left = [lefts[q, pl.ds(c, half, owned), :].astype(BF16) for q in range(splits)]
+        right = [rights[q, pl.ds(c, residues, owned), :].astype(BF16) for q in range(splits)]
+        empty = jnp.zeros((gap, cols), BF16)
+        spread = [
+            jnp.concatenate(
+                [p for q in range(splits) for p in (r[q * cols : (q + 1) * cols], empty)], axis=0
+            )
+            for r in right
+        ]
+        none = jnp.zeros((half, gap), BF16)
+        wide_left = jnp.concatenate([p for l in left for p in (l, none)], axis=1)
+        none = jnp.zeros((splits * LANES, gap), BF16)
+        wide_right = jnp.concatenate([p for r in spread for p in (r, none)], axis=1)
+        total = dot(wide_left, wide_right, NT)
+        for q in range(splits):
+            products[q, pl.ds(c, half, owned), :] = total[:, q * LANES : q * LANES + cols]
+    for q in range(splits):
+        for r in range(near_rows):
+            pieces = [products[q, pl.ds((r * rows + i) * owned, owned), :] for i in range(rows)]
+            out_ref[q * near_rows + r] = jnp.concatenate(pieces, axis=1).astype(BF16)
+
+
+def swap(block, distance, members):
+    splits, blocks = lax.axis_size("col"), lax.axis_size("row")
+    near_rows = members // splits
+    pairs = []
+    for q in range(splits):
+        for r in range(blocks):
+            source = q * near_rows + r % near_rows
+            to = source ^ distance
+            target = (r // near_rows * near_rows + to % near_rows) * splits + to // near_rows
+            pairs.append((r * splits + q, target))
+    return lax.ppermute(block, ("row", "col"), pairs)
+
+
+def by_halves(pair_act, tile_mask, w_left_gate, w_left, w_right_gate, w_right, w_out_gate, w_out):
+    rows, cols, width = pair_act.shape
+    blocks, splits = lax.axis_size("row"), lax.axis_size("col")
+    halves = 2
+    members = blocks * splits // halves
+    near_rows = blocks // halves
+    channels = w_left.shape[1]
+    owned = channels // members
+    pairs = rows * cols
+    tile = rows * blocks // TILES
+    flat = pair_act.reshape(pairs, width)
+    operands = (flat, tile_mask, w_left_gate, w_left, w_right_gate, w_right, w_out_gate)
+    left, right, gate = call(
+        functools.partial(halves_project_kernel, rows, tile, owned),
+        (
+            pltpu.VMEM((members, owned, pairs), BF16),
+            pltpu.HBM((splits, halves, near_rows, owned, pairs), BF16),
+            pltpu.VMEM((pairs, width), F32),
+        ),
+        operands,
+        scratch=[pltpu.VMEM(a.shape, a.dtype) for a in operands]
+        + [
+            pltpu.VMEM((splits, near_rows, owned, pairs), BF16),
+            pltpu.VMEM((pairs, width), BF16),
+            pltpu.SemaphoreType.DMA((len(operands),)),
+            pltpu.SemaphoreType.DMA((halves,)),
+        ],
+        flops=10 * pairs * width * channels,
+        space=pltpu.HBM,
+    )
+    right = lax.all_to_all(
+        right.reshape(blocks * splits, owned, pairs), ("col", "row"), 0, 0, tiled=True
+    )
+    held = {0: {d: left[d] for d in range(members)}}
+    core, y, z, x = 1, 2, 4, near_rows
+    for n, stage in enumerate(((z,), (x, y, x | y), (core,))):
+        arrived = {}
+        bits = functools.reduce(lambda a, b: a | b, stage)
+        for step in stage:
+            sent = [(s, d) for s in held for d in held[s] if d & bits == step]
+            got = swap(jnp.stack([held[s][d] for s, d in sent]), step, members)
+            for m, (s, d) in enumerate(sent):
+                arrived.setdefault(s | step, {})[d & ~bits] = got[m]
+            if n == 2:
+                last, last_steps = got, [s | step for s, d in sent]
+        kept = {s: {d: b for d, b in held[s].items() if d & bits == 0} for s in held}
+        if n == 2:
+            first_steps = sorted(kept)
+            first = jnp.stack([kept[s][0] for s in first_steps])
+        for s in arrived:
+            kept.setdefault(s, {}).update(arrived[s])
+        held = kept
+    residues = rows * blocks
+    triangle = call(
+        functools.partial(halves_triangle_kernel, rows, cols, members, (first_steps, last_steps)),
+        pltpu.VMEM((members, owned, pairs), BF16),
+        (first, last, right.reshape(splits, blocks, owned, pairs)),
+        scratch=(
+            pltpu.VMEM((splits, near_rows * rows * owned, cols), F32),
+            pltpu.VMEM((splits, residues * owned, cols), F32),
+            pltpu.VMEM((splits, near_rows * rows * owned, cols), F32),
+        ),
+        flops=2 * owned * residues**3,
+    )
+    groups = [
+        [q * blocks + h * near_rows + r for q in range(splits) for r in range(near_rows)]
+        for h in range(halves)
+    ]
+    owned_pairs = lax.all_to_all(
+        triangle, ("col", "row"), 0, 0, tiled=True, axis_index_groups=groups
+    )
+    out = call(
+        output_kernel,
+        jax.ShapeDtypeStruct((pairs, width), BF16),
+        (owned_pairs, gate, w_out),
+        flops=2 * pairs * width * channels,
+    )
+    return out.reshape(rows, cols, width)
+
+
 def by_rows(pair_act, tile_mask, w_left_gate, w_left, w_right_gate, w_right, w_out_gate, w_out):
-    rows, cols, width = pair_act.shape
+    rows, cols, _ = pair_act.shape
     normed = norm_axis(pair_act.astype(F32), 2).astype(BF16)
     pair_mask = mask_of(tile_mask, rows, cols)
 
@@ -222,11 +423,13 @@
 
 def local(pair_act, tile_mask, w_left_gate, *weights):
     devices = lax.axis_size("row") * lax.axis_size("col")
-    rows, cols, width = pair_act.shape
+    rows, cols, _ = pair_act.shape
     channels = w_left_gate.shape[1]
     whole = channels % devices == 0 and 2 * channels // devices % SUBLANES == 0
     aligned = rows * cols % LANES == 0 and cols % SUBLANES == 0 and cols <= LANES
     form = by_channels if whole and aligned else by_rows
+    if whole and aligned and lax.axis_size("row") == 16 and lax.axis_size("col") == 2:
+        form = by_halves
     return form(pair_act, tile_mask, w_left_gate, *weights)
 
 

time: 41.7 us -> 47.8 us (1.15)
  blocking collectives: 37.4 us -> 10.8 us
  waiting for transfers between devices: 0 us -> 18.6 us
  starting transfers between devices: 0 us -> 12.9 us
  Pallas kernels: 3.98 us -> 4.79 us
    all_to_all x2 -> x1, blocking collectives: 37.4 us -> 10.8 us  [by_halves(): lax.all_to_all(triangle, ('col', 'row'), 0, 0, tiled=True, axis_index_gro...]
    ppermute x0 -> x5, waiting for transfers between devices: none -> 18.6 us  [swap(): return lax.ppermute(block, ('row', 'col'), pairs)]
    all_to_all x0 -> x1, starting transfers between devices: none -> 7.33 us  [by_halves(): lax.all_to_all(right.reshape(blocks * splits, owned, pairs), ('col', 'row...]
    ppermute x0 -> x5, starting transfers between devices: none -> 5.59 us  [swap(): return lax.ppermute(block, ('row', 'col'), pairs)]
    pallas_call x3, Pallas kernels: 3.98 us -> 4.79 us  [call(): pl.pallas_call(body, out_shape=out, in_specs=[pl.BlockSpec(memory_space=s...]
  transfers between devices with their start and end apart: 0 -> 6, of which waited for: 0 -> 5; matrix products, arithmetic and copies ran while one was open for 0% -> 0% of each run, Pallas kernels for 0% -> 0%
where the time goes in v6:
time: 47.8 us; the launch traced here: 47.5 us
  waiting for transfers between devices  18.6 us (39%)
  starting transfers between devices  12.9 us (27%)
  blocking collectives  10.8 us (23%)
  Pallas kernels  4.79 us (10%)
    ppermute x5, waiting for transfers between devices, swap(): return lax.ppermute(block, ('row', 'col'), pairs)  18.6 us
    all_to_all x1, blocking collectives, by_halves(): lax.all_to_all(triangle, ('col', 'row'), 0, 0, tiled=True, axis_index_gro...  10.8 us
    all_to_all x1, starting transfers between devices, by_halves(): lax.all_to_all(right.reshape(blocks * splits, owned, pairs), ('col', 'row...  7.33 us
    ppermute x5, starting transfers between devices, swap(): return lax.ppermute(block, ('row', 'col'), pairs)  5.59 us
    pallas_call x3, Pallas kernels, call(): pl.pallas_call(body, out_shape=out, in_specs=[pl.BlockSpec(memory_space=s...  4.79 us
  transfers between devices with their start and end apart: 6, of which 5 were waited for; matrix products, arithmetic and copies ran while one was open for 0% of the time, Pallas kernels for 0%

profile of v6, /device:TPU:0, one launch (start us, length us, event | category | flops | bytes accessed | tf_op | source)
XLA Modules:
  0.0 47.5 jit_solution(11678987874105756193)
XLA Ops:
  0.0 2.6 %shard_map.82 = (bf16[16,8,1152]{2,1,0:T(8,128)(2,1)S(1)}, bf16[2,2,8,8,1152]{4,3,2,1,0:T(8,128)(2,1)}, f32[1152,128]{1,0:T(8,128)S(1)}) custom-call(bf16[1152,128]{1,0:T(8,128)(2,1)} %bitcast.6, s32[12,12]{1,0:T(8,128)} %refs_1_.1, bf16[128,128]{1,0:T(8,128)(2,1)} %refs_2_.1, bf16[128,128]{1,0:T(8,128)(2,1)} %refs_3_.1, bf16[128,128]{1,0:T(8,128)(2,1)} %refs_4_.1, ...), custom_call_target="tpu_custom_call" | custom-call | flops 188743680 | bytes 1887436 | tf_op jit(solution)/shard_map/pallas_call | solution.py:132
  2.6 7.3 %all-to-all-start = ((bf16[32,8,1152]{2,1,0:T(8,128)(2,1)}), bf16[32,8,1152]{2,1,0:T(8,128)(2,1)S(1)}, u32[]{:S(2)}, u32[]{:S(2)}) async-start(bf16[32,8,1152]{2,1,0:T(8,128)(2,1)} %bitcast.5), calls=%async_computation | async-start | bytes 1179648 | tf_op jit(solution)/shard_map/all_to_all | solution.py:343
  10.0 1.8 %collective-permute-start = (bf16[8,8,1152]{2,1,0:T(8,128)(2,1)S(1)}, bf16[8,8,1152]{2,1,0:T(8,128)(2,1)S(1)}, u32[]{:S(2)}, u32[]{:S(2)}) collective-permute-start(bf16[8,8,1152]{2,1,0:T(8,128)(2,1)S(1)} %pad_maximum_fusion), channel_id=1, source_target_pairs={{0,8},{2,10},{4,12},{6,14},{8,0},{10,2},{12,4},{14,6},{16,24},{18,... | collective-permute-start | bytes 442376 | tf_op jit(solution)/shard_map/ppermute | solution.py:310
  11.9 12.3 %collective-permute-done = bf16[8,8,1152]{2,1,0:T(8,128)(2,1)S(1)} collective-permute-done((bf16[8,8,1152]{2,1,0:T(8,128)(2,1)S(1)}, bf16[8,8,1152]{2,1,0:T(8,128)(2,1)S(1)}, u32[]{:S(2)}, u32[]{:S(2)}) %collective-permute-start) | collective-permute-done | bytes 147488 | tf_op jit(solution)/shard_map/ppermute | solution.py:310
  24.2 1.9 %collective-permute-start.1 = (bf16[4,8,1152]{2,1,0:T(8,128)(2,1)S(1)}, bf16[4,8,1152]{2,1,0:T(8,128)(2,1)S(1)}, u32[]{:S(2)}, u32[]{:S(2)}) collective-permute-start(bf16[4,8,1152]{2,1,0:T(8,128)(2,1)S(1)} %pad_maximum_fusion.1), channel_id=1, source_target_pairs={{0,4},{2,6},{4,0},{6,2},{8,12},{10,14},{12,8},{14,10},{16,20},{18,... | collective-permute-start | bytes 221192 | tf_op jit(solution)/shard_map/ppermute | solution.py:310
  26.1 1.5 %collective-permute-start.2 = (bf16[4,8,1152]{2,1,0:T(8,128)(2,1)S(1)}, bf16[4,8,1152]{2,1,0:T(8,128)(2,1)S(1)}, u32[]{:S(2)}, u32[]{:S(2)}) collective-permute-start(bf16[4,8,1152]{2,1,0:T(8,128)(2,1)S(1)} %pad_maximum_fusion.2), channel_id=1, source_target_pairs={{0,1},{2,3},{4,5},{6,7},{8,9},{10,11},{12,13},{14,15},{16,17},{18,... | collective-permute-start | bytes 221192 | tf_op jit(solution)/shard_map/ppermute | solution.py:310
  27.7 0.3 collective-permute-start.3
  27.9 0.8 %collective-permute-done.1 = bf16[4,8,1152]{2,1,0:T(8,128)(2,1)S(1)} collective-permute-done((bf16[4,8,1152]{2,1,0:T(8,128)(2,1)S(1)}, bf16[4,8,1152]{2,1,0:T(8,128)(2,1)S(1)}, u32[]{:S(2)}, u32[]{:S(2)}) %collective-permute-start.1) | collective-permute-done | bytes 73760 | tf_op jit(solution)/shard_map/ppermute | solution.py:310
  28.8 1.8 %collective-permute-done.2 = bf16[4,8,1152]{2,1,0:T(8,128)(2,1)S(1)} collective-permute-done((bf16[4,8,1152]{2,1,0:T(8,128)(2,1)S(1)}, bf16[4,8,1152]{2,1,0:T(8,128)(2,1)S(1)}, u32[]{:S(2)}, u32[]{:S(2)}) %collective-permute-start.2) | collective-permute-done | bytes 73760 | tf_op jit(solution)/shard_map/ppermute | solution.py:310
  30.6 2.4 %collective-permute-done.3 = bf16[4,8,1152]{2,1,0:T(8,128)(2,1)S(1)} collective-permute-done((bf16[4,8,1152]{2,1,0:T(8,128)(2,1)S(1)}, bf16[4,8,1152]{2,1,0:T(8,128)(2,1)S(1)}, u32[]{:S(2)}, u32[]{:S(2)}) %collective-permute-start.3) | collective-permute-done | bytes 73760 | tf_op jit(solution)/shard_map/ppermute | solution.py:310
  33.0 0.1 collective-permute-start.4
  33.1 1.4 %collective-permute-done.4.refs_1_ = bf16[8,8,1152]{2,1,0:T(8,128)(2,1)S(1)} collective-permute-done((bf16[8,8,1152]{2,1,0:T(8,128)(2,1)S(1)}, bf16[8,8,1152]{2,1,0:T(8,128)(2,1)S(1)}, u32[]{:S(2)}, u32[]{:S(2)}) %collective-permute-start.4) | collective-permute-done | bytes 147488 | tf_op jit(solution)/shard_map/ppermute | solution.py:310
  34.4 0.0 all-to-all-done
  34.4 1.1 %shard_map.83 = bf16[16,8,1152]{2,1,0:T(8,128)(2,1)S(1)} custom-call(bf16[8,8,1152]{2,1,0:T(8,128)(2,1)S(1)} %get-tuple-element.24.refs_0_, bf16[8,8,1152]{2,1,0:T(8,128)(2,1)S(1)} %collective-permute-done.4.refs_1_, bf16[2,16,8,1152]{3,2,1,0:T(8,128)(2,1)S(1)} %bitcast.4), custom_call_target="tpu_custom_call" | custom-call | flops 113246208 | bytes 1132462 | tf_op jit(solution)/shard_map/pallas_call | solution.py:132
  35.5 0.0 copy-start
  35.5 10.8 %all_to_all.10.t_ref = bf16[16,8,1152]{2,1,0:T(8,128)(2,1)S(1)} all-to-all(bf16[16,8,1152]{2,1,0:T(8,128)(2,1)S(1)} %shard_map.83), channel_id=1, replica_groups={{0,2,4,6,8,10,12,14,1,3,5,7,9,11,13,15},{16,18,20,22,24,26,28,30,17,19,..., dimensions={0} | all-to-all | bytes 589824 | tf_op jit(solution)/shard_map/all_to_all | solution.py:381
  46.4 0.0 copy-done
  46.4 1.1 %shard_map.84 = bf16[1152,128]{1,0:T(8,128)(2,1)} custom-call(bf16[16,8,1152]{2,1,0:T(8,128)(2,1)S(1)} %all_to_all.10.t_ref, f32[1152,128]{1,0:T(8,128)S(1)} %get-tuple-element.10.gate_ref, bf16[128,128]{1,0:T(8,128)(2,1)S(1)} %copy-done), custom_call_target="tpu_custom_call" | custom-call | flops 37748736 | bytes 377487 | tf_op jit(solution)/shard_map/pallas_call | solution.py:132
  (18 shorter events, 0.2 us)
Async XLA Ops:
  2.6 31.8 %all-to-all-start = ((bf16[32,8,1152]{2,1,0:T(8,128)(2,1)}), bf16[32,8,1152]{2,1,0:T(8,128)(2,1)S(1)}, u32[]{:S(2)}, u32[]{:S(2)}) async-start(bf16[32,8,1152]{2,1,0:T(8,128)(2,1)} %bitcast.5), calls=%async_computation | async-start | bytes 1179648 | tf_op jit(solution)/shard_map/all_to_all | solution.py:343
  10.0 14.2 %collective-permute-start = (bf16[8,8,1152]{2,1,0:T(8,128)(2,1)S(1)}, bf16[8,8,1152]{2,1,0:T(8,128)(2,1)S(1)}, u32[]{:S(2)}, u32[]{:S(2)}) collective-permute-start(bf16[8,8,1152]{2,1,0:T(8,128)(2,1)S(1)} %pad_maximum_fusion), channel_id=1, source_target_pairs={{0,8},{2,10},{4,12},{6,14},{8,0},{10,2},{12,4},{14,6},{16,24},{18,... | collective-permute-start | bytes 442376 | tf_op jit(solution)/shard_map/ppermute | solution.py:310
  24.2 4.6 %collective-permute-start.1 = (bf16[4,8,1152]{2,1,0:T(8,128)(2,1)S(1)}, bf16[4,8,1152]{2,1,0:T(8,128)(2,1)S(1)}, u32[]{:S(2)}, u32[]{:S(2)}) collective-permute-start(bf16[4,8,1152]{2,1,0:T(8,128)(2,1)S(1)} %pad_maximum_fusion.1), channel_id=1, source_target_pairs={{0,4},{2,6},{4,0},{6,2},{8,12},{10,14},{12,8},{14,10},{16,20},{18,... | collective-permute-start | bytes 221192 | tf_op jit(solution)/shard_map/ppermute | solution.py:310
  26.1 4.4 %collective-permute-start.2 = (bf16[4,8,1152]{2,1,0:T(8,128)(2,1)S(1)}, bf16[4,8,1152]{2,1,0:T(8,128)(2,1)S(1)}, u32[]{:S(2)}, u32[]{:S(2)}) collective-permute-start(bf16[4,8,1152]{2,1,0:T(8,128)(2,1)S(1)} %pad_maximum_fusion.2), channel_id=1, source_target_pairs={{0,1},{2,3},{4,5},{6,7},{8,9},{10,11},{12,13},{14,15},{16,17},{18,... | collective-permute-start | bytes 221192 | tf_op jit(solution)/shard_map/ppermute | solution.py:310
  27.7 5.3 %collective-permute-start.3 = (bf16[4,8,1152]{2,1,0:T(8,128)(2,1)S(1)}, bf16[4,8,1152]{2,1,0:T(8,128)(2,1)S(1)}, u32[]{:S(2)}, u32[]{:S(2)}) collective-permute-start(bf16[4,8,1152]{2,1,0:T(8,128)(2,1)S(1)} %pad_maximum_fusion.3), channel_id=1, source_target_pairs={{0,5},{2,7},{4,1},{6,3},{8,13},{10,15},{12,9},{14,11},{16,21},{18,... | collective-permute-start | bytes 221192 | tf_op jit(solution)/shard_map/ppermute | solution.py:310
  33.0 1.4 %collective-permute-start.4 = (bf16[8,8,1152]{2,1,0:T(8,128)(2,1)S(1)}, bf16[8,8,1152]{2,1,0:T(8,128)(2,1)S(1)}, u32[]{:S(2)}, u32[]{:S(2)}) collective-permute-start(bf16[8,8,1152]{2,1,0:T(8,128)(2,1)S(1)} %get-tuple-element.23), channel_id=1, source_target_pairs={{0,2},{2,0},{4,6},{6,4},{8,10},{10,8},{12,14},{14,12},{16,18},{18,... | collective-permute-start | bytes 442376 | tf_op jit(solution)/shard_map/ppermute | solution.py:310
  35.5 10.9 %copy-start = (bf16[128,128]{1,0:T(8,128)(2,1)S(1)}, bf16[128,128]{1,0:T(8,128)(2,1)}, u32[]{:S(2)}) copy-start(bf16[128,128]{1,0:T(8,128)(2,1)} %w_ref.1) | copy-start | bytes 98308

commit v7 on v6

--- a/solution.py
+++ b/solution.py
@@ -194,41 +194,52 @@
     return out.reshape(rows, cols, width)
 
 
-def halves_project_kernel(rows, tile, owned, *refs):
-    far, (left_ref, right_far, gate_ref), near = refs[:7], refs[7:10], refs[10:17]
-    right_ref, normed_ref, sems, right_sems = refs[17:]
+def pick_slots(channels, owned, far_bit, value):
+    members = channels // owned
+    row = lax.broadcasted_iota(jnp.int32, (channels // 2, channels), 0)
+    channel = lax.broadcasted_iota(jnp.int32, (channels // 2, channels), 1)
+    slot = row // owned
+    distance = slot // far_bit * (2 * far_bit) + slot % far_bit + value * far_bit
+    owner = distance ^ member_number(members)
+    return jnp.where(owner * owned + row % owned == channel, 1.0, 0.0).astype(BF16)
+
+
+def factor_maker(pick, gate_w, value_w, mask, target):
+    gates = dot(pick, gate_w[...], NT).astype(BF16)
+    values = dot(pick, value_w[...], NT).astype(BF16)
+
+    def make(normed, start, wide):
+        gate = jax.nn.sigmoid(dot(gates, normed, NT))
+        made = (gate * dot(values, normed, NT)).astype(BF16) * mask[:, start : start + wide]
+        target[..., pl.ds(start, wide)] = made.reshape(*target.shape[:-1], wide)
+
+    return make
+
+
+def strips_of(pairs):
+    return [(start, min(WIDE, pairs - start)) for start in range(0, pairs, WIDE)]
+
+
+def halves_project_kernel(rows, tile, owned, far_bit, *refs):
+    far, (left_ref, right_far, normed_ref), near = refs[:6], refs[6:9], refs[9:15]
+    right_ref, sems, right_sems = refs[15:]
     copies = [pltpu.make_async_copy(a, b, sems.at[n]) for n, (a, b) in enumerate(zip(far, near))]
     for copy in copies:
         copy.start()
-    x_ref, tiles_ref, lg_ref, l_ref, rg_ref, r_ref, og_ref = near
+    x_ref, tiles_ref, lg_ref, l_ref, rg_ref, r_ref = near
     pairs, _ = x_ref.shape
     channels = l_ref.shape[1]
-    members = channels // owned
+    pick_left = pick_slots(channels, owned, far_bit, 1)
     row = lax.broadcasted_iota(jnp.int32, (channels, channels), 0)
     channel = lax.broadcasted_iota(jnp.int32, (channels, channels), 1)
-    owner = (row // owned) ^ member_number(members)
-    pick_left = jnp.where(owner * owned + row % owned == channel, 1.0, 0.0).astype(BF16)
     pick_right = jnp.where(row == channel, 1.0, 0.0).astype(BF16)
     for copy in copies:
         copy.wait()
     mask = lane_mask(pairs // rows, tile, pairs, rows, tiles_ref[...]).astype(BF16)
-    _, halves, _ = right_far.shape[:3]
-
-    def factor(pick, gate_w, value_w, target):
-        gates = dot(pick, gate_w[...], NT).astype(BF16)
-        values = dot(pick, value_w[...], NT).astype(BF16)
-
-        def make(normed, start, wide):
-            gate = jax.nn.sigmoid(dot(gates, normed, NT))
-            made = (gate * dot(values, normed, NT)).astype(BF16) * mask[:, start : start + wide]
-            target[..., pl.ds(start, wide)] = made.reshape(*target.shape[:-1], wide)
-
-        return make
-
-    make_right = factor(pick_right, rg_ref, r_ref, right_ref)
-    make_left = factor(pick_left, lg_ref, l_ref, left_ref)
-    strips = [(start, min(WIDE, pairs - start)) for start in range(0, pairs, WIDE)]
-    for start, wide in strips:
+    halves = right_far.shape[1]
+    make_right = factor_maker(pick_right, rg_ref, r_ref, mask, right_ref)
+    make_left = factor_maker(pick_left, lg_ref, l_ref, mask, left_ref)
+    for start, wide in strips_of(pairs):
         here = pl.ds(start, wide)
         normed = norm_axis(x_ref[here, :].astype(F32), 1).astype(BF16)
         normed_ref[here, :] = normed
@@ -239,30 +250,28 @@
     ]
     for copy in sent:
         copy.start()
-    for start, wide in strips:
-        here = pl.ds(start, wide)
-        normed = normed_ref[here, :]
-        make_left(normed, start, wide)
-        gate_ref[here, :] = jax.nn.sigmoid(dot(normed, og_ref[...]))
+    for start, wide in strips_of(pairs):
+        make_left(normed_ref[pl.ds(start, wide), :], start, wide)
     for copy in sent:
         copy.wait()
 
 
-def member_number(members):
-    near_rows = members // lax.axis_size("col")
-    return lax.axis_index("col") * near_rows + lax.axis_index("row") % near_rows
-
-
-def halves_triangle_kernel(rows, cols, members, steps, *refs):
-    left_refs, (right_ref, out_ref, lefts, rights, products) = refs[: len(steps)], refs[len(steps) :]
-    splits, blocks, owned = right_ref.shape[:3]
+def beside_kernel(rows, tile, owned, far_bit, *refs):
+    normed_ref, tiles_ref, lg_ref, l_ref, og_ref, left_ref, gate_ref = refs
+    pairs = normed_ref.shape[0]
+    pick = pick_slots(l_ref.shape[1], owned, far_bit, 0)
+    mask = lane_mask(pairs // rows, tile, pairs, rows, tiles_ref[...]).astype(BF16)
+    make_left = factor_maker(pick, lg_ref, l_ref, mask, left_ref)
+    for start, wide in strips_of(pairs):
+        normed = normed_ref[pl.ds(start, wide), :]
+        make_left(normed, start, wide)
+        gate_ref[pl.ds(start, wide), :] = jax.nn.sigmoid(dot(normed, og_ref[...]))
+
+
+def layout_kernel(rows, cols, members, splits, steps, *refs):
+    left_refs, (out_ref, lefts) = refs[: len(steps)], refs[len(steps) :]
+    owned, half = out_ref.shape[:2]
     near_rows = members // splits
-    for q in range(splits):
-        for r in range(blocks):
-            flat = right_ref[q, r].astype(F32)
-            for i in range(rows):
-                at = (r * rows + i) * owned
-                rights[q, pl.ds(at, owned), :] = flat[:, i * cols : (i + 1) * cols]
     me = member_number(members)
     for left_ref, distances in zip(left_refs, steps):
         for n, distance in enumerate(distances):
@@ -272,10 +281,29 @@
             for i in range(rows):
                 at = pl.multiple_of((r * rows + i) * owned, owned)
                 lefts[q, pl.ds(at, owned), :] = flat[:, i * cols : (i + 1) * cols]
+    none = jnp.zeros((half, LANES - cols), BF16)
+    for c in range(owned):
+        parts = [lefts[q, pl.ds(c, half, owned), :].astype(BF16) for q in range(splits)]
+        out_ref[c] = jnp.concatenate([p for part in parts for p in (part, none)], axis=1)
+
+
+def member_number(members):
+    near_rows = members // lax.axis_size("col")
+    return lax.axis_index("col") * near_rows + lax.axis_index("row") % near_rows
+
+
+def halves_triangle_kernel(rows, cols, members, left_ref, right_ref, out_ref, rights, products):
+    splits, blocks, owned = right_ref.shape[:3]
+    near_rows = members // splits
+    for q in range(splits):
+        for r in range(blocks):
+            flat = right_ref[q, r].astype(F32)
+            for i in range(rows):
+                at = (r * rows + i) * owned
+                rights[q, pl.ds(at, owned), :] = flat[:, i * cols : (i + 1) * cols]
     residues, half = blocks * rows, near_rows * rows
     gap = LANES - cols
     for c in range(owned):
-        left = [lefts[q, pl.ds(c, half, owned), :].astype(BF16) for q in range(splits)]
         right = [rights[q, pl.ds(c, residues, owned), :].astype(BF16) for q in range(splits)]
         empty = jnp.zeros((gap, cols), BF16)
         spread = [
@@ -284,11 +312,9 @@
             )
             for r in right
         ]
-        none = jnp.zeros((half, gap), BF16)
-        wide_left = jnp.concatenate([p for l in left for p in (l, none)], axis=1)
         none = jnp.zeros((splits * LANES, gap), BF16)
         wide_right = jnp.concatenate([p for r in spread for p in (r, none)], axis=1)
-        total = dot(wide_left, wide_right, NT)
+        total = dot(left_ref[c], wide_right, NT)
         for q in range(splits):
             products[q, pl.ds(c, half, owned), :] = total[:, q * LANES : q * LANES + cols]
     for q in range(splits):
@@ -321,54 +347,66 @@
     pairs = rows * cols
     tile = rows * blocks // TILES
     flat = pair_act.reshape(pairs, width)
-    operands = (flat, tile_mask, w_left_gate, w_left, w_right_gate, w_right, w_out_gate)
-    left, right, gate = call(
-        functools.partial(halves_project_kernel, rows, tile, owned),
+    core, y, z, x = 1, 2, 4, near_rows
+    operands = (flat, tile_mask, w_left_gate, w_left, w_right_gate, w_right)
+    left, right, normed = call(
+        functools.partial(halves_project_kernel, rows, tile, owned, z),
         (
-            pltpu.VMEM((members, owned, pairs), BF16),
+            pltpu.VMEM((members // 2, owned, pairs), BF16),
             pltpu.HBM((splits, halves, near_rows, owned, pairs), BF16),
-            pltpu.VMEM((pairs, width), F32),
+            pltpu.VMEM((pairs, width), BF16),
         ),
         operands,
         scratch=[pltpu.VMEM(a.shape, a.dtype) for a in operands]
         + [
             pltpu.VMEM((splits, near_rows, owned, pairs), BF16),
-            pltpu.VMEM((pairs, width), BF16),
             pltpu.SemaphoreType.DMA((len(operands),)),
             pltpu.SemaphoreType.DMA((halves,)),
         ],
-        flops=10 * pairs * width * channels,
+        flops=8 * pairs * width * channels,
         space=pltpu.HBM,
     )
     right = lax.all_to_all(
         right.reshape(blocks * splits, owned, pairs), ("col", "row"), 0, 0, tiled=True
     )
-    held = {0: {d: left[d] for d in range(members)}}
-    core, y, z, x = 1, 2, 4, near_rows
-    for n, stage in enumerate(((z,), (x, y, x | y), (core,))):
-        arrived = {}
+    got = swap(left, z, members)
+    stayed, gate = call(
+        functools.partial(beside_kernel, rows, tile, owned, z),
+        (
+            pltpu.VMEM((members // 2, owned, pairs), BF16),
+            pltpu.VMEM((pairs, width), F32),
+        ),
+        (normed, tile_mask, w_left_gate, w_left, w_out_gate),
+        flops=6 * pairs * width * channels,
+    )
+    near = [d for d in range(members) if not d & z]
+    held = {0: dict(zip(near, stayed)), z: dict(zip(near, got))}
+    for stage in ((x, y, x | y), (core,)):
+        arrived, kept = {}, {}
         bits = functools.reduce(lambda a, b: a | b, stage)
         for step in stage:
             sent = [(s, d) for s in held for d in held[s] if d & bits == step]
             got = swap(jnp.stack([held[s][d] for s, d in sent]), step, members)
+            last_steps = [s | step for s, d in sent]
             for m, (s, d) in enumerate(sent):
                 arrived.setdefault(s | step, {})[d & ~bits] = got[m]
-            if n == 2:
-                last, last_steps = got, [s | step for s, d in sent]
-        kept = {s: {d: b for d, b in held[s].items() if d & bits == 0} for s in held}
-        if n == 2:
-            first_steps = sorted(kept)
-            first = jnp.stack([kept[s][0] for s in first_steps])
-        for s in arrived:
-            kept.setdefault(s, {}).update(arrived[s])
-        held = kept
+        for s in held:
+            kept[s] = {d: b for d, b in held[s].items() if d & bits == 0}
+        first_steps, first = sorted(kept), [kept[s][0] for s in sorted(kept)]
+        held = {**kept, **arrived}
+    left = call(
+        functools.partial(layout_kernel, rows, cols, members, splits, (first_steps, last_steps)),
+        pltpu.VMEM((owned, near_rows * rows, splits * LANES), BF16),
+        (jnp.stack(first), got),
+        scratch=[pltpu.VMEM((splits, near_rows * rows * owned, cols), F32)],
+        flops=pairs * channels * 10,
+    )
     residues = rows * blocks
     triangle = call(
-        functools.partial(halves_triangle_kernel, rows, cols, members, (first_steps, last_steps)),
+        functools.partial(halves_triangle_kernel, rows, cols, members),
         pltpu.VMEM((members, owned, pairs), BF16),
-        (first, last, right.reshape(splits, blocks, owned, pairs)),
+        (left, right.reshape(splits, blocks, owned, pairs)),
         scratch=(
-            pltpu.VMEM((splits, near_rows * rows * owned, cols), F32),
             pltpu.VMEM((splits, residues * owned, cols), F32),
             pltpu.VMEM((splits, near_rows * rows * owned, cols), F32),
         ),

time: 47.8 us -> 48.1 us (level)
  Pallas kernels: 4.79 us -> 5.51 us
    pallas_call x3 -> x5, Pallas kernels: 4.79 us -> 5.51 us  [call(): pl.pallas_call(body, out_shape=out, in_specs=[pl.BlockSpec(memory_space=s...]
  transfers between devices with their start and end apart: 6 -> 6, of which waited for: 5 -> 5; matrix products, arithmetic and copies ran while one was open for 0% -> 0% of each run, Pallas kernels for 0% -> 2%
where the time goes in v7:
time: 48.1 us; the launch traced here: 47.8 us
  waiting for transfers between devices  18.2 us (38%)
  starting transfers between devices  12.9 us (27%)
  blocking collectives  10.8 us (22%)
  Pallas kernels  5.51 us (11%)
    ppermute x5, waiting for transfers between devices, swap(): return lax.ppermute(block, ('row', 'col'), pairs)  18.2 us
    all_to_all x1, blocking collectives, by_halves(): lax.all_to_all(triangle, ('col', 'row'), 0, 0, tiled=True, axis_index_gro...  10.8 us
    all_to_all x1, starting transfers between devices, by_halves(): lax.all_to_all(right.reshape(blocks * splits, owned, pairs), ('col', 'row...  7.33 us
    ppermute x5, starting transfers between devices, swap(): return lax.ppermute(block, ('row', 'col'), pairs)  5.59 us
    pallas_call x5, Pallas kernels, call(): pl.pallas_call(body, out_shape=out, in_specs=[pl.BlockSpec(memory_space=s...  5.51 us
  transfers between devices with their start and end apart: 6, of which 5 were waited for; matrix products, arithmetic and copies ran while one was open for 0% of the time, Pallas kernels for 2%

profile of v7, /device:TPU:0, one launch (start us, length us, event | category | flops | bytes accessed | tf_op | source)
XLA Modules:
  0.0 47.8 jit_solution(17775603777733936695)
XLA Ops:
  0.0 2.7 %shard_map.82 = (bf16[8,8,1152]{2,1,0:T(8,128)(2,1)S(1)}, bf16[2,2,8,8,1152]{4,3,2,1,0:T(8,128)(2,1)}, bf16[1152,128]{1,0:T(8,128)(2,1)S(1)}) custom-call(bf16[1152,128]{1,0:T(8,128)(2,1)} %bitcast.6, s32[12,12]{1,0:T(8,128)} %refs_1_.3, bf16[128,128]{1,0:T(8,128)(2,1)} %refs_2_.3, bf16[128,128]{1,0:T(8,128)(2,1)} %refs_3_.3, bf16[128,128]{1,0:T(8,128)(2,1)} %refs_4_.2, ...), custom_call_target="tpu_custom_call" | custom-call | flops 150994944 | bytes 1509949 | tf_op jit(solution)/shard_map/pallas_call | solution.py:132
  2.7 0.0 copy-start.1
  2.7 0.0 copy-start.2
  2.7 0.0 copy-start.3
  2.7 0.0 copy-start.4
  2.7 7.3 %all-to-all-start = ((bf16[32,8,1152]{2,1,0:T(8,128)(2,1)}), bf16[32,8,1152]{2,1,0:T(8,128)(2,1)S(1)}, u32[]{:S(2)}, u32[]{:S(2)}) async-start(bf16[32,8,1152]{2,1,0:T(8,128)(2,1)} %bitcast.5), calls=%async_computation | async-start | bytes 1179648 | tf_op jit(solution)/shard_map/all_to_all | solution.py:369
  10.1 1.8 %collective-permute-start = (bf16[8,8,1152]{2,1,0:T(8,128)(2,1)S(1)}, bf16[8,8,1152]{2,1,0:T(8,128)(2,1)S(1)}, u32[]{:S(2)}, u32[]{:S(2)}) collective-permute-start(bf16[8,8,1152]{2,1,0:T(8,128)(2,1)S(1)} %get-tuple-element.12), channel_id=1, source_target_pairs={{0,8},{2,10},{4,12},{6,14},{8,0},{10,2},{12,4},{14,6},{16,24},{18,... | collective-permute-start | bytes 442376 | tf_op jit(solution)/shard_map/ppermute | solution.py:336
  11.9 0.0 copy-done.1
  11.9 0.0 copy-done.2
  11.9 0.0 copy-done.3
  11.9 0.0 copy-done.4
  11.9 0.5 %shard_map.83 = (bf16[8,8,1152]{2,1,0:T(8,128)(2,1)S(1)}, f32[1152,128]{1,0:T(8,128)S(1)}) custom-call(bf16[1152,128]{1,0:T(8,128)(2,1)S(1)} %get-tuple-element.10.refs_0_, s32[12,12]{1,0:T(8,128)S(1)} %copy-done.4, bf16[128,128]{1,0:T(8,128)(2,1)S(1)} %copy-done.1, bf16[128,128]{1,0:T(8,128)(2,1)S(1)} %copy-done.2, bf16[128,128]{1,0:T(8,128)(2,1)S(1)} %copy-done.3), custom_call_target="tpu_custom_call" | custom-call | flops 113246208 | bytes 1132462 | tf_op jit(solution)/shard_map/pallas_call | solution.py:132
  12.4 11.8 %collective-permute-done = bf16[8,8,1152]{2,1,0:T(8,128)(2,1)S(1)} collective-permute-done((bf16[8,8,1152]{2,1,0:T(8,128)(2,1)S(1)}, bf16[8,8,1152]{2,1,0:T(8,128)(2,1)S(1)}, u32[]{:S(2)}, u32[]{:S(2)}) %collective-permute-start) | collective-permute-done | bytes 147488 | tf_op jit(solution)/shard_map/ppermute | solution.py:336
  24.3 1.9 %collective-permute-start.1 = (bf16[4,8,1152]{2,1,0:T(8,128)(2,1)S(1)}, bf16[4,8,1152]{2,1,0:T(8,128)(2,1)S(1)}, u32[]{:S(2)}, u32[]{:S(2)}) collective-permute-start(bf16[4,8,1152]{2,1,0:T(8,128)(2,1)S(1)} %pad_maximum_fusion), channel_id=1, source_target_pairs={{0,4},{2,6},{4,0},{6,2},{8,12},{10,14},{12,8},{14,10},{16,20},{18,... | collective-permute-start | bytes 221192 | tf_op jit(solution)/shard_map/ppermute | solution.py:336
  26.2 1.5 %collective-permute-start.2 = (bf16[4,8,1152]{2,1,0:T(8,128)(2,1)S(1)}, bf16[4,8,1152]{2,1,0:T(8,128)(2,1)S(1)}, u32[]{:S(2)}, u32[]{:S(2)}) collective-permute-start(bf16[4,8,1152]{2,1,0:T(8,128)(2,1)S(1)} %pad_maximum_fusion.1), channel_id=1, source_target_pairs={{0,1},{2,3},{4,5},{6,7},{8,9},{10,11},{12,13},{14,15},{16,17},{18,... | collective-permute-start | bytes 221192 | tf_op jit(solution)/shard_map/ppermute | solution.py:336
  27.7 0.3 collective-permute-start.3
  28.0 0.8 %collective-permute-done.1 = bf16[4,8,1152]{2,1,0:T(8,128)(2,1)S(1)} collective-permute-done((bf16[4,8,1152]{2,1,0:T(8,128)(2,1)S(1)}, bf16[4,8,1152]{2,1,0:T(8,128)(2,1)S(1)}, u32[]{:S(2)}, u32[]{:S(2)}) %collective-permute-start.1) | collective-permute-done | bytes 73760 | tf_op jit(solution)/shard_map/ppermute | solution.py:336
  28.9 1.8 %collective-permute-done.2 = bf16[4,8,1152]{2,1,0:T(8,128)(2,1)S(1)} collective-permute-done((bf16[4,8,1152]{2,1,0:T(8,128)(2,1)S(1)}, bf16[4,8,1152]{2,1,0:T(8,128)(2,1)S(1)}, u32[]{:S(2)}, u32[]{:S(2)}) %collective-permute-start.2) | collective-permute-done | bytes 73760 | tf_op jit(solution)/shard_map/ppermute | solution.py:336
  30.7 2.4 %collective-permute-done.3 = bf16[4,8,1152]{2,1,0:T(8,128)(2,1)S(1)} collective-permute-done((bf16[4,8,1152]{2,1,0:T(8,128)(2,1)S(1)}, bf16[4,8,1152]{2,1,0:T(8,128)(2,1)S(1)}, u32[]{:S(2)}, u32[]{:S(2)}) %collective-permute-start.3) | collective-permute-done | bytes 73760 | tf_op jit(solution)/shard_map/ppermute | solution.py:336
  33.1 0.1 collective-permute-start.4
  33.2 1.4 %collective-permute-done.4.refs_1_ = bf16[8,8,1152]{2,1,0:T(8,128)(2,1)S(1)} collective-permute-done((bf16[8,8,1152]{2,1,0:T(8,128)(2,1)S(1)}, bf16[8,8,1152]{2,1,0:T(8,128)(2,1)S(1)}, u32[]{:S(2)}, u32[]{:S(2)}) %collective-permute-start.4) | collective-permute-done | bytes 147488 | tf_op jit(solution)/shard_map/ppermute | solution.py:336
  34.5 0.4 shard_map.84.left_ref
  34.9 0.0 all-to-all-done
  34.9 0.9 %shard_map.85 = bf16[16,8,1152]{2,1,0:T(8,128)(2,1)S(1)} custom-call(bf16[8,96,256]{2,1,0:T(8,128)(2,1)S(1)} %shard_map.84.left_ref, bf16[2,16,8,1152]{3,2,1,0:T(8,128)(2,1)S(1)} %bitcast.4), custom_call_target="tpu_custom_call" | custom-call | flops 113246208 | bytes 1132462 | tf_op jit(solution)/shard_map/pallas_call | solution.py:132
  35.8 0.0 copy-start
  35.8 10.8 %all_to_all.10.t_ref = bf16[16,8,1152]{2,1,0:T(8,128)(2,1)S(1)} all-to-all(bf16[16,8,1152]{2,1,0:T(8,128)(2,1)S(1)} %shard_map.85), channel_id=1, replica_groups={{0,2,4,6,8,10,12,14,1,3,5,7,9,11,13,15},{16,18,20,22,24,26,28,30,17,19,..., dimensions={0} | all-to-all | bytes 589824 | tf_op jit(solution)/shard_map/all_to_all | solution.py:419
  46.7 0.0 copy-done
  46.7 1.1 %shard_map.86 = bf16[1152,128]{1,0:T(8,128)(2,1)} custom-call(bf16[16,8,1152]{2,1,0:T(8,128)(2,1)S(1)} %all_to_all.10.t_ref, f32[1152,128]{1,0:T(8,128)S(1)} %get-tuple-element.14.gate_ref, bf16[128,128]{1,0:T(8,128)(2,1)S(1)} %copy-done), custom_call_target="tpu_custom_call" | custom-call | flops 37748736 | bytes 377487 | tf_op jit(solution)/shard_map/pallas_call | solution.py:132
  (16 shorter events, 0.2 us)
Async XLA Ops:
  2.7 9.2 %copy-start.1 = (bf16[128,128]{1,0:T(8,128)(2,1)S(1)}, bf16[128,128]{1,0:T(8,128)(2,1)}, u32[]{:S(2)}) copy-start(bf16[128,128]{1,0:T(8,128)(2,1)} %refs_2_.3) | copy-start | bytes 98308
  2.7 9.2 %copy-start.2 = (bf16[128,128]{1,0:T(8,128)(2,1)S(1)}, bf16[128,128]{1,0:T(8,128)(2,1)}, u32[]{:S(2)}) copy-start(bf16[128,128]{1,0:T(8,128)(2,1)} %refs_3_.3) | copy-start | bytes 98308
  2.7 9.2 %copy-start.3 = (bf16[128,128]{1,0:T(8,128)(2,1)S(1)}, bf16[128,128]{1,0:T(8,128)(2,1)}, u32[]{:S(2)}) copy-start(bf16[128,128]{1,0:T(8,128)(2,1)} %refs_4_.3) | copy-start | bytes 98308
  2.7 9.2 %copy-start.4 = (s32[12,12]{1,0:T(8,128)S(1)}, s32[12,12]{1,0:T(8,128)}, u32[]{:S(2)}) copy-start(s32[12,12]{1,0:T(8,128)} %refs_1_.3) | copy-start | bytes 1732
  2.7 32.2 %all-to-all-start = ((bf16[32,8,1152]{2,1,0:T(8,128)(2,1)}), bf16[32,8,1152]{2,1,0:T(8,128)(2,1)S(1)}, u32[]{:S(2)}, u32[]{:S(2)}) async-start(bf16[32,8,1152]{2,1,0:T(8,128)(2,1)} %bitcast.5), calls=%async_computation | async-start | bytes 1179648 | tf_op jit(solution)/shard_map/all_to_all | solution.py:369
  10.1 14.2 %collective-permute-start = (bf16[8,8,1152]{2,1,0:T(8,128)(2,1)S(1)}, bf16[8,8,1152]{2,1,0:T(8,128)(2,1)S(1)}, u32[]{:S(2)}, u32[]{:S(2)}) collective-permute-start(bf16[8,8,1152]{2,1,0:T(8,128)(2,1)S(1)} %get-tuple-element.12), channel_id=1, source_target_pairs={{0,8},{2,10},{4,12},{6,14},{8,0},{10,2},{12,4},{14,6},{16,24},{18,... | collective-permute-start | bytes 442376 | tf_op jit(solution)/shard_map/ppermute | solution.py:336
  24.3 4.6 %collective-permute-start.1 = (bf16[4,8,1152]{2,1,0:T(8,128)(2,1)S(1)}, bf16[4,8,1152]{2,1,0:T(8,128)(2,1)S(1)}, u32[]{:S(2)}, u32[]{:S(2)}) collective-permute-start(bf16[4,8,1152]{2,1,0:T(8,128)(2,1)S(1)} %pad_maximum_fusion), channel_id=1, source_target_pairs={{0,4},{2,6},{4,0},{6,2},{8,12},{10,14},{12,8},{14,10},{16,20},{18,... | collective-permute-start | bytes 221192 | tf_op jit(solution)/shard_map/ppermute | solution.py:336
  26.2 4.4 %collective-permute-start.2 = (bf16[4,8,1152]{2,1,0:T(8,128)(2,1)S(1)}, bf16[4,8,1152]{2,1,0:T(8,128)(2,1)S(1)}, u32[]{:S(2)}, u32[]{:S(2)}) collective-permute-start(bf16[4,8,1152]{2,1,0:T(8,128)(2,1)S(1)} %pad_maximum_fusion.1), channel_id=1, source_target_pairs={{0,1},{2,3},{4,5},{6,7},{8,9},{10,11},{12,13},{14,15},{16,17},{18,... | collective-permute-start | bytes 221192 | tf_op jit(solution)/shard_map/ppermute | solution.py:336
  27.7 5.3 %collective-permute-start.3 = (bf16[4,8,1152]{2,1,0:T(8,128)(2,1)S(1)}, bf16[4,8,1152]{2,1,0:T(8,128)(2,1)S(1)}, u32[]{:S(2)}, u32[]{:S(2)}) collective-permute-start(bf16[4,8,1152]{2,1,0:T(8,128)(2,1)S(1)} %pad_maximum_fusion.2), channel_id=1, source_target_pairs={{0,5},{2,7},{4,1},{6,3},{8,13},{10,15},{12,9},{14,11},{16,21},{18,... | collective-permute-start | bytes 221192 | tf_op jit(solution)/shard_map/ppermute | solution.py:336
  33.1 1.4 %collective-permute-start.4 = (bf16[8,8,1152]{2,1,0:T(8,128)(2,1)S(1)}, bf16[8,8,1152]{2,1,0:T(8,128)(2,1)S(1)}, u32[]{:S(2)}, u32[]{:S(2)}) collective-permute-start(bf16[8,8,1152]{2,1,0:T(8,128)(2,1)S(1)} %get-tuple-element.25), channel_id=1, source_target_pairs={{0,2},{2,0},{4,6},{6,4},{8,10},{10,8},{12,14},{14,12},{16,18},{18,... | collective-permute-start | bytes 442376 | tf_op jit(solution)/shard_map/ppermute | solution.py:336
  35.8 10.9 %copy-start = (bf16[128,128]{1,0:T(8,128)(2,1)S(1)}, bf16[128,128]{1,0:T(8,128)(2,1)}, u32[]{:S(2)}) copy-start(bf16[128,128]{1,0:T(8,128)(2,1)} %w_ref.1) | copy-start | bytes 98308

commit v8 on v7

--- a/solution.py
+++ b/solution.py
@@ -32,9 +32,56 @@
     return lax.dot_general(a, b, dims, preferred_element_type=F32)
 
 
+def gather_strip(ref, start, wide, cols):
+    gap = LANES - cols
+    tail = ref.shape[0] // LANES * cols
+    parts = []
+    for group in range(start // LANES, (start + wide) // LANES):
+        parts.append(ref[pl.ds(group * cols, cols), :])
+        parts.append(ref[pl.ds(tail + group * gap, gap), :])
+    return jnp.concatenate(parts, axis=0)
+
+
+def scatter_strip(ref, start, wide, cols, values):
+    gap = LANES - cols
+    tail = ref.shape[0] // LANES * cols
+    for n, group in enumerate(range(start // LANES, (start + wide) // LANES)):
+        at = n * LANES
+        ref[pl.ds(group * cols, cols), :] = values[at : at + cols]
+        ref[pl.ds(tail + group * gap, gap), :] = values[at + cols : at + LANES]
+
+
+def rows_of(flat, rows, cols):
+    groups = flat.shape[1] // LANES
+    gap = LANES - cols
+    pieces = [flat[:, g * LANES : g * LANES + cols] for g in range(groups)]
+    ends = [flat[:, g * LANES + cols : (g + 1) * LANES] for g in range(groups)]
+    each = cols // gap
+    for n in range(rows - groups):
+        pieces.append(jnp.concatenate(ends[n * each : (n + 1) * each], axis=1))
+    return pieces
+
+
+def flat_of(pieces, cols):
+    gap = LANES - cols
+    each = cols // gap
+    groups = len(pieces) * cols // LANES
+    parts = []
+    for g in range(groups):
+        end = pieces[groups + g // each]
+        parts += [pieces[g], end[:, g % each * gap : (g % each + 1) * gap]]
+    return jnp.concatenate(parts, axis=1)
+
+
 def lane_mask(cols, tile, pairs, rows, tiles):
     kinds = tiles.shape[0]
-    place = lax.broadcasted_iota(jnp.int32, (kinds, pairs), 1).astype(F32) + 0.5
+    lane = lax.broadcasted_iota(jnp.int32, (kinds, pairs), 1)
+    gap = LANES - cols
+    tail = pairs // LANES * cols - cols
+    within = lane % LANES
+    group = lane // LANES
+    flat = jnp.where(within < cols, group * cols + within, tail + group * gap + within)
+    place = flat.astype(F32) + 0.5
     kind = lax.broadcasted_iota(jnp.int32, (kinds, pairs), 0).astype(F32)
     row = jnp.floor(place * (1.0 / cols))
     col = place - row * cols
@@ -47,81 +94,16 @@
     return jnp.sum(row_hot * dot(tiles.astype(F32).astype(BF16), col_hot), axis=0, keepdims=True)
 
 
-def project_kernel(rows, tile, owned, *refs):
-    far, (out_ref, gate_ref), near, sems = refs[:7], refs[7:9], refs[9:16], refs[16]
-    copies = [pltpu.make_async_copy(a, b, sems.at[n]) for n, (a, b) in enumerate(zip(far, near))]
-    for copy in copies:
-        copy.start()
-    x_ref, tiles_ref, lg_ref, l_ref, rg_ref, r_ref, og_ref = near
-    pairs, _ = x_ref.shape
-    channels = l_ref.shape[1]
-    row = lax.broadcasted_iota(jnp.int32, (2 * channels, channels), 0)
-    channel = lax.broadcasted_iota(jnp.int32, (2 * channels, channels), 1)
-    within = row % (2 * owned)
-    source = row // (2 * owned) * owned + within % owned
-    hit = source == channel
-    pick_left = jnp.where(hit & (within < owned), 1.0, 0.0).astype(BF16)
-    pick_right = jnp.where(hit & (within >= owned), 1.0, 0.0).astype(BF16)
-    for copy in copies:
-        copy.wait()
-    gates = (dot(pick_left, lg_ref[...], NT) + dot(pick_right, rg_ref[...], NT)).astype(BF16)
-    values = (dot(pick_left, l_ref[...], NT) + dot(pick_right, r_ref[...], NT)).astype(BF16)
-    mask = lane_mask(pairs // rows, tile, pairs, rows, tiles_ref[...]).astype(BF16)
-    for start in range(0, pairs, WIDE):
-        wide = min(WIDE, pairs - start)
-        here = pl.ds(start, wide)
-        normed = norm_axis(x_ref[here, :].astype(F32), 1).astype(BF16)
-        gate = jax.nn.sigmoid(dot(gates, normed, NT))
-        value = dot(values, normed, NT)
-        made = (gate * value).astype(BF16) * mask[:, start : start + wide]
-        out_ref[:, :, here] = made.reshape(out_ref.shape[0], 2 * owned, wide)
-        gate_ref[here, :] = jax.nn.sigmoid(dot(normed, og_ref[...]))
-
-
-def triangle_kernel(rows, cols, owned, in_ref, out_ref, factors, products):
-    splits, blocks = in_ref.shape[0], in_ref.shape[1]
-    group = 2 * owned
-    for q in range(splits):
-        for r in range(blocks):
-            flat = in_ref[q, r].astype(F32)
-            for i in range(rows):
-                at = (r * rows + i) * group
-                factors[q, pl.ds(at, group), :] = flat[:, i * cols : (i + 1) * cols]
-    residues = blocks * rows
-    gap = LANES - cols
-    for c in range(owned):
-        left = [factors[q, pl.ds(c, residues, group), :].astype(BF16) for q in range(splits)]
-        right = [factors[q, pl.ds(owned + c, residues, group), :].astype(BF16) for q in range(splits)]
-        empty = jnp.zeros((gap, cols), BF16)
-        spread = [
-            jnp.concatenate(
-                [p for q in range(splits) for p in (r[q * cols : (q + 1) * cols], empty)], axis=0
-            )
-            for r in right
-        ]
-        none = jnp.zeros((residues, gap), BF16)
-        lefts = jnp.concatenate([p for l in left for p in (l, none)], axis=1)
-        none = jnp.zeros((splits * LANES, gap), BF16)
-        rights = jnp.concatenate([p for r in spread for p in (r, none)], axis=1)
-        total = dot(lefts, rights, NT)
-        for q in range(splits):
-            products[q, pl.ds(c, residues, owned), :] = total[:, q * LANES : q * LANES + cols]
-    for q in range(splits):
-        for r in range(blocks):
-            pieces = [products[q, pl.ds((r * rows + i) * owned, owned), :] for i in range(rows)]
-            out_ref[q, r] = jnp.concatenate(pieces, axis=1).astype(BF16)
-
-
-def output_kernel(t_ref, gate_ref, w_ref, out_ref):
+def output_kernel(cols, places, t_ref, gate_ref, w_ref, out_ref):
     pairs = gate_ref.shape[0]
-    channels = w_ref.shape[0]
     for start in range(0, pairs, OWIDE):
         wide = min(OWIDE, pairs - start)
-        triangle = t_ref[:, :, pl.ds(start, wide)].reshape(channels, wide).astype(F32)
+        here = pl.ds(start, wide)
+        triangle = jnp.concatenate([t_ref[p, :, here].astype(F32) for p in places], axis=0)
         scaled = norm_axis(triangle, 0).astype(BF16)
         projected = dot(scaled, w_ref[...], TN)
         here = pl.ds(start, wide)
-        out_ref[here, :] = (gate_ref[here, :] * projected).astype(BF16)
+        scatter_strip(out_ref, start, wide, cols, (gate_ref[here, :] * projected).astype(BF16))
 
 
 def space_of(out):
@@ -149,49 +131,6 @@
     col_hot = (col_ids[:, None] == tile_range[None, :]).astype(F32)
     some = dot(row_hot, tile_mask.astype(F32))
     return dot(some, col_hot.T)
-
-
-def by_channels(pair_act, tile_mask, w_left_gate, w_left, w_right_gate, w_right, w_out_gate, w_out):
-    rows, cols, width = pair_act.shape
-    blocks, splits = lax.axis_size("row"), lax.axis_size("col")
-    devices = blocks * splits
-    channels = w_left.shape[1]
-    owned = channels // devices
-    pairs = rows * cols
-    tile = rows * blocks // TILES
-    flat = pair_act.reshape(pairs, width)
-    operands = (flat, tile_mask, w_left_gate, w_left, w_right_gate, w_right, w_out_gate)
-    factors, gate = call(
-        functools.partial(project_kernel, rows, tile, owned),
-        (pltpu.VMEM((devices, 2 * owned, pairs), BF16), pltpu.VMEM((pairs, width), F32)),
-        operands,
-        scratch=[pltpu.VMEM(a.shape, a.dtype) for a in operands]
-        + [pltpu.SemaphoreType.DMA((len(operands),))],
-        flops=10 * pairs * width * channels,
-        space=pltpu.HBM,
-    )
-    factors = lax.all_to_all(factors, ("col", "row"), 0, 0, tiled=True)
-    residues = rows * blocks
-    triangle = call(
-        functools.partial(triangle_kernel, rows, cols, owned),
-        pltpu.VMEM((splits, blocks, owned, pairs), BF16),
-        (factors.reshape(splits, blocks, 2 * owned, pairs),),
-        scratch=(
-            pltpu.VMEM((splits, residues * 2 * owned, cols), F32),
-            pltpu.VMEM((splits, residues * owned, cols), F32),
-        ),
-        flops=2 * owned * residues**3,
-    )
-    owned_pairs = lax.all_to_all(
-        triangle.reshape(devices, owned, pairs), ("col", "row"), 0, 0, tiled=True
-    )
-    out = call(
-        output_kernel,
-        jax.ShapeDtypeStruct((pairs, width), BF16),
-        (owned_pairs, gate, w_out),
-        flops=2 * pairs * width * channels,
-    )
-    return out.reshape(rows, cols, width)
 
 
 def pick_slots(channels, owned, far_bit, value):
@@ -241,11 +180,14 @@
     make_left = factor_maker(pick_left, lg_ref, l_ref, mask, left_ref)
     for start, wide in strips_of(pairs):
         here = pl.ds(start, wide)
-        normed = norm_axis(x_ref[here, :].astype(F32), 1).astype(BF16)
+        strip = gather_strip(x_ref, start, wide, pairs // rows)
+        normed = norm_axis(strip.astype(F32), 1).astype(BF16)
         normed_ref[here, :] = normed
         make_right(normed, start, wide)
+    splits = right_far.shape[0]
     sent = [
-        pltpu.make_async_copy(right_ref, right_far.at[:, half], right_sems.at[half])
+        pltpu.make_async_copy(right_ref.at[q], right_far.at[q, half], right_sems.at[q, half])
+        for q in range(splits)
         for half in range(halves)
     ]
     for copy in sent:
@@ -277,10 +219,9 @@
         for n, distance in enumerate(distances):
             source = me ^ distance
             q, r = source // near_rows, source % near_rows
-            flat = left_ref[n].astype(F32)
-            for i in range(rows):
+            for i, piece in enumerate(rows_of(left_ref[n].astype(F32), rows, cols)):
                 at = pl.multiple_of((r * rows + i) * owned, owned)
-                lefts[q, pl.ds(at, owned), :] = flat[:, i * cols : (i + 1) * cols]
+                lefts[q, pl.ds(at, owned), :] = piece
     none = jnp.zeros((half, LANES - cols), BF16)
     for c in range(owned):
         parts = [lefts[q, pl.ds(c, half, owned), :].astype(BF16) for q in range(splits)]
@@ -297,10 +238,8 @@
     near_rows = members // splits
     for q in range(splits):
         for r in range(blocks):
-            flat = right_ref[q, r].astype(F32)
-            for i in range(rows):
-                at = (r * rows + i) * owned
-                rights[q, pl.ds(at, owned), :] = flat[:, i * cols : (i + 1) * cols]
+            for i, piece in enumerate(rows_of(right_ref[q, r].astype(F32), rows, cols)):
+                rights[q, pl.ds((r * rows + i) * owned, owned), :] = piece
     residues, half = blocks * rows, near_rows * rows
     gap = LANES - cols
     for c in range(owned):
@@ -320,7 +259,13 @@
     for q in range(splits):
         for r in range(near_rows):
             pieces = [products[q, pl.ds((r * rows + i) * owned, owned), :] for i in range(rows)]
-            out_ref[q * near_rows + r] = jnp.concatenate(pieces, axis=1).astype(BF16)
+            out_ref[place_of(q * near_rows + r, near_rows)] = flat_of(pieces, cols).astype(BF16)
+
+
+def place_of(member, near_rows):
+    far_bit = near_rows // 2
+    row = member % near_rows
+    return member - row + row % far_bit * 2 + row // far_bit
 
 
 def swap(block, distance, members):
@@ -361,7 +306,7 @@
         + [
             pltpu.VMEM((splits, near_rows, owned, pairs), BF16),
             pltpu.SemaphoreType.DMA((len(operands),)),
-            pltpu.SemaphoreType.DMA((halves,)),
+            pltpu.SemaphoreType.DMA((splits, halves)),
         ],
         flops=8 * pairs * width * channels,
         space=pltpu.HBM,
@@ -412,15 +357,16 @@
         ),
         flops=2 * owned * residues**3,
     )
+    order = sorted(range(members), key=lambda m: place_of(m, near_rows))
     groups = [
-        [q * blocks + h * near_rows + r for q in range(splits) for r in range(near_rows)]
+        [m // near_rows * blocks + h * near_rows + m % near_rows for m in order]
         for h in range(halves)
     ]
     owned_pairs = lax.all_to_all(
         triangle, ("col", "row"), 0, 0, tiled=True, axis_index_groups=groups
     )
     out = call(
-        output_kernel,
+        functools.partial(output_kernel, cols, [place_of(m, near_rows) for m in range(members)]),
         jax.ShapeDtypeStruct((pairs, width), BF16),
         (owned_pairs, gate, w_out),
         flops=2 * pairs * width * channels,
@@ -460,14 +406,13 @@
 
 
 def local(pair_act, tile_mask, w_left_gate, *weights):
-    devices = lax.axis_size("row") * lax.axis_size("col")
+    blocks, splits = lax.axis_size("row"), lax.axis_size("col")
     rows, cols, _ = pair_act.shape
     channels = w_left_gate.shape[1]
-    whole = channels % devices == 0 and 2 * channels // devices % SUBLANES == 0
-    aligned = rows * cols % LANES == 0 and cols % SUBLANES == 0 and cols <= LANES
-    form = by_channels if whole and aligned else by_rows
-    if whole and aligned and lax.axis_size("row") == 16 and lax.axis_size("col") == 2:
-        form = by_halves
+    halved = blocks == 2 * 2**3 and splits == 2 and channels * 2 == blocks * splits * SUBLANES
+    aligned = rows * cols % LANES == 0 and cols < LANES and cols % (LANES - cols) == 0
+    packed = (LANES - cols) % (2 * SUBLANES) == 0 and cols % (2 * SUBLANES) == 0
+    form = by_halves if halved and aligned and packed else by_rows
     return form(pair_act, tile_mask, w_left_gate, *weights)
 
 

time: 48.1 us -> 46.7 us (0.971)
  blocking collectives: 10.8 us -> 9.59 us
    all_to_all x1, blocking collectives: 10.8 us -> 9.59 us  [by_halves(): lax.all_to_all(triangle, ('col', 'row'), 0, 0, tiled=True, axis_index_gro...]
where the time goes in v8:
time: 46.7 us; the launch traced here: 46.4 us
  waiting for transfers between devices  18.2 us (39%)
  starting transfers between devices  12.9 us (28%)
  blocking collectives  9.59 us (21%)
  Pallas kernels  5.41 us (12%)
    ppermute x5, waiting for transfers between devices, swap(): return lax.ppermute(block, ('row', 'col'), pairs)  18.2 us
    all_to_all x1, blocking collectives, by_halves(): lax.all_to_all(triangle, ('col', 'row'), 0, 0, tiled=True, axis_index_gro...  9.59 us
    all_to_all x1, starting transfers between devices, by_halves(): lax.all_to_all(right.reshape(blocks * splits, owned, pairs), ('col', 'row...  7.33 us
    ppermute x5, starting transfers between devices, swap(): return lax.ppermute(block, ('row', 'col'), pairs)  5.59 us
    pallas_call x5, Pallas kernels, call(): pl.pallas_call(body, out_shape=out, in_specs=[pl.BlockSpec(memory_space=s...  5.41 us
  transfers between devices with their start and end apart: 6, of which 5 were waited for; matrix products, arithmetic and copies ran while one was open for 0% of the time, Pallas kernels for 2%

profile of v8, /device:TPU:0, one launch (start us, length us, event | category | flops | bytes accessed | tf_op | source)
XLA Modules:
  0.0 46.4 jit_solution(2814279406337166644)
XLA Ops:
  0.0 2.7 %shard_map.82 = (bf16[8,8,1152]{2,1,0:T(8,128)(2,1)S(1)}, bf16[2,2,8,8,1152]{4,3,2,1,0:T(8,128)(2,1)}, bf16[1152,128]{1,0:T(8,128)(2,1)S(1)}) custom-call(bf16[1152,128]{1,0:T(8,128)(2,1)} %bitcast.6, s32[12,12]{1,0:T(8,128)} %refs_1_.3, bf16[128,128]{1,0:T(8,128)(2,1)} %refs_2_.3, bf16[128,128]{1,0:T(8,128)(2,1)} %refs_3_.3, bf16[128,128]{1,0:T(8,128)(2,1)} %refs_4_.2, ...), custom_call_target="tpu_custom_call" | custom-call | flops 150994944 | bytes 1509949 | tf_op jit(solution)/shard_map/pallas_call | solution.py:114
  2.7 0.0 copy-start.1
  2.7 0.0 copy-start.2
  2.7 0.0 copy-start.3
  2.7 0.0 copy-start.4
  2.7 7.3 %all-to-all-start = ((bf16[32,8,1152]{2,1,0:T(8,128)(2,1)}), bf16[32,8,1152]{2,1,0:T(8,128)(2,1)S(1)}, u32[]{:S(2)}, u32[]{:S(2)}) async-start(bf16[32,8,1152]{2,1,0:T(8,128)(2,1)} %bitcast.5), calls=%async_computation | async-start | bytes 1179648 | tf_op jit(solution)/shard_map/all_to_all | solution.py:314
  10.1 1.8 %collective-permute-start = (bf16[8,8,1152]{2,1,0:T(8,128)(2,1)S(1)}, bf16[8,8,1152]{2,1,0:T(8,128)(2,1)S(1)}, u32[]{:S(2)}, u32[]{:S(2)}) collective-permute-start(bf16[8,8,1152]{2,1,0:T(8,128)(2,1)S(1)} %get-tuple-element.12), channel_id=1, source_target_pairs={{0,8},{2,10},{4,12},{6,14},{8,0},{10,2},{12,4},{14,6},{16,24},{18,... | collective-permute-start | bytes 442376 | tf_op jit(solution)/shard_map/ppermute | solution.py:281
  11.9 0.0 copy-done.1
  11.9 0.0 copy-done.2
  11.9 0.0 copy-done.3
  11.9 0.0 copy-done.4
  11.9 0.5 %shard_map.83 = (bf16[8,8,1152]{2,1,0:T(8,128)(2,1)S(1)}, f32[1152,128]{1,0:T(8,128)S(1)}) custom-call(bf16[1152,128]{1,0:T(8,128)(2,1)S(1)} %get-tuple-element.10.refs_0_, s32[12,12]{1,0:T(8,128)S(1)} %copy-done.4, bf16[128,128]{1,0:T(8,128)(2,1)S(1)} %copy-done.1, bf16[128,128]{1,0:T(8,128)(2,1)S(1)} %copy-done.2, bf16[128,128]{1,0:T(8,128)(2,1)S(1)} %copy-done.3), custom_call_target="tpu_custom_call" | custom-call | flops 113246208 | bytes 1132462 | tf_op jit(solution)/shard_map/pallas_call | solution.py:114
  12.5 11.8 %collective-permute-done = bf16[8,8,1152]{2,1,0:T(8,128)(2,1)S(1)} collective-permute-done((bf16[8,8,1152]{2,1,0:T(8,128)(2,1)S(1)}, bf16[8,8,1152]{2,1,0:T(8,128)(2,1)S(1)}, u32[]{:S(2)}, u32[]{:S(2)}) %collective-permute-start) | collective-permute-done | bytes 147488 | tf_op jit(solution)/shard_map/ppermute | solution.py:281
  24.3 1.9 %collective-permute-start.1 = (bf16[4,8,1152]{2,1,0:T(8,128)(2,1)S(1)}, bf16[4,8,1152]{2,1,0:T(8,128)(2,1)S(1)}, u32[]{:S(2)}, u32[]{:S(2)}) collective-permute-start(bf16[4,8,1152]{2,1,0:T(8,128)(2,1)S(1)} %pad_maximum_fusion), channel_id=1, source_target_pairs={{0,4},{2,6},{4,0},{6,2},{8,12},{10,14},{12,8},{14,10},{16,20},{18,... | collective-permute-start | bytes 221192 | tf_op jit(solution)/shard_map/ppermute | solution.py:281
  26.2 1.5 %collective-permute-start.2 = (bf16[4,8,1152]{2,1,0:T(8,128)(2,1)S(1)}, bf16[4,8,1152]{2,1,0:T(8,128)(2,1)S(1)}, u32[]{:S(2)}, u32[]{:S(2)}) collective-permute-start(bf16[4,8,1152]{2,1,0:T(8,128)(2,1)S(1)} %pad_maximum_fusion.1), channel_id=1, source_target_pairs={{0,1},{2,3},{4,5},{6,7},{8,9},{10,11},{12,13},{14,15},{16,17},{18,... | collective-permute-start | bytes 221192 | tf_op jit(solution)/shard_map/ppermute | solution.py:281
  27.8 0.3 collective-permute-start.3
  28.0 0.8 %collective-permute-done.1 = bf16[4,8,1152]{2,1,0:T(8,128)(2,1)S(1)} collective-permute-done((bf16[4,8,1152]{2,1,0:T(8,128)(2,1)S(1)}, bf16[4,8,1152]{2,1,0:T(8,128)(2,1)S(1)}, u32[]{:S(2)}, u32[]{:S(2)}) %collective-permute-start.1) | collective-permute-done | bytes 73760 | tf_op jit(solution)/shard_map/ppermute | solution.py:281
  28.9 1.8 %collective-permute-done.2 = bf16[4,8,1152]{2,1,0:T(8,128)(2,1)S(1)} collective-permute-done((bf16[4,8,1152]{2,1,0:T(8,128)(2,1)S(1)}, bf16[4,8,1152]{2,1,0:T(8,128)(2,1)S(1)}, u32[]{:S(2)}, u32[]{:S(2)}) %collective-permute-start.2) | collective-permute-done | bytes 73760 | tf_op jit(solution)/shard_map/ppermute | solution.py:281
  30.7 2.4 %collective-permute-done.3 = bf16[4,8,1152]{2,1,0:T(8,128)(2,1)S(1)} collective-permute-done((bf16[4,8,1152]{2,1,0:T(8,128)(2,1)S(1)}, bf16[4,8,1152]{2,1,0:T(8,128)(2,1)S(1)}, u32[]{:S(2)}, u32[]{:S(2)}) %collective-permute-start.3) | collective-permute-done | bytes 73760 | tf_op jit(solution)/shard_map/ppermute | solution.py:281
  33.1 0.1 collective-permute-start.4
  33.2 1.4 %collective-permute-done.4.refs_1_ = bf16[8,8,1152]{2,1,0:T(8,128)(2,1)S(1)} collective-permute-done((bf16[8,8,1152]{2,1,0:T(8,128)(2,1)S(1)}, bf16[8,8,1152]{2,1,0:T(8,128)(2,1)S(1)}, u32[]{:S(2)}, u32[]{:S(2)}) %collective-permute-start.4) | collective-permute-done | bytes 147488 | tf_op jit(solution)/shard_map/ppermute | solution.py:281
  34.5 0.3 shard_map.84.left_ref
  34.9 0.0 all-to-all-done
  34.9 0.8 %shard_map.85 = bf16[16,8,1152]{2,1,0:T(8,128)(2,1)S(1)} custom-call(bf16[8,96,256]{2,1,0:T(8,128)(2,1)S(1)} %shard_map.84.left_ref, bf16[2,16,8,1152]{3,2,1,0:T(8,128)(2,1)S(1)} %bitcast.4), custom_call_target="tpu_custom_call" | custom-call | flops 113246208 | bytes 1132462 | tf_op jit(solution)/shard_map/pallas_call | solution.py:114
  35.7 0.0 copy-start
  35.7 9.6 %all_to_all.10.t_ref = bf16[16,8,1152]{2,1,0:T(8,128)(2,1)S(1)} all-to-all(bf16[16,8,1152]{2,1,0:T(8,128)(2,1)S(1)} %shard_map.85), channel_id=1, replica_groups={{0,8,2,10,4,12,6,14,1,9,3,11,5,13,7,15},{16,24,18,26,20,28,22,30,17,25,..., dimensions={0} | all-to-all | bytes 589824 | tf_op jit(solution)/shard_map/all_to_all | solution.py:365
  45.3 0.0 copy-done
  45.3 1.1 %shard_map.86 = bf16[1152,128]{1,0:T(8,128)(2,1)} custom-call(bf16[16,8,1152]{2,1,0:T(8,128)(2,1)S(1)} %all_to_all.10.t_ref, f32[1152,128]{1,0:T(8,128)S(1)} %get-tuple-element.14.gate_ref, bf16[128,128]{1,0:T(8,128)(2,1)S(1)} %copy-done), custom_call_target="tpu_custom_call" | custom-call | flops 37748736 | bytes 377487 | tf_op jit(solution)/shard_map/pallas_call | solution.py:114
  (16 shorter events, 0.2 us)
Async XLA Ops:
  2.7 9.2 %copy-start.1 = (bf16[128,128]{1,0:T(8,128)(2,1)S(1)}, bf16[128,128]{1,0:T(8,128)(2,1)}, u32[]{:S(2)}) copy-start(bf16[128,128]{1,0:T(8,128)(2,1)} %refs_2_.3) | copy-start | bytes 98308
  2.7 9.2 %copy-start.2 = (bf16[128,128]{1,0:T(8,128)(2,1)S(1)}, bf16[128,128]{1,0:T(8,128)(2,1)}, u32[]{:S(2)}) copy-start(bf16[128,128]{1,0:T(8,128)(2,1)} %refs_3_.3) | copy-start | bytes 98308
  2.7 9.2 %copy-start.3 = (bf16[128,128]{1,0:T(8,128)(2,1)S(1)}, bf16[128,128]{1,0:T(8,128)(2,1)}, u32[]{:S(2)}) copy-start(bf16[128,128]{1,0:T(8,128)(2,1)} %refs_4_.3) | copy-start | bytes 98308
  2.7 9.2 %copy-start.4 = (s32[12,12]{1,0:T(8,128)S(1)}, s32[12,12]{1,0:T(8,128)}, u32[]{:S(2)}) copy-start(s32[12,12]{1,0:T(8,128)} %refs_1_.3) | copy-start | bytes 1732
  2.7 32.1 %all-to-all-start = ((bf16[32,8,1152]{2,1,0:T(8,128)(2,1)}), bf16[32,8,1152]{2,1,0:T(8,128)(2,1)S(1)}, u32[]{:S(2)}, u32[]{:S(2)}) async-start(bf16[32,8,1152]{2,1,0:T(8,128)(2,1)} %bitcast.5), calls=%async_computation | async-start | bytes 1179648 | tf_op jit(solution)/shard_map/all_to_all | solution.py:314
  10.1 14.2 %collective-permute-start = (bf16[8,8,1152]{2,1,0:T(8,128)(2,1)S(1)}, bf16[8,8,1152]{2,1,0:T(8,128)(2,1)S(1)}, u32[]{:S(2)}, u32[]{:S(2)}) collective-permute-start(bf16[8,8,1152]{2,1,0:T(8,128)(2,1)S(1)} %get-tuple-element.12), channel_id=1, source_target_pairs={{0,8},{2,10},{4,12},{6,14},{8,0},{10,2},{12,4},{14,6},{16,24},{18,... | collective-permute-start | bytes 442376 | tf_op jit(solution)/shard_map/ppermute | solution.py:281
  24.3 4.6 %collective-permute-start.1 = (bf16[4,8,1152]{2,1,0:T(8,128)(2,1)S(1)}, bf16[4,8,1152]{2,1,0:T(8,128)(2,1)S(1)}, u32[]{:S(2)}, u32[]{:S(2)}) collective-permute-start(bf16[4,8,1152]{2,1,0:T(8,128)(2,1)S(1)} %pad_maximum_fusion), channel_id=1, source_target_pairs={{0,4},{2,6},{4,0},{6,2},{8,12},{10,14},{12,8},{14,10},{16,20},{18,... | collective-permute-start | bytes 221192 | tf_op jit(solution)/shard_map/ppermute | solution.py:281
  26.2 4.4 %collective-permute-start.2 = (bf16[4,8,1152]{2,1,0:T(8,128)(2,1)S(1)}, bf16[4,8,1152]{2,1,0:T(8,128)(2,1)S(1)}, u32[]{:S(2)}, u32[]{:S(2)}) collective-permute-start(bf16[4,8,1152]{2,1,0:T(8,128)(2,1)S(1)} %pad_maximum_fusion.1), channel_id=1, source_target_pairs={{0,1},{2,3},{4,5},{6,7},{8,9},{10,11},{12,13},{14,15},{16,17},{18,... | collective-permute-start | bytes 221192 | tf_op jit(solution)/shard_map/ppermute | solution.py:281
  27.8 5.3 %collective-permute-start.3 = (bf16[4,8,1152]{2,1,0:T(8,128)(2,1)S(1)}, bf16[4,8,1152]{2,1,0:T(8,128)(2,1)S(1)}, u32[]{:S(2)}, u32[]{:S(2)}) collective-permute-start(bf16[4,8,1152]{2,1,0:T(8,128)(2,1)S(1)} %pad_maximum_fusion.2), channel_id=1, source_target_pairs={{0,5},{2,7},{4,1},{6,3},{8,13},{10,15},{12,9},{14,11},{16,21},{18,... | collective-permute-start | bytes 221192 | tf_op jit(solution)/shard_map/ppermute | solution.py:281
  33.1 1.4 %collective-permute-start.4 = (bf16[8,8,1152]{2,1,0:T(8,128)(2,1)S(1)}, bf16[8,8,1152]{2,1,0:T(8,128)(2,1)S(1)}, u32[]{:S(2)}, u32[]{:S(2)}) collective-permute-start(bf16[8,8,1152]{2,1,0:T(8,128)(2,1)S(1)} %get-tuple-element.25), channel_id=1, source_target_pairs={{0,2},{2,0},{4,6},{6,4},{8,10},{10,8},{12,14},{14,12},{16,18},{18,... | collective-permute-start | bytes 442376 | tf_op jit(solution)/shard_map/ppermute | solution.py:281
  35.7 9.6 %copy-start = (bf16[128,128]{1,0:T(8,128)(2,1)S(1)}, bf16[128,128]{1,0:T(8,128)(2,1)}, u32[]{:S(2)}) copy-start(bf16[128,128]{1,0:T(8,128)(2,1)} %w_ref.1) | copy-start | bytes 98308

commit v9 on v8

--- a/solution.py
+++ b/solution.py
@@ -171,11 +171,15 @@
     pick_left = pick_slots(channels, owned, far_bit, 1)
     row = lax.broadcasted_iota(jnp.int32, (channels, channels), 0)
     channel = lax.broadcasted_iota(jnp.int32, (channels, channels), 1)
-    pick_right = jnp.where(row == channel, 1.0, 0.0).astype(BF16)
+    splits, far_rows = right_ref.shape[0], right_ref.shape[2]
+    near_rows = right_ref.shape[1] * far_rows
+    slot = row // owned
+    member = slot // near_rows * near_rows + slot % far_rows * far_bit + slot % near_rows // far_rows
+    pick_right = jnp.where(member * owned + row % owned == channel, 1.0, 0.0).astype(BF16)
     for copy in copies:
         copy.wait()
     mask = lane_mask(pairs // rows, tile, pairs, rows, tiles_ref[...]).astype(BF16)
-    halves = right_far.shape[1]
+    halves = right_far.shape[2]
     make_right = factor_maker(pick_right, rg_ref, r_ref, mask, right_ref)
     make_left = factor_maker(pick_left, lg_ref, l_ref, mask, left_ref)
     for start, wide in strips_of(pairs):
@@ -184,9 +188,8 @@
         normed = norm_axis(strip.astype(F32), 1).astype(BF16)
         normed_ref[here, :] = normed
         make_right(normed, start, wide)
-    splits = right_far.shape[0]
     sent = [
-        pltpu.make_async_copy(right_ref.at[q], right_far.at[q, half], right_sems.at[q, half])
+        pltpu.make_async_copy(right_ref.at[q], right_far.at[q, :, half], right_sems.at[q, half])
         for q in range(splits)
         for half in range(halves)
     ]
@@ -233,12 +236,12 @@
     return lax.axis_index("col") * near_rows + lax.axis_index("row") % near_rows
 
 
-def halves_triangle_kernel(rows, cols, members, left_ref, right_ref, out_ref, rights, products):
+def halves_triangle_kernel(rows, cols, members, lines, left_ref, right_ref, out_ref, rights, products):
     splits, blocks, owned = right_ref.shape[:3]
     near_rows = members // splits
     for q in range(splits):
-        for r in range(blocks):
-            for i, piece in enumerate(rows_of(right_ref[q, r].astype(F32), rows, cols)):
+        for n, r in enumerate(lines):
+            for i, piece in enumerate(rows_of(right_ref[q, n].astype(F32), rows, cols)):
                 rights[q, pl.ds((r * rows + i) * owned, owned), :] = piece
     residues, half = blocks * rows, near_rows * rows
     gap = LANES - cols
@@ -298,21 +301,28 @@
         functools.partial(halves_project_kernel, rows, tile, owned, z),
         (
             pltpu.VMEM((members // 2, owned, pairs), BF16),
-            pltpu.HBM((splits, halves, near_rows, owned, pairs), BF16),
+            pltpu.HBM((splits, z, halves, near_rows // z, owned, pairs), BF16),
             pltpu.VMEM((pairs, width), BF16),
         ),
         operands,
         scratch=[pltpu.VMEM(a.shape, a.dtype) for a in operands]
         + [
-            pltpu.VMEM((splits, near_rows, owned, pairs), BF16),
+            pltpu.VMEM((splits, z, near_rows // z, owned, pairs), BF16),
             pltpu.SemaphoreType.DMA((len(operands),)),
             pltpu.SemaphoreType.DMA((splits, halves)),
         ],
         flops=8 * pairs * width * channels,
         space=pltpu.HBM,
     )
+    lines = sorted(range(blocks), key=lambda r: (r % z, r // z))
+    everyone = [[q * blocks + r for q in range(splits) for r in lines]]
     right = lax.all_to_all(
-        right.reshape(blocks * splits, owned, pairs), ("col", "row"), 0, 0, tiled=True
+        right.reshape(blocks * splits, owned, pairs),
+        ("col", "row"),
+        0,
+        0,
+        tiled=True,
+        axis_index_groups=everyone,
     )
     got = swap(left, z, members)
     stayed, gate = call(
@@ -348,7 +358,7 @@
     )
     residues = rows * blocks
     triangle = call(
-        functools.partial(halves_triangle_kernel, rows, cols, members),
+        functools.partial(halves_triangle_kernel, rows, cols, members, lines),
         pltpu.VMEM((members, owned, pairs), BF16),
         (left, right.reshape(splits, blocks, owned, pairs)),
         scratch=(

time: 46.7 us -> 46.8 us (level)
  no operation moved by 1% of the time
where the time goes in v9:
time: 46.8 us; the launch traced here: 46.4 us
  waiting for transfers between devices  18.3 us (39%)
  starting transfers between devices  12.9 us (28%)
  blocking collectives  9.41 us (20%)
  Pallas kernels  5.42 us (12%)
    ppermute x5, waiting for transfers between devices, swap(): return lax.ppermute(block, ('row', 'col'), pairs)  18.3 us
    all_to_all x1, blocking collectives, by_halves(): lax.all_to_all(triangle, ('col', 'row'), 0, 0, tiled=True, axis_index_gro...  9.41 us
    all_to_all x1, starting transfers between devices, by_halves(): lax.all_to_all(right.reshape(blocks * splits, owned, pairs), ('col', 'row...  7.33 us
    ppermute x5, starting transfers between devices, swap(): return lax.ppermute(block, ('row', 'col'), pairs)  5.59 us
    pallas_call x5, Pallas kernels, call(): pl.pallas_call(body, out_shape=out, in_specs=[pl.BlockSpec(memory_space=s...  5.42 us
  transfers between devices with their start and end apart: 6, of which 5 were waited for; matrix products, arithmetic and copies ran while one was open for 0% of the time, Pallas kernels for 2%

profile of v9, /device:TPU:0, one launch (start us, length us, event | category | flops | bytes accessed | tf_op | source)
XLA Modules:
  0.0 46.4 jit_solution(4545348976524678080)
XLA Ops:
  0.0 2.7 %shard_map.82 = (bf16[8,8,1152]{2,1,0:T(8,128)(2,1)S(1)}, bf16[2,4,2,2,8,1152]{5,4,3,2,1,0:T(8,128)(2,1)}, bf16[1152,128]{1,0:T(8,128)(2,1)S(1)}) custom-call(bf16[1152,128]{1,0:T(8,128)(2,1)} %bitcast.6, s32[12,12]{1,0:T(8,128)} %refs_1_.3, bf16[128,128]{1,0:T(8,128)(2,1)} %refs_2_.3, bf16[128,128]{1,0:T(8,128)(2,1)} %refs_3_.3, bf16[128,128]{1,0:T(8,128)(2,1)} %refs_4_.2, ...), custom_call_target="tpu_custom_call" | custom-call | flops 150994944 | bytes 1509949 | tf_op jit(solution)/shard_map/pallas_call | solution.py:114
  2.7 0.0 copy-start.1
  2.7 0.0 copy-start.2
  2.7 0.0 copy-start.3
  2.7 0.0 copy-start.4
  2.7 7.3 %all-to-all-start = ((bf16[32,8,1152]{2,1,0:T(8,128)(2,1)}), bf16[32,8,1152]{2,1,0:T(8,128)(2,1)S(1)}, u32[]{:S(2)}, u32[]{:S(2)}) async-start(bf16[32,8,1152]{2,1,0:T(8,128)(2,1)} %bitcast.5), calls=%async_computation | async-start | bytes 1179648 | tf_op jit(solution)/shard_map/all_to_all | solution.py:319
  10.1 1.8 %collective-permute-start = (bf16[8,8,1152]{2,1,0:T(8,128)(2,1)S(1)}, bf16[8,8,1152]{2,1,0:T(8,128)(2,1)S(1)}, u32[]{:S(2)}, u32[]{:S(2)}) collective-permute-start(bf16[8,8,1152]{2,1,0:T(8,128)(2,1)S(1)} %get-tuple-element.12), channel_id=1, source_target_pairs={{0,8},{2,10},{4,12},{6,14},{8,0},{10,2},{12,4},{14,6},{16,24},{18,... | collective-permute-start | bytes 442376 | tf_op jit(solution)/shard_map/ppermute | solution.py:284
  11.9 0.0 copy-done.1
  11.9 0.0 copy-done.2
  11.9 0.0 copy-done.3
  11.9 0.0 copy-done.4
  11.9 0.5 %shard_map.83 = (bf16[8,8,1152]{2,1,0:T(8,128)(2,1)S(1)}, f32[1152,128]{1,0:T(8,128)S(1)}) custom-call(bf16[1152,128]{1,0:T(8,128)(2,1)S(1)} %get-tuple-element.10.refs_0_, s32[12,12]{1,0:T(8,128)S(1)} %copy-done.4, bf16[128,128]{1,0:T(8,128)(2,1)S(1)} %copy-done.1, bf16[128,128]{1,0:T(8,128)(2,1)S(1)} %copy-done.2, bf16[128,128]{1,0:T(8,128)(2,1)S(1)} %copy-done.3), custom_call_target="tpu_custom_call" | custom-call | flops 113246208 | bytes 1132462 | tf_op jit(solution)/shard_map/pallas_call | solution.py:114
  12.5 12.4 %collective-permute-done = bf16[8,8,1152]{2,1,0:T(8,128)(2,1)S(1)} collective-permute-done((bf16[8,8,1152]{2,1,0:T(8,128)(2,1)S(1)}, bf16[8,8,1152]{2,1,0:T(8,128)(2,1)S(1)}, u32[]{:S(2)}, u32[]{:S(2)}) %collective-permute-start) | collective-permute-done | bytes 147488 | tf_op jit(solution)/shard_map/ppermute | solution.py:284
  24.9 1.5 %collective-permute-start.1 = (bf16[4,8,1152]{2,1,0:T(8,128)(2,1)S(1)}, bf16[4,8,1152]{2,1,0:T(8,128)(2,1)S(1)}, u32[]{:S(2)}, u32[]{:S(2)}) collective-permute-start(bf16[4,8,1152]{2,1,0:T(8,128)(2,1)S(1)} %pad_maximum_fusion), channel_id=1, source_target_pairs={{0,4},{2,6},{4,0},{6,2},{8,12},{10,14},{12,8},{14,10},{16,20},{18,... | collective-permute-start | bytes 221192 | tf_op jit(solution)/shard_map/ppermute | solution.py:284
  26.4 1.5 %collective-permute-start.2 = (bf16[4,8,1152]{2,1,0:T(8,128)(2,1)S(1)}, bf16[4,8,1152]{2,1,0:T(8,128)(2,1)S(1)}, u32[]{:S(2)}, u32[]{:S(2)}) collective-permute-start(bf16[4,8,1152]{2,1,0:T(8,128)(2,1)S(1)} %pad_maximum_fusion.1), channel_id=1, source_target_pairs={{0,1},{2,3},{4,5},{6,7},{8,9},{10,11},{12,13},{14,15},{16,17},{18,... | collective-permute-start | bytes 221192 | tf_op jit(solution)/shard_map/ppermute | solution.py:284
  27.9 0.7 %collective-permute-start.3 = (bf16[4,8,1152]{2,1,0:T(8,128)(2,1)S(1)}, bf16[4,8,1152]{2,1,0:T(8,128)(2,1)S(1)}, u32[]{:S(2)}, u32[]{:S(2)}) collective-permute-start(bf16[4,8,1152]{2,1,0:T(8,128)(2,1)S(1)} %pad_maximum_fusion.2), channel_id=1, source_target_pairs={{0,5},{2,7},{4,1},{6,3},{8,13},{10,15},{12,9},{14,11},{16,21},{18,... | collective-permute-start | bytes 221192 | tf_op jit(solution)/shard_map/ppermute | solution.py:284
  28.6 0.7 %collective-permute-done.1 = bf16[4,8,1152]{2,1,0:T(8,128)(2,1)S(1)} collective-permute-done((bf16[4,8,1152]{2,1,0:T(8,128)(2,1)S(1)}, bf16[4,8,1152]{2,1,0:T(8,128)(2,1)S(1)}, u32[]{:S(2)}, u32[]{:S(2)}) %collective-permute-start.1) | collective-permute-done | bytes 73760 | tf_op jit(solution)/shard_map/ppermute | solution.py:284
  29.3 1.5 %collective-permute-done.2 = bf16[4,8,1152]{2,1,0:T(8,128)(2,1)S(1)} collective-permute-done((bf16[4,8,1152]{2,1,0:T(8,128)(2,1)S(1)}, bf16[4,8,1152]{2,1,0:T(8,128)(2,1)S(1)}, u32[]{:S(2)}, u32[]{:S(2)}) %collective-permute-start.2) | collective-permute-done | bytes 73760 | tf_op jit(solution)/shard_map/ppermute | solution.py:284
  30.9 2.4 %collective-permute-done.3 = bf16[4,8,1152]{2,1,0:T(8,128)(2,1)S(1)} collective-permute-done((bf16[4,8,1152]{2,1,0:T(8,128)(2,1)S(1)}, bf16[4,8,1152]{2,1,0:T(8,128)(2,1)S(1)}, u32[]{:S(2)}, u32[]{:S(2)}) %collective-permute-start.3) | collective-permute-done | bytes 73760 | tf_op jit(solution)/shard_map/ppermute | solution.py:284
  33.3 0.1 collective-permute-start.4
  33.4 1.4 %collective-permute-done.4.refs_1_ = bf16[8,8,1152]{2,1,0:T(8,128)(2,1)S(1)} collective-permute-done((bf16[8,8,1152]{2,1,0:T(8,128)(2,1)S(1)}, bf16[8,8,1152]{2,1,0:T(8,128)(2,1)S(1)}, u32[]{:S(2)}, u32[]{:S(2)}) %collective-permute-start.4) | collective-permute-done | bytes 147488 | tf_op jit(solution)/shard_map/ppermute | solution.py:284
  34.7 0.3 shard_map.84.left_ref
  35.1 0.0 all-to-all-done
  35.1 0.8 %shard_map.85 = bf16[16,8,1152]{2,1,0:T(8,128)(2,1)S(1)} custom-call(bf16[8,96,256]{2,1,0:T(8,128)(2,1)S(1)} %shard_map.84.left_ref, bf16[2,16,8,1152]{3,2,1,0:T(8,128)(2,1)S(1)} %bitcast.4), custom_call_target="tpu_custom_call" | custom-call | flops 113246208 | bytes 1132462 | tf_op jit(solution)/shard_map/pallas_call | solution.py:114
  35.9 0.0 copy-start
  35.9 9.4 %all_to_all.10.t_ref = bf16[16,8,1152]{2,1,0:T(8,128)(2,1)S(1)} all-to-all(bf16[16,8,1152]{2,1,0:T(8,128)(2,1)S(1)} %shard_map.85), channel_id=1, replica_groups={{0,8,2,10,4,12,6,14,1,9,3,11,5,13,7,15},{16,24,18,26,20,28,22,30,17,25,..., dimensions={0} | all-to-all | bytes 589824 | tf_op jit(solution)/shard_map/all_to_all | solution.py:375
  45.3 0.0 copy-done
  45.3 1.1 %shard_map.86 = bf16[1152,128]{1,0:T(8,128)(2,1)} custom-call(bf16[16,8,1152]{2,1,0:T(8,128)(2,1)S(1)} %all_to_all.10.t_ref, f32[1152,128]{1,0:T(8,128)S(1)} %get-tuple-element.14.gate_ref, bf16[128,128]{1,0:T(8,128)(2,1)S(1)} %copy-done), custom_call_target="tpu_custom_call" | custom-call | flops 37748736 | bytes 377487 | tf_op jit(solution)/shard_map/pallas_call | solution.py:114
  (16 shorter events, 0.2 us)
Async XLA Ops:
  2.7 9.2 %copy-start.1 = (bf16[128,128]{1,0:T(8,128)(2,1)S(1)}, bf16[128,128]{1,0:T(8,128)(2,1)}, u32[]{:S(2)}) copy-start(bf16[128,128]{1,0:T(8,128)(2,1)} %refs_2_.3) | copy-start | bytes 98308
  2.7 9.2 %copy-start.2 = (bf16[128,128]{1,0:T(8,128)(2,1)S(1)}, bf16[128,128]{1,0:T(8,128)(2,1)}, u32[]{:S(2)}) copy-start(bf16[128,128]{1,0:T(8,128)(2,1)} %refs_3_.3) | copy-start | bytes 98308
  2.7 9.2 %copy-start.3 = (bf16[128,128]{1,0:T(8,128)(2,1)S(1)}, bf16[128,128]{1,0:T(8,128)(2,1)}, u32[]{:S(2)}) copy-start(bf16[128,128]{1,0:T(8,128)(2,1)} %refs_4_.3) | copy-start | bytes 98308
  2.7 9.2 %copy-start.4 = (s32[12,12]{1,0:T(8,128)S(1)}, s32[12,12]{1,0:T(8,128)}, u32[]{:S(2)}) copy-start(s32[12,12]{1,0:T(8,128)} %refs_1_.3) | copy-start | bytes 1732
  2.7 32.3 %all-to-all-start = ((bf16[32,8,1152]{2,1,0:T(8,128)(2,1)}), bf16[32,8,1152]{2,1,0:T(8,128)(2,1)S(1)}, u32[]{:S(2)}, u32[]{:S(2)}) async-start(bf16[32,8,1152]{2,1,0:T(8,128)(2,1)} %bitcast.5), calls=%async_computation | async-start | bytes 1179648 | tf_op jit(solution)/shard_map/all_to_all | solution.py:319
  10.1 14.8 %collective-permute-start = (bf16[8,8,1152]{2,1,0:T(8,128)(2,1)S(1)}, bf16[8,8,1152]{2,1,0:T(8,128)(2,1)S(1)}, u32[]{:S(2)}, u32[]{:S(2)}) collective-permute-start(bf16[8,8,1152]{2,1,0:T(8,128)(2,1)S(1)} %get-tuple-element.12), channel_id=1, source_target_pairs={{0,8},{2,10},{4,12},{6,14},{8,0},{10,2},{12,4},{14,6},{16,24},{18,... | collective-permute-start | bytes 442376 | tf_op jit(solution)/shard_map/ppermute | solution.py:284
  24.9 4.4 %collective-permute-start.1 = (bf16[4,8,1152]{2,1,0:T(8,128)(2,1)S(1)}, bf16[4,8,1152]{2,1,0:T(8,128)(2,1)S(1)}, u32[]{:S(2)}, u32[]{:S(2)}) collective-permute-start(bf16[4,8,1152]{2,1,0:T(8,128)(2,1)S(1)} %pad_maximum_fusion), channel_id=1, source_target_pairs={{0,4},{2,6},{4,0},{6,2},{8,12},{10,14},{12,8},{14,10},{16,20},{18,... | collective-permute-start | bytes 221192 | tf_op jit(solution)/shard_map/ppermute | solution.py:284
  26.4 4.4 %collective-permute-start.2 = (bf16[4,8,1152]{2,1,0:T(8,128)(2,1)S(1)}, bf16[4,8,1152]{2,1,0:T(8,128)(2,1)S(1)}, u32[]{:S(2)}, u32[]{:S(2)}) collective-permute-start(bf16[4,8,1152]{2,1,0:T(8,128)(2,1)S(1)} %pad_maximum_fusion.1), channel_id=1, source_target_pairs={{0,1},{2,3},{4,5},{6,7},{8,9},{10,11},{12,13},{14,15},{16,17},{18,... | collective-permute-start | bytes 221192 | tf_op jit(solution)/shard_map/ppermute | solution.py:284
  27.9 5.3 %collective-permute-start.3 = (bf16[4,8,1152]{2,1,0:T(8,128)(2,1)S(1)}, bf16[4,8,1152]{2,1,0:T(8,128)(2,1)S(1)}, u32[]{:S(2)}, u32[]{:S(2)}) collective-permute-start(bf16[4,8,1152]{2,1,0:T(8,128)(2,1)S(1)} %pad_maximum_fusion.2), channel_id=1, source_target_pairs={{0,5},{2,7},{4,1},{6,3},{8,13},{10,15},{12,9},{14,11},{16,21},{18,... | collective-permute-start | bytes 221192 | tf_op jit(solution)/shard_map/ppermute | solution.py:284
  33.3 1.4 %collective-permute-start.4 = (bf16[8,8,1152]{2,1,0:T(8,128)(2,1)S(1)}, bf16[8,8,1152]{2,1,0:T(8,128)(2,1)S(1)}, u32[]{:S(2)}, u32[]{:S(2)}) collective-permute-start(bf16[8,8,1152]{2,1,0:T(8,128)(2,1)S(1)} %get-tuple-element.25), channel_id=1, source_target_pairs={{0,2},{2,0},{4,6},{6,4},{8,10},{10,8},{12,14},{14,12},{16,18},{18,... | collective-permute-start | bytes 442376 | tf_op jit(solution)/shard_map/ppermute | solution.py:284
  35.9 9.4 %copy-start = (bf16[128,128]{1,0:T(8,128)(2,1)S(1)}, bf16[128,128]{1,0:T(8,128)(2,1)}, u32[]{:S(2)}) copy-start(bf16[128,128]{1,0:T(8,128)(2,1)} %w_ref.1) | copy-start | bytes 98308

commit v10 on v9

--- a/solution.py
+++ b/solution.py
@@ -10,7 +10,7 @@
 
 TILES = 12
 LANES = 128
-WIDE = 256
+WIDE = 1152
 OWIDE = 256
 SUBLANES = 8
 EPS = 1e-05
@@ -73,8 +73,7 @@
     return jnp.concatenate(parts, axis=1)
 
 
-def lane_mask(cols, tile, pairs, rows, tiles):
-    kinds = tiles.shape[0]
+def lane_hots(cols, tile, pairs, rows, kinds):
     lane = lax.broadcasted_iota(jnp.int32, (kinds, pairs), 1)
     gap = LANES - cols
     tail = pairs // LANES * cols - cols
@@ -91,6 +90,11 @@
     col_kind = jnp.floor((col + first_col) * (1.0 / tile))
     row_hot = jnp.where(row_kind == kind, 1.0, 0.0)
     col_hot = jnp.where(col_kind == kind, 1.0, 0.0).astype(BF16)
+    return row_hot, col_hot
+
+
+def lane_mask(hots, tiles):
+    row_hot, col_hot = hots
     return jnp.sum(row_hot * dot(tiles.astype(F32).astype(BF16), col_hot), axis=0, keepdims=True)
 
 
@@ -176,12 +180,12 @@
     slot = row // owned
     member = slot // near_rows * near_rows + slot % far_rows * far_bit + slot % near_rows // far_rows
     pick_right = jnp.where(member * owned + row % owned == channel, 1.0, 0.0).astype(BF16)
-    for copy in copies:
+    hots = lane_hots(pairs // rows, tile, pairs, rows, tiles_ref.shape[0])
+    for copy in copies[:2] + copies[4:]:
         copy.wait()
-    mask = lane_mask(pairs // rows, tile, pairs, rows, tiles_ref[...]).astype(BF16)
+    mask = lane_mask(hots, tiles_ref[...]).astype(BF16)
     halves = right_far.shape[2]
     make_right = factor_maker(pick_right, rg_ref, r_ref, mask, right_ref)
-    make_left = factor_maker(pick_left, lg_ref, l_ref, mask, left_ref)
     for start, wide in strips_of(pairs):
         here = pl.ds(start, wide)
         strip = gather_strip(x_ref, start, wide, pairs // rows)
@@ -195,6 +199,9 @@
     ]
     for copy in sent:
         copy.start()
+    for copy in copies[2:4]:
+        copy.wait()
+    make_left = factor_maker(pick_left, lg_ref, l_ref, mask, left_ref)
     for start, wide in strips_of(pairs):
         make_left(normed_ref[pl.ds(start, wide), :], start, wide)
     for copy in sent:
@@ -205,7 +212,8 @@
     normed_ref, tiles_ref, lg_ref, l_ref, og_ref, left_ref, gate_ref = refs
     pairs = normed_ref.shape[0]
     pick = pick_slots(l_ref.shape[1], owned, far_bit, 0)
-    mask = lane_mask(pairs // rows, tile, pairs, rows, tiles_ref[...]).astype(BF16)
+    hots = lane_hots(pairs // rows, tile, pairs, rows, tiles_ref.shape[0])
+    mask = lane_mask(hots, tiles_ref[...]).astype(BF16)
     make_left = factor_maker(pick, lg_ref, l_ref, mask, left_ref)
     for start, wide in strips_of(pairs):
         normed = normed_ref[pl.ds(start, wide), :]

time: 46.8 us -> 46.6 us (level)
  no operation moved by 1% of the time
where the time goes in v10:
time: 46.6 us; the launch traced here: 46.3 us
  waiting for transfers between devices  18.3 us (39%)
  starting transfers between devices  12.9 us (28%)
  blocking collectives  9.41 us (20%)
  Pallas kernels  5.37 us (12%)
    ppermute x5, waiting for transfers between devices, swap(): return lax.ppermute(block, ('row', 'col'), pairs)  18.3 us
    all_to_all x1, blocking collectives, by_halves(): lax.all_to_all(triangle, ('col', 'row'), 0, 0, tiled=True, axis_index_gro...  9.41 us
    all_to_all x1, starting transfers between devices, by_halves(): lax.all_to_all(right.reshape(blocks * splits, owned, pairs), ('col', 'row...  7.33 us
    ppermute x5, starting transfers between devices, swap(): return lax.ppermute(block, ('row', 'col'), pairs)  5.59 us
    pallas_call x5, Pallas kernels, call(): pl.pallas_call(body, out_shape=out, in_specs=[pl.BlockSpec(memory_space=s...  5.37 us
  transfers between devices with their start and end apart: 6, of which 5 were waited for; matrix products, arithmetic and copies ran while one was open for 0% of the time, Pallas kernels for 2%

profile of v10, /device:TPU:0, one launch (start us, length us, event | category | flops | bytes accessed | tf_op | source)
XLA Modules:
  0.0 46.3 jit_solution(11799997794948175491)
XLA Ops:
  0.0 2.6 %shard_map.82 = (bf16[8,8,1152]{2,1,0:T(8,128)(2,1)S(1)}, bf16[2,4,2,2,8,1152]{5,4,3,2,1,0:T(8,128)(2,1)}, bf16[1152,128]{1,0:T(8,128)(2,1)S(1)}) custom-call(bf16[1152,128]{1,0:T(8,128)(2,1)} %bitcast.6, s32[12,12]{1,0:T(8,128)} %refs_1_.3, bf16[128,128]{1,0:T(8,128)(2,1)} %refs_2_.3, bf16[128,128]{1,0:T(8,128)(2,1)} %refs_3_.3, bf16[128,128]{1,0:T(8,128)(2,1)} %refs_4_.2, ...), custom_call_target="tpu_custom_call" | custom-call | flops 150994944 | bytes 1509949 | tf_op jit(solution)/shard_map/pallas_call | solution.py:118
  2.6 0.0 copy-start.1
  2.6 0.0 copy-start.2
  2.6 0.0 copy-start.3
  2.6 0.0 copy-start.4
  2.6 7.3 %all-to-all-start = ((bf16[32,8,1152]{2,1,0:T(8,128)(2,1)}), bf16[32,8,1152]{2,1,0:T(8,128)(2,1)S(1)}, u32[]{:S(2)}, u32[]{:S(2)}) async-start(bf16[32,8,1152]{2,1,0:T(8,128)(2,1)} %bitcast.5), calls=%async_computation | async-start | bytes 1179648 | tf_op jit(solution)/shard_map/all_to_all | solution.py:327
  9.9 1.8 %collective-permute-start = (bf16[8,8,1152]{2,1,0:T(8,128)(2,1)S(1)}, bf16[8,8,1152]{2,1,0:T(8,128)(2,1)S(1)}, u32[]{:S(2)}, u32[]{:S(2)}) collective-permute-start(bf16[8,8,1152]{2,1,0:T(8,128)(2,1)S(1)} %get-tuple-element.12), channel_id=1, source_target_pairs={{0,8},{2,10},{4,12},{6,14},{8,0},{10,2},{12,4},{14,6},{16,24},{18,... | collective-permute-start | bytes 442376 | tf_op jit(solution)/shard_map/ppermute | solution.py:292
  11.8 0.0 copy-done.1
  11.8 0.0 copy-done.2
  11.8 0.0 copy-done.3
  11.8 0.0 copy-done.4
  11.8 0.6 %shard_map.83 = (bf16[8,8,1152]{2,1,0:T(8,128)(2,1)S(1)}, f32[1152,128]{1,0:T(8,128)S(1)}) custom-call(bf16[1152,128]{1,0:T(8,128)(2,1)S(1)} %get-tuple-element.10.refs_0_, s32[12,12]{1,0:T(8,128)S(1)} %copy-done.4, bf16[128,128]{1,0:T(8,128)(2,1)S(1)} %copy-done.1, bf16[128,128]{1,0:T(8,128)(2,1)S(1)} %copy-done.2, bf16[128,128]{1,0:T(8,128)(2,1)S(1)} %copy-done.3), custom_call_target="tpu_custom_call" | custom-call | flops 113246208 | bytes 1132462 | tf_op jit(solution)/shard_map/pallas_call | solution.py:118
  12.4 12.3 %collective-permute-done = bf16[8,8,1152]{2,1,0:T(8,128)(2,1)S(1)} collective-permute-done((bf16[8,8,1152]{2,1,0:T(8,128)(2,1)S(1)}, bf16[8,8,1152]{2,1,0:T(8,128)(2,1)S(1)}, u32[]{:S(2)}, u32[]{:S(2)}) %collective-permute-start) | collective-permute-done | bytes 147488 | tf_op jit(solution)/shard_map/ppermute | solution.py:292
  24.8 1.5 %collective-permute-start.1 = (bf16[4,8,1152]{2,1,0:T(8,128)(2,1)S(1)}, bf16[4,8,1152]{2,1,0:T(8,128)(2,1)S(1)}, u32[]{:S(2)}, u32[]{:S(2)}) collective-permute-start(bf16[4,8,1152]{2,1,0:T(8,128)(2,1)S(1)} %pad_maximum_fusion), channel_id=1, source_target_pairs={{0,4},{2,6},{4,0},{6,2},{8,12},{10,14},{12,8},{14,10},{16,20},{18,... | collective-permute-start | bytes 221192 | tf_op jit(solution)/shard_map/ppermute | solution.py:292
  26.3 1.5 %collective-permute-start.2 = (bf16[4,8,1152]{2,1,0:T(8,128)(2,1)S(1)}, bf16[4,8,1152]{2,1,0:T(8,128)(2,1)S(1)}, u32[]{:S(2)}, u32[]{:S(2)}) collective-permute-start(bf16[4,8,1152]{2,1,0:T(8,128)(2,1)S(1)} %pad_maximum_fusion.1), channel_id=1, source_target_pairs={{0,1},{2,3},{4,5},{6,7},{8,9},{10,11},{12,13},{14,15},{16,17},{18,... | collective-permute-start | bytes 221192 | tf_op jit(solution)/shard_map/ppermute | solution.py:292
  27.8 0.7 %collective-permute-start.3 = (bf16[4,8,1152]{2,1,0:T(8,128)(2,1)S(1)}, bf16[4,8,1152]{2,1,0:T(8,128)(2,1)S(1)}, u32[]{:S(2)}, u32[]{:S(2)}) collective-permute-start(bf16[4,8,1152]{2,1,0:T(8,128)(2,1)S(1)} %pad_maximum_fusion.2), channel_id=1, source_target_pairs={{0,5},{2,7},{4,1},{6,3},{8,13},{10,15},{12,9},{14,11},{16,21},{18,... | collective-permute-start | bytes 221192 | tf_op jit(solution)/shard_map/ppermute | solution.py:292
  28.5 0.7 %collective-permute-done.1 = bf16[4,8,1152]{2,1,0:T(8,128)(2,1)S(1)} collective-permute-done((bf16[4,8,1152]{2,1,0:T(8,128)(2,1)S(1)}, bf16[4,8,1152]{2,1,0:T(8,128)(2,1)S(1)}, u32[]{:S(2)}, u32[]{:S(2)}) %collective-permute-start.1) | collective-permute-done | bytes 73760 | tf_op jit(solution)/shard_map/ppermute | solution.py:292
  29.2 1.5 %collective-permute-done.2 = bf16[4,8,1152]{2,1,0:T(8,128)(2,1)S(1)} collective-permute-done((bf16[4,8,1152]{2,1,0:T(8,128)(2,1)S(1)}, bf16[4,8,1152]{2,1,0:T(8,128)(2,1)S(1)}, u32[]{:S(2)}, u32[]{:S(2)}) %collective-permute-start.2) | collective-permute-done | bytes 73760 | tf_op jit(solution)/shard_map/ppermute | solution.py:292
  30.8 2.4 %collective-permute-done.3 = bf16[4,8,1152]{2,1,0:T(8,128)(2,1)S(1)} collective-permute-done((bf16[4,8,1152]{2,1,0:T(8,128)(2,1)S(1)}, bf16[4,8,1152]{2,1,0:T(8,128)(2,1)S(1)}, u32[]{:S(2)}, u32[]{:S(2)}) %collective-permute-start.3) | collective-permute-done | bytes 73760 | tf_op jit(solution)/shard_map/ppermute | solution.py:292
  33.2 0.1 collective-permute-start.4
  33.2 1.4 %collective-permute-done.4.refs_1_ = bf16[8,8,1152]{2,1,0:T(8,128)(2,1)S(1)} collective-permute-done((bf16[8,8,1152]{2,1,0:T(8,128)(2,1)S(1)}, bf16[8,8,1152]{2,1,0:T(8,128)(2,1)S(1)}, u32[]{:S(2)}, u32[]{:S(2)}) %collective-permute-start.4) | collective-permute-done | bytes 147488 | tf_op jit(solution)/shard_map/ppermute | solution.py:292
  34.6 0.3 shard_map.84.left_ref
  34.9 0.0 all-to-all-done
  34.9 0.8 %shard_map.85 = bf16[16,8,1152]{2,1,0:T(8,128)(2,1)S(1)} custom-call(bf16[8,96,256]{2,1,0:T(8,128)(2,1)S(1)} %shard_map.84.left_ref, bf16[2,16,8,1152]{3,2,1,0:T(8,128)(2,1)S(1)} %bitcast.4), custom_call_target="tpu_custom_call" | custom-call | flops 113246208 | bytes 1132462 | tf_op jit(solution)/shard_map/pallas_call | solution.py:118
  35.8 0.0 copy-start
  35.8 9.4 %all_to_all.10.t_ref = bf16[16,8,1152]{2,1,0:T(8,128)(2,1)S(1)} all-to-all(bf16[16,8,1152]{2,1,0:T(8,128)(2,1)S(1)} %shard_map.85), channel_id=1, replica_groups={{0,8,2,10,4,12,6,14,1,9,3,11,5,13,7,15},{16,24,18,26,20,28,22,30,17,25,..., dimensions={0} | all-to-all | bytes 589824 | tf_op jit(solution)/shard_map/all_to_all | solution.py:383
  45.2 0.0 copy-done
  45.2 1.1 %shard_map.86 = bf16[1152,128]{1,0:T(8,128)(2,1)} custom-call(bf16[16,8,1152]{2,1,0:T(8,128)(2,1)S(1)} %all_to_all.10.t_ref, f32[1152,128]{1,0:T(8,128)S(1)} %get-tuple-element.14.gate_ref, bf16[128,128]{1,0:T(8,128)(2,1)S(1)} %copy-done), custom_call_target="tpu_custom_call" | custom-call | flops 37748736 | bytes 377487 | tf_op jit(solution)/shard_map/pallas_call | solution.py:118
  (16 shorter events, 0.2 us)
Async XLA Ops:
  2.6 9.2 %copy-start.1 = (bf16[128,128]{1,0:T(8,128)(2,1)S(1)}, bf16[128,128]{1,0:T(8,128)(2,1)}, u32[]{:S(2)}) copy-start(bf16[128,128]{1,0:T(8,128)(2,1)} %refs_2_.3) | copy-start | bytes 98308
  2.6 9.2 %copy-start.2 = (bf16[128,128]{1,0:T(8,128)(2,1)S(1)}, bf16[128,128]{1,0:T(8,128)(2,1)}, u32[]{:S(2)}) copy-start(bf16[128,128]{1,0:T(8,128)(2,1)} %refs_3_.3) | copy-start | bytes 98308
  2.6 9.2 %copy-start.3 = (bf16[128,128]{1,0:T(8,128)(2,1)S(1)}, bf16[128,128]{1,0:T(8,128)(2,1)}, u32[]{:S(2)}) copy-start(bf16[128,128]{1,0:T(8,128)(2,1)} %refs_4_.3) | copy-start | bytes 98308
  2.6 9.2 %copy-start.4 = (s32[12,12]{1,0:T(8,128)S(1)}, s32[12,12]{1,0:T(8,128)}, u32[]{:S(2)}) copy-start(s32[12,12]{1,0:T(8,128)} %refs_1_.3) | copy-start | bytes 1732
  2.6 32.3 %all-to-all-start = ((bf16[32,8,1152]{2,1,0:T(8,128)(2,1)}), bf16[32,8,1152]{2,1,0:T(8,128)(2,1)S(1)}, u32[]{:S(2)}, u32[]{:S(2)}) async-start(bf16[32,8,1152]{2,1,0:T(8,128)(2,1)} %bitcast.5), calls=%async_computation | async-start | bytes 1179648 | tf_op jit(solution)/shard_map/all_to_all | solution.py:327
  9.9 14.8 %collective-permute-start = (bf16[8,8,1152]{2,1,0:T(8,128)(2,1)S(1)}, bf16[8,8,1152]{2,1,0:T(8,128)(2,1)S(1)}, u32[]{:S(2)}, u32[]{:S(2)}) collective-permute-start(bf16[8,8,1152]{2,1,0:T(8,128)(2,1)S(1)} %get-tuple-element.12), channel_id=1, source_target_pairs={{0,8},{2,10},{4,12},{6,14},{8,0},{10,2},{12,4},{14,6},{16,24},{18,... | collective-permute-start | bytes 442376 | tf_op jit(solution)/shard_map/ppermute | solution.py:292
  24.8 4.4 %collective-permute-start.1 = (bf16[4,8,1152]{2,1,0:T(8,128)(2,1)S(1)}, bf16[4,8,1152]{2,1,0:T(8,128)(2,1)S(1)}, u32[]{:S(2)}, u32[]{:S(2)}) collective-permute-start(bf16[4,8,1152]{2,1,0:T(8,128)(2,1)S(1)} %pad_maximum_fusion), channel_id=1, source_target_pairs={{0,4},{2,6},{4,0},{6,2},{8,12},{10,14},{12,8},{14,10},{16,20},{18,... | collective-permute-start | bytes 221192 | tf_op jit(solution)/shard_map/ppermute | solution.py:292
  26.3 4.4 %collective-permute-start.2 = (bf16[4,8,1152]{2,1,0:T(8,128)(2,1)S(1)}, bf16[4,8,1152]{2,1,0:T(8,128)(2,1)S(1)}, u32[]{:S(2)}, u32[]{:S(2)}) collective-permute-start(bf16[4,8,1152]{2,1,0:T(8,128)(2,1)S(1)} %pad_maximum_fusion.1), channel_id=1, source_target_pairs={{0,1},{2,3},{4,5},{6,7},{8,9},{10,11},{12,13},{14,15},{16,17},{18,... | collective-permute-start | bytes 221192 | tf_op jit(solution)/shard_map/ppermute | solution.py:292
  27.8 5.3 %collective-permute-start.3 = (bf16[4,8,1152]{2,1,0:T(8,128)(2,1)S(1)}, bf16[4,8,1152]{2,1,0:T(8,128)(2,1)S(1)}, u32[]{:S(2)}, u32[]{:S(2)}) collective-permute-start(bf16[4,8,1152]{2,1,0:T(8,128)(2,1)S(1)} %pad_maximum_fusion.2), channel_id=1, source_target_pairs={{0,5},{2,7},{4,1},{6,3},{8,13},{10,15},{12,9},{14,11},{16,21},{18,... | collective-permute-start | bytes 221192 | tf_op jit(solution)/shard_map/ppermute | solution.py:292
  33.2 1.4 %collective-permute-start.4 = (bf16[8,8,1152]{2,1,0:T(8,128)(2,1)S(1)}, bf16[8,8,1152]{2,1,0:T(8,128)(2,1)S(1)}, u32[]{:S(2)}, u32[]{:S(2)}) collective-permute-start(bf16[8,8,1152]{2,1,0:T(8,128)(2,1)S(1)} %get-tuple-element.25), channel_id=1, source_target_pairs={{0,2},{2,0},{4,6},{6,4},{8,10},{10,8},{12,14},{14,12},{16,18},{18,... | collective-permute-start | bytes 442376 | tf_op jit(solution)/shard_map/ppermute | solution.py:292
  35.8 9.4 %copy-start = (bf16[128,128]{1,0:T(8,128)(2,1)S(1)}, bf16[128,128]{1,0:T(8,128)(2,1)}, u32[]{:S(2)}) copy-start(bf16[128,128]{1,0:T(8,128)(2,1)} %w_ref.1) | copy-start | bytes 98308
